TPU v7x, 32 devices: a whole 2x2x4 slice. The times are simulated.
32 devices in a mesh: seq: 16 (over z, y, x), head: 2 (over core).
Axes of the slice: x: 2, y: 2, z: 4, core: 2. Of those that a mesh axis runs over, the one named last changes fastest.
Arguments:
- query_rows: bfloat16 [16, 4096, 128], P('head', 'seq'), may hold values from -6 to 6
- key_rows: bfloat16 [16, 4096, 128], P('head', 'seq'), may hold values from -6 to 6
- value_rows: bfloat16 [16, 4096, 128], P('head', 'seq'), may hold values from -6 to 6
- norm_gain: float32 [16, 128], P('head'), may hold values from 0.25 to 1.75
- level_table: float32 [16, 16, 6], P(None, 'head'), may hold values from 0.3 to 4.5
- level_index: int32 [4096, 6], P('seq'), may hold values from 0 to 15
- window_length: int32 [16], P('head'), may hold values from 512 to 1024, as said below
- out_grad: bfloat16 [16, 4096, 128], P('head', 'seq'), may hold values from -18 to 18
Outputs:
- layer_out: bfloat16 [16, 4096, 128], P('head', 'seq')
- query_grad: bfloat16 [16, 4096, 128], P('head', 'seq')
- key_grad: bfloat16 [16, 4096, 128], P('head', 'seq')
- value_grad: bfloat16 [16, 4096, 128], P('head', 'seq')
- table_grad: float32 [16, 16, 6], P(None, 'head')
- gain_grad: float32 [16, 128], P('head')
Inputs may be any that keep to these rules, and one draw needn't show every extreme that they name: `window_length`: every head's window holds at least half of 1024 tokens and at most 1024; some head's window is exactly 1024.
All inputs are finite; a program needn't handle non-finite values.
Results may differ from a plain program's by a relative error of at most 0.0078.
Values may be sent and summed in bfloat16 or wider, within the bound.
No kernel may reach another device: no remote copies, remote signals or barrier semaphores. Data moves between devices by JAX's collectives and lax.ppermute only.
A program may use at most 128 MiB of HBM per device.

v0:
```python
import math

import jax
import jax.numpy as jnp
from jax import lax
from jax.sharding import PartitionSpec as P

H = 16
BLOCK = 64
WINDOW = 1024
LEVELS = 6
TABLE_ROWS = 16


epsilon = 1e-06
block_cap = 512


def shifted(block, axis, distance):
    devices = range(lax.axis_size(axis))
    route = [(i - distance, i) for i in devices if i - distance in devices]
    return lax.ppermute(block, axis, route)


def from_partner(shard, axis, bit):
    return lax.ppermute(shard, axis, [(i, i ^ 1 << bit) for i in range(lax.axis_size(axis))])


def contract(pattern, left_side, right_side):
    return jnp.einsum(pattern, left_side, right_side, preferred_element_type=jnp.float32)


def causal_mask():
    row_pos = lax.broadcasted_iota(jnp.int32, (BLOCK, BLOCK), 0)
    col_pos = lax.broadcasted_iota(jnp.int32, (BLOCK, BLOCK), 1)
    return row_pos >= col_pos


def window_mask(block_rows, shift_rows, key_count, span_len):
    query_pos = lax.broadcasted_iota(jnp.int32, (block_rows, key_count), 0)
    key_pos = lax.broadcasted_iota(jnp.int32, (block_rows, key_count), 1)
    offset = query_pos + shift_rows - key_pos
    return (offset >= 0) & (offset < span_len)


def leaf_view(tensor):
    head_count, token_count, head_dim = tensor.shape
    return tensor.reshape(head_count, token_count // BLOCK, BLOCK, head_dim)


def split_level(tensor, group_len):
    head_count, token_count, head_dim = tensor.shape
    return tensor.reshape(head_count, token_count // (2 * group_len), 2, group_len, head_dim)


def level_summary(key_rows, value_rows, group_len):
    lower_sum = contract(
        "hpse,hpsf->hpef",
        split_level(key_rows, group_len)[:, :, 0],
        split_level(value_rows, group_len)[:, :, 0],
    )
    return (lower_sum * (1.0 / math.sqrt(group_len * key_rows.shape[-1]))).astype(jnp.bfloat16)


def level_area(query_rows, summary, group_len):
    upper_half = contract("hpse,hpef->hpsf", split_level(query_rows, group_len)[:, :, 1], summary)
    return jnp.stack([jnp.zeros_like(upper_half), upper_half], axis=2).reshape(query_rows.shape)


def level_grads(query_rows, key_rows, value_rows, summary, upstream, group_len):
    upstream_up = split_level(upstream, group_len)[:, :, 1]
    query_up = contract("hpsf,hpef->hpse", upstream_up, summary)
    summary_grad = contract(
        "hpse,hpsf->hpef", split_level(query_rows, group_len)[:, :, 1], upstream_up
    )
    low_grad = (summary_grad * (1.0 / math.sqrt(group_len * query_rows.shape[-1]))).astype(
        jnp.bfloat16
    )
    key_low = contract("hpsf,hpef->hpse", split_level(value_rows, group_len)[:, :, 0], low_grad)
    value_low = contract("hpse,hpef->hpsf", split_level(key_rows, group_len)[:, :, 0], low_grad)
    blank = jnp.zeros_like(query_up)
    full_shape = query_rows.shape
    return (
        jnp.stack([blank, query_up], axis=2).reshape(full_shape),
        jnp.stack([key_low, blank], axis=2).reshape(full_shape),
        jnp.stack([value_low, blank], axis=2).reshape(full_shape),
    )


def window_head(query_head, key_head, value_head, span_len):
    token_count, head_dim = query_head.shape
    block_rows = min(block_cap, token_count)
    score_scale = lax.rsqrt((head_dim * span_len).astype(jnp.float32))
    inside = window_mask(block_rows, WINDOW, WINDOW + block_rows, span_len)
    scores = contract("qe,ke->qk", query_head, key_head) * score_scale
    prob_low = jnp.where(inside, scores, 0.0).astype(jnp.bfloat16)
    outputs = [contract("qk,ke->qe", prob_low, value_head)]
    return jnp.concatenate(outputs, axis=0)


def window_back_head(query_head, key_head, value_head, grad_head, span_len, keep_from):
    token_count, head_dim = query_head.shape
    block_rows = min(block_cap, token_count)
    score_scale = lax.rsqrt((head_dim * span_len).astype(jnp.float32))
    inside = window_mask(block_rows, WINDOW, WINDOW + block_rows, span_len)
    key_grad = jnp.zeros((WINDOW + token_count - keep_from, head_dim), jnp.float32)
    value_grad = jnp.zeros((WINDOW + token_count - keep_from, head_dim), jnp.float32)
    grad_part = grad_head[0:block_rows]
    scores = contract("qe,ke->qk", query_head, key_head) * score_scale
    prob_low = jnp.where(inside, scores, 0.0).astype(jnp.bfloat16)
    prob_grad = contract("qe,ke->qk", grad_part, value_head)
    score_grad = jnp.where(inside, prob_grad * score_scale, 0.0).astype(jnp.bfloat16)
    query_grad = [contract("qk,ke->qe", score_grad, key_head)]
    skip_cols = max(keep_from, 0)
    target = skip_cols - keep_from
    length_now = WINDOW + block_rows - skip_cols
    key_grad = key_grad.at[target : target + length_now].add(
        contract("qk,qe->ke", score_grad[:, skip_cols:], query_head)
    )
    value_grad = value_grad.at[target : target + length_now].add(
        contract("qk,qe->ke", prob_low, grad_part)
    )
    return (jnp.concatenate(query_grad, axis=0), key_grad, value_grad)


def shards(
    query_rows, key_rows, value_rows, norm_gain, level_table, level_index, window_length, out_grad
):
    heads_here, tok_here, head_dim = query_rows.shape
    seq_index = lax.axis_index("seq")
    seq_levels = lax.axis_size("seq").bit_length() - 1
    local_levels = (tok_here // BLOCK).bit_length() - 1
    reach_count = WINDOW // tok_here
    onehot = (
        level_index[:, :, None] == lax.broadcasted_iota(jnp.int32, (1, 1, TABLE_ROWS), 2)
    ).astype(jnp.float32)
    weights = jnp.einsum("tjk,khj->htj", onehot, level_table, precision=lax.Precision.HIGHEST)

    def weight_of(level_no):
        return weights[:, :, min(level_no, LEVELS - 1)][:, :, None]

    own_pair = jnp.stack([key_rows, value_rows])
    pieces = []
    for step_no in range(reach_count, 0, -1):
        pieces.append(shifted(own_pair, "seq", step_no))
    pieces.append(own_pair)
    wide_pair = jnp.concatenate(pieces, axis=2)
    device_summary = contract("hte,htf->hef", key_rows, value_rows)
    sibling = []
    running = device_summary
    for bit_no in range(seq_levels):
        partner = from_partner(running, "seq", bit_no)
        upper_half = seq_index >> bit_no & 1 == 1
        sibling.append(jnp.where(upper_half, partner, 0.0))
        running = running + partner
    query_leaf = leaf_view(query_rows)
    key_leaf = leaf_view(key_rows)
    value_leaf = leaf_view(value_rows)
    leaf_scale = 1.0 / math.sqrt(BLOCK * head_dim)
    causal = causal_mask()
    leaf_prob = jnp.where(
        causal, contract("hcte,hcse->hcts", query_leaf, key_leaf) * leaf_scale, 0.0
    ).astype(jnp.bfloat16)
    area_list = [contract("hcts,hcse->hcte", leaf_prob, value_leaf).reshape(query_rows.shape)]
    summaries = []
    for level_no in range(1, local_levels + 1):
        group_len = BLOCK * 2 ** (level_no - 1)
        summary = level_summary(key_rows, value_rows, group_len)
        summaries.append(summary)
        area_list.append(level_area(query_rows, summary, group_len))
    for bit_no in range(seq_levels):
        group_len = tok_here * 2**bit_no
        summary = (sibling[bit_no] * (1.0 / math.sqrt(group_len * head_dim))).astype(jnp.bfloat16)
        summaries.append(summary)
        area_list.append(contract("hte,hef->htf", query_rows, summary))
    mixed = lax.map(
        lambda head_items: window_head(head_items[0], head_items[1], head_items[2], head_items[3]),
        (query_rows, wide_pair[0], wide_pair[1], window_length),
    )
    for level_no in range(len(area_list)):
        mixed = mixed + weight_of(level_no) * area_list[level_no]
    grad_full = out_grad.astype(jnp.float32)
    scaled = grad_full * norm_gain[:, None, :]
    square_sum, cross_sum = lax.psum(
        (jnp.sum(mixed * mixed, axis=(0, 2)), jnp.sum(scaled * mixed, axis=(0, 2))), "head"
    )
    inv_rms = lax.rsqrt(square_sum / (H * head_dim) + epsilon)
    layer_out = (mixed * inv_rms[None, :, None] * norm_gain[:, None, :]).astype(jnp.bfloat16)
    mixed_grad = (
        scaled * inv_rms[None, :, None]
        - mixed * (inv_rms**3 * cross_sum / (H * head_dim))[None, :, None]
    )
    gain_part = jnp.sum(grad_full * mixed * inv_rms[None, :, None], axis=1)
    grad_low = mixed_grad.astype(jnp.bfloat16)
    columns = [jnp.zeros((heads_here, tok_here), jnp.float32) for column_no in range(LEVELS)]
    for level_no in range(len(area_list)):
        column_no = min(level_no, LEVELS - 1)
        columns[column_no] = columns[column_no] + jnp.sum(mixed_grad * area_list[level_no], axis=2)
    upstream_leaf = leaf_view((weight_of(0) * mixed_grad).astype(jnp.bfloat16))
    prob_grad = contract("hcte,hcse->hcts", upstream_leaf, value_leaf)
    score_grad = jnp.where(causal, prob_grad * leaf_scale, 0.0).astype(jnp.bfloat16)
    query_grad = contract("hcts,hcse->hcte", score_grad, key_leaf).reshape(query_rows.shape)
    key_grad = contract("hcts,hcte->hcse", score_grad, query_leaf).reshape(query_rows.shape)
    value_grad = contract("hcts,hcte->hcse", leaf_prob, upstream_leaf).reshape(query_rows.shape)
    for level_no in range(1, local_levels + 1):
        group_len = BLOCK * 2 ** (level_no - 1)
        upstream = (weight_of(level_no) * mixed_grad).astype(jnp.bfloat16)
        query_part, key_part, value_part = level_grads(
            query_rows, key_rows, value_rows, summaries[level_no - 1], upstream, group_len
        )
        query_grad = query_grad + query_part
        key_grad = key_grad + key_part
        value_grad = value_grad + value_part
    summary_grads = []
    for bit_no in range(seq_levels):
        level_no = local_levels + 1 + bit_no
        upstream = (weight_of(level_no) * mixed_grad).astype(jnp.bfloat16)
        query_grad = query_grad + contract("htf,hef->hte", upstream, summaries[level_no - 1])
        group_len = tok_here * 2**bit_no
        partial_value = contract("hte,htf->hef", query_rows, upstream) * (
            1.0 / math.sqrt(group_len * head_dim)
        )
        upper_half = seq_index >> bit_no & 1 == 1
        summary_grads.append(jnp.where(upper_half, partial_value, 0.0))
    pending = jnp.stack(summary_grads)
    for bit_no in range(seq_levels):
        partner = from_partner(pending[bit_no:], "seq", bit_no)
        lower_half = seq_index >> bit_no & 1 == 0
        received = jnp.where(lower_half, partner[0], 0.0).astype(jnp.bfloat16)
        key_grad = key_grad + contract("htf,hef->hte", value_rows, received)
        value_grad = value_grad + contract("hte,hef->htf", key_rows, received)
        pending = jnp.concatenate(
            [pending[: bit_no + 1], pending[bit_no + 1 :] + partner[1:]], axis=0
        )
    keep_from = 0
    window_query, window_key, window_value = lax.map(
        lambda head_items: window_back_head(
            head_items[0], head_items[1], head_items[2], head_items[3], head_items[4], keep_from
        ),
        (query_rows, wide_pair[0], wide_pair[1], grad_low, window_length),
    )
    query_grad = query_grad + window_query
    key_grad = key_grad + window_key[:, WINDOW:]
    value_grad = value_grad + window_value[:, WINDOW:]
    for step_no in range(1, reach_count + 1):
        first_row = (reach_count - step_no) * tok_here
        piece = jnp.stack(
            [
                window_key[:, first_row : first_row + tok_here],
                window_value[:, first_row : first_row + tok_here],
            ]
        )
        arrived = shifted(piece.astype(jnp.bfloat16), "seq", -step_no).astype(piece.dtype)
        key_grad = key_grad + arrived[0]
        value_grad = value_grad + arrived[1]
    weight_grad = jnp.stack(columns, axis=-1)
    table_part = jnp.einsum("tjk,htj->khj", onehot, weight_grad, precision=lax.Precision.HIGHEST)
    table_grad, gain_grad = lax.psum((table_part, gain_part), "seq")
    return (
        layer_out,
        query_grad.astype(jnp.bfloat16),
        key_grad.astype(jnp.bfloat16),
        value_grad.astype(jnp.bfloat16),
        table_grad,
        gain_grad,
    )


def solution(mesh):
    placed = (
        P("head", "seq", None),
        P("head", "seq", None),
        P("head", "seq", None),
        P("head", None),
        P(None, "head", None),
        P("seq", None),
        P("head"),
        P("head", "seq", None),
    )
    return jax.shard_map(
        shards,
        mesh=mesh,
        in_specs=placed,
        out_specs=(
            P("head", "seq", None),
            P("head", "seq", None),
            P("head", "seq", None),
            P("head", "seq", None),
            P(None, "head", None),
            P("head", None),
        ),
        check_vma=False,
    )
```

profile of v0, /device:TPU:0, one launch (start us, length us, event | category | flops | bytes accessed | tf_op | source)
XLA Modules:
  0.0 521.0 jit_solution(10716536842684379148)
XLA Ops:
  3.1 5.9 %collective-permute-start = (bf16[2,8,256,128]{3,2,1,0:T(8,128)(2,1)}, bf16[2,8,256,128]{3,2,1,0:T(8,128)(2,1)}, u32[]{:S(2)}, u32[]{:S(2)}) collective-permute-start(bf16[2,8,256,128]{3,2,1,0:T(8,128)(2,1)} %pad_maximum_fusion.1), channel_id=1, source_target_pairs={{0,8},{2,10},{4,12},{6,14},{8,16},{10,18},{12,20},{14,22},{16,24},... | collective-permute-start | bytes 3145736 | tf_op jit(solution)/shard_map/ppermute | solution.py:22
  9.0 5.3 %collective-permute-start.1 = (bf16[2,8,256,128]{3,2,1,0:T(8,128)(2,1)}, bf16[2,8,256,128]{3,2,1,0:T(8,128)(2,1)}, u32[]{:S(2)}, u32[]{:S(2)}) collective-permute-start(bf16[2,8,256,128]{3,2,1,0:T(8,128)(2,1)} %pad_maximum_fusion.1), channel_id=1, source_target_pairs={{0,6},{2,8},{4,10},{6,12},{8,14},{10,16},{12,18},{14,20},{16,22},{... | collective-permute-start | bytes 3145736 | tf_op jit(solution)/shard_map/ppermute | solution.py:22
  14.3 3.5 collective-permute-start.2
  23.8 45.6 %collective-permute-done.4 = f32[8,128,128]{2,1,0:T(8,128)S(1)} collective-permute-done((f32[8,128,128]{2,1,0:T(8,128)S(1)}, f32[8,128,128]{2,1,0:T(8,128)S(1)}, u32[]{:S(2)}, u32[]{:S(2)}) %collective-permute-start.4) | collective-permute-done | bytes 524320 | tf_op jit(solution)/shard_map/ppermute | solution.py:26
  86.9 28.5 %collective-permute-start.6 = (f32[8,128,128]{2,1,0:T(8,128)}, f32[8,128,128]{2,1,0:T(8,128)S(1)}, u32[]{:S(2)}, u32[]{:S(2)}) collective-permute-start(f32[8,128,128]{2,1,0:T(8,128)} %add.219), channel_id=1, source_target_pairs={{0,8},{2,10},{4,12},{6,14},{8,0},{10,2},{12,4},{14,6},{16,24},{18,... | collective-permute-start | bytes 1572872 | tf_op jit(solution)/shard_map/ppermute | solution.py:26
  123.8 34.8 %while.31 = (s32[]{:T(128)}, f32[8,256,128]{1,2,0:T(8,128)}, s32[8]{0:T(128)S(1)}, bf16[8,256,128]{2,1,0:T(8,128)(2,1)S(1)}, bf16[8,1280,128]{2,1,0:T(8,128)(2,1...) while((s32[]{:T(128)}, f32[8,256,128]{1,2,0:T(8,128)}, s32[8]{0:T(128)S(1)}, ...), condition=%wide.region_1.2_spmd, body=%wide.region_0.1_spmd.sunk | while | flops 170066176 | bytes 857221 | solution.py:176
  125.1 3.1 fusion.225
  133.8 3.1 fusion.225
  146.9 3.1 fusion.225
  155.6 3.1 fusion.225
  162.9 22.2 %collective-permute-done.7 = f32[8,128,128]{2,1,0:T(8,128)S(1)} collective-permute-done((f32[8,128,128]{2,1,0:T(8,128)S(1)}, f32[8,128,128]{2,1,0:T(8,128)S(1)}, u32[]{:S(2)}, u32[]{:S(2)}) %collective-permute-start.7) | collective-permute-done | bytes 524320 | tf_op jit(solution)/shard_map/ppermute | solution.py:26
  194.3 5.4 %multiply_reduce_fusion = (f32[8,256]{1,0:T(8,128)S(1)}, f32[8,256]{1,0:T(8,128)S(1)}, f32[8,256]{1,0:T(8,128)S(1)}, f32[8,256]{1,0:T(8,128)S(1)}, f32[8,256]{1,...) fusion(f32[8,256,128]{1,2,0:T(8,128)} %get-tuple-element.327, ...), kind=kLoop, calls=%fused_computation.158 | loop fusion | flops 5752832 | bytes 10549248 | tf_op jit(solution)/shard_map/reduce_sum | solution.py:198
  211.7 77.1 %while.32 = (s32[]{:T(128)}, f32[8,256,128]{2,1,0:T(8,128)}, f32[8,1280,128]{1,2,0:T(8,128)}, f32[8,1280,128]{1,2,0:T(8,128)}, s32[8]{0:T(128)S(1)}, /*index=5*/...) while((s32[]{:T(128)}, f32[8,256,128]{2,1,0:T(8,128)}, ...), condition=%wide.region_7.8_spmd, body=%wide.region_6.7_spmd.sunk | while | flops 424018176 | bytes 4663453 | solution.py:236
  218.2 3.1 fusion.238
  227.9 3.1 fusion.238
  247.2 3.1 fusion.238
  256.8 3.1 fusion.238
  266.5 3.1 fusion.238
  285.7 3.1 fusion.238
  318.4 51.0 %collective-permute-done.8 = f32[4,8,128,128]{2,3,1,0:T(8,128)S(1)} collective-permute-done((f32[4,8,128,128]{2,3,1,0:T(8,128)S(1)}, f32[4,8,128,128]{2,3,1,0:T(8,128)S(1)}, u32[]{:S(2)}, u32[]{:S(2)}) %collective-permute-start.8) | collective-permute-done | bytes 2097184 | tf_op jit(solution)/shard_map/ppermute | solution.py:26
  391.7 3.1 reshape.259
  401.0 71.9 %all-reduce.8 = (f32[16,8,6]{0,1,2:T(8,128)}, f32[8,128]{1,0:T(8,128)}) all-reduce(f32[16,8,6]{0,1,2:T(8,128)S(1)} %convolution_bitcast_fusion.24, f32[8,128]{1,0:T(8,128)S(1)} %get-tuple-element.259), channel_id=1, replica_groups=mesh['seq'=16,'head'=2] {'seq'}, use_global_device_ids=true, to_apply=%region_15.16 | all-reduce | flops 1792 | bytes 14336 | tf_op jit(solution)/shard_map/psum | solution.py:258
  493.3 11.7 %collective-permute-done.10 = f32[2,8,128,128]{2,3,1,0:T(8,128)S(1)} collective-permute-done((f32[2,8,128,128]{2,3,1,0:T(8,128)S(1)}, f32[2,8,128,128]{2,3,1,0:T(8,128)S(1)}, u32[]{:S(2)}, u32[]{:S(2)}) %collective-permute-start.10) | collective-permute-done | bytes 1048608 | tf_op jit(solution)/shard_map/ppermute | solution.py:26
  505.8 8.4 %collective-permute-done.11 = bf16[1,8,128,128]{2,3,1,0:T(8,128)(2,1)S(1)} collective-permute-done((bf16[1,8,128,128]{2,3,1,0:T(8,128)(2,1)S(1)}, bf16[1,8,128,128]{2,3,1,0:T(8,128)(2,1)S(1)}, u32[]{:S(2)}, u32[]{:S(2)}) %collective-permute-start.11) | collective-permute-done | bytes 262176 | tf_op jit(solution)/shard_map/ppermute | solution.py:26
  (302 shorter events, 214.9 us)
Async XLA Ops:
  3.1 112.4 %collective-permute-start = (bf16[2,8,256,128]{3,2,1,0:T(8,128)(2,1)}, bf16[2,8,256,128]{3,2,1,0:T(8,128)(2,1)}, u32[]{:S(2)}, u32[]{:S(2)}) collective-permute-start(bf16[2,8,256,128]{3,2,1,0:T(8,128)(2,1)} %pad_maximum_fusion.1), channel_id=1, source_target_pairs={{0,8},{2,10},{4,12},{6,14},{8,16},{10,18},{12,20},{14,22},{16,24},... | collective-permute-start | bytes 3145736 | tf_op jit(solution)/shard_map/ppermute | solution.py:22
  9.0 107.8 %collective-permute-start.1 = (bf16[2,8,256,128]{3,2,1,0:T(8,128)(2,1)}, bf16[2,8,256,128]{3,2,1,0:T(8,128)(2,1)}, u32[]{:S(2)}, u32[]{:S(2)}) collective-permute-start(bf16[2,8,256,128]{3,2,1,0:T(8,128)(2,1)} %pad_maximum_fusion.1), channel_id=1, source_target_pairs={{0,6},{2,8},{4,10},{6,12},{8,14},{10,16},{12,18},{14,20},{16,22},{... | collective-permute-start | bytes 3145736 | tf_op jit(solution)/shard_map/ppermute | solution.py:22
  14.3 103.9 %collective-permute-start.2 = (bf16[2,8,256,128]{3,2,1,0:T(8,128)(2,1)}, bf16[2,8,256,128]{3,2,1,0:T(8,128)(2,1)}, u32[]{:S(2)}, u32[]{:S(2)}) collective-permute-start(bf16[2,8,256,128]{3,2,1,0:T(8,128)(2,1)} %pad_maximum_fusion.1), channel_id=1, source_target_pairs={{0,4},{2,6},{4,8},{6,10},{8,12},{10,14},{12,16},{14,18},{16,20},{1... | collective-permute-start | bytes 3145736 | tf_op jit(solution)/shard_map/ppermute | solution.py:22
  17.8 101.8 %collective-permute-start.3 = (bf16[2,8,256,128]{3,2,1,0:T(8,128)(2,1)}, bf16[2,8,256,128]{3,2,1,0:T(8,128)(2,1)}, u32[]{:S(2)}, u32[]{:S(2)}) collective-permute-start(bf16[2,8,256,128]{3,2,1,0:T(8,128)(2,1)} %pad_maximum_fusion.1), channel_id=1, source_target_pairs={{0,2},{2,4},{4,6},{6,8},{8,10},{10,12},{12,14},{14,16},{16,18},{18... | collective-permute-start | bytes 3145736 | tf_op jit(solution)/shard_map/ppermute | solution.py:22
  20.7 48.7 %collective-permute-start.4 = (f32[8,128,128]{2,1,0:T(8,128)S(1)}, f32[8,128,128]{2,1,0:T(8,128)S(1)}, u32[]{:S(2)}, u32[]{:S(2)}) collective-permute-start(f32[8,128,128]{2,1,0:T(8,128)S(1)} %fusion.157), channel_id=1, source_target_pairs={{0,2},{2,0},{4,6},{6,4},{8,10},{10,8},{12,14},{14,12},{16,18},{18,... | collective-permute-start | bytes 1572872 | tf_op jit(solution)/shard_map/ppermute | solution.py:26
  22.6 47.8 %copy-start.45 = (bf16[8,128,128]{2,1,0:T(8,128)(2,1)}, bf16[8,128,128]{2,1,0:T(8,128)(2,1)S(1)}, u32[]{:S(2)}) copy-start(bf16[8,128,128]{2,1,0:T(8,128)(2,1)S(1)} %fusion.100) | copy-start | bytes 786436
  70.4 14.1 %collective-permute-start.5 = (f32[8,128,128]{2,1,0:T(8,128)}, f32[8,128,128]{2,1,0:T(8,128)}, u32[]{:S(2)}, u32[]{:S(2)}) collective-permute-start(f32[8,128,128]{2,1,0:T(8,128)} %add.217), channel_id=1, source_target_pairs={{0,4},{2,6},{4,0},{6,2},{8,12},{10,14},{12,8},{14,10},{16,20},{18,... | collective-permute-start | bytes 1572872 | tf_op jit(solution)/shard_map/ppermute | solution.py:26
  84.5 100.6 %copy-start.5 = (f32[8,256,128]{1,2,0:T(8,128)}, f32[8,256,128]{1,2,0:T(8,128)S(1)}, u32[]{:S(2)}) copy-start(f32[8,256,128]{1,2,0:T(8,128)S(1)} %convolution_bitcast_fusion.14) | copy-start | bytes 3145732
  86.9 71.7 %collective-permute-start.6 = (f32[8,128,128]{2,1,0:T(8,128)}, f32[8,128,128]{2,1,0:T(8,128)S(1)}, u32[]{:S(2)}, u32[]{:S(2)}) collective-permute-start(f32[8,128,128]{2,1,0:T(8,128)} %add.219), channel_id=1, source_target_pairs={{0,8},{2,10},{4,12},{6,14},{8,0},{10,2},{12,4},{14,6},{16,24},{18,... | collective-permute-start | bytes 1572872 | tf_op jit(solution)/shard_map/ppermute | solution.py:26
  160.0 25.1 %copy-start.8 = (f32[8,256,128]{1,2,0:T(8,128)S(1)}, f32[8,256,128]{1,2,0:T(8,128)}, u32[]{:S(2)}) copy-start(f32[8,256,128]{1,2,0:T(8,128)} %copy.62) | copy-start | bytes 3145732
  160.0 25.1 %collective-permute-start.7 = (f32[8,128,128]{2,1,0:T(8,128)S(1)}, f32[8,128,128]{2,1,0:T(8,128)S(1)}, u32[]{:S(2)}, u32[]{:S(2)}) collective-permute-start(f32[8,128,128]{2,1,0:T(8,128)S(1)} %add.221), channel_id=1, source_target_pairs={{0,16},{2,18},{4,20},{6,22},{8,24},{10,26},{12,28},{14,30},{16,0},... | collective-permute-start | bytes 1572872 | tf_op jit(solution)/shard_map/ppermute | solution.py:26
  298.3 71.0 %collective-permute-start.8 = (f32[4,8,128,128]{2,3,1,0:T(8,128)S(1)}, f32[4,8,128,128]{2,3,1,0:T(8,128)S(1)}, u32[]{:S(2)}, u32[]{:S(2)}) collective-permute-start(f32[4,8,128,128]{2,3,1,0:T(8,128)S(1)} %pad_maximum_fusion), channel_id=1, source_target_pairs={{0,2},{2,0},{4,6},{6,4},{8,10},{10,8},{12,14},{14,12},{16,18},{18,... | collective-permute-start | bytes 6291464 | tf_op jit(solution)/shard_map/ppermute | solution.py:26
  303.7 173.8 %collective-permute-start.15 = (bf16[2,8,256,128]{2,3,1,0:T(8,128)(2,1)}, bf16[2,8,256,128]{2,3,1,0:T(8,128)(2,1)}, u32[]{:S(2)}, u32[]{:S(2)}) collective-permute-start(bf16[2,8,256,128]{2,3,1,0:T(8,128)(2,1)} %pad_maximum_fusion.5), channel_id=1, source_target_pairs={{8,0},{10,2},{12,4},{14,6},{16,8},{18,10},{20,12},{22,14},{24,16},... | collective-permute-start | bytes 3145736 | tf_op jit(solution)/shard_map/ppermute | solution.py:22
  306.1 172.8 %collective-permute-start.14 = (bf16[2,8,256,128]{2,3,1,0:T(8,128)(2,1)}, bf16[2,8,256,128]{2,3,1,0:T(8,128)(2,1)}, u32[]{:S(2)}, u32[]{:S(2)}) collective-permute-start(bf16[2,8,256,128]{2,3,1,0:T(8,128)(2,1)} %pad_maximum_fusion.4), channel_id=1, source_target_pairs={{6,0},{8,2},{10,4},{12,6},{14,8},{16,10},{18,12},{20,14},{22,16},{... | collective-permute-start | bytes 3145736 | tf_op jit(solution)/shard_map/ppermute | solution.py:22
  308.5 172.7 %collective-permute-start.13 = (bf16[2,8,256,128]{2,3,1,0:T(8,128)(2,1)}, bf16[2,8,256,128]{2,3,1,0:T(8,128)(2,1)}, u32[]{:S(2)}, u32[]{:S(2)}) collective-permute-start(bf16[2,8,256,128]{2,3,1,0:T(8,128)(2,1)} %pad_maximum_fusion.3), channel_id=1, source_target_pairs={{4,0},{6,2},{8,4},{10,6},{12,8},{14,10},{16,12},{18,14},{20,16},{2... | collective-permute-start | bytes 3145736 | tf_op jit(solution)/shard_map/ppermute | solution.py:22
  310.9 172.5 %collective-permute-start.12 = (bf16[2,8,256,128]{2,3,1,0:T(8,128)(2,1)}, bf16[2,8,256,128]{2,3,1,0:T(8,128)(2,1)}, u32[]{:S(2)}, u32[]{:S(2)}) collective-permute-start(bf16[2,8,256,128]{2,3,1,0:T(8,128)(2,1)} %pad_maximum_fusion.2), channel_id=1, source_target_pairs={{2,0},{4,2},{6,4},{8,6},{10,8},{12,10},{14,12},{16,14},{18,16},{20... | collective-permute-start | bytes 3145736 | tf_op jit(solution)/shard_map/ppermute | solution.py:22
  318.4 54.0 %copy-start.19 = (f32[8,128,128]{2,1,0:T(8,128)S(1)}, f32[8,128,128]{2,1,0:T(8,128)}, u32[]{:S(2)}) copy-start(f32[8,128,128]{2,1,0:T(8,128)} %copy-done.18) | copy-start | bytes 1572868
  371.2 114.4 %collective-permute-start.9 = (f32[3,8,128,128]{2,3,1,0:T(8,128)}, f32[3,8,128,128]{2,3,1,0:T(8,128)}, u32[]{:S(2)}, u32[]{:S(2)}) collective-permute-start(f32[3,8,128,128]{2,3,1,0:T(8,128)} %slice_add_fusion), channel_id=1, source_target_pairs={{0,4},{2,6},{4,0},{6,2},{8,12},{10,14},{12,8},{14,10},{16,20},{18,... | collective-permute-start | bytes 4718600 | tf_op jit(solution)/shard_map/ppermute | solution.py:26
  478.9 35.3 %copy-start.11 = (f32[2,8,256,128]{2,3,1,0:T(8,128)}, f32[2,8,256,128]{2,3,1,0:T(8,128)S(1)}, u32[]{:S(2)}) copy-start(f32[2,8,256,128]{2,3,1,0:T(8,128)S(1)} %convert_element_type.170) | copy-start | bytes 6291460
  481.1 33.0 %copy-start.12 = (f32[2,8,256,128]{2,3,1,0:T(8,128)}, f32[2,8,256,128]{2,3,1,0:T(8,128)S(1)}, u32[]{:S(2)}) copy-start(f32[2,8,256,128]{2,3,1,0:T(8,128)S(1)} %convert_element_type.169) | copy-start | bytes 6291460
  483.4 30.8 %copy-start.13 = (f32[2,8,256,128]{2,3,1,0:T(8,128)}, f32[2,8,256,128]{2,3,1,0:T(8,128)S(1)}, u32[]{:S(2)}) copy-start(f32[2,8,256,128]{2,3,1,0:T(8,128)S(1)} %convert_element_type.168) | copy-start | bytes 6291460
  485.6 28.6 %copy-start.14 = (f32[2,8,256,128]{2,3,1,0:T(8,128)}, f32[2,8,256,128]{2,3,1,0:T(8,128)S(1)}, u32[]{:S(2)}) copy-start(f32[2,8,256,128]{2,3,1,0:T(8,128)S(1)} %convert_element_type.167) | copy-start | bytes 6291460
  488.2 16.8 %collective-permute-start.10 = (f32[2,8,128,128]{2,3,1,0:T(8,128)S(1)}, f32[2,8,128,128]{2,3,1,0:T(8,128)S(1)}, u32[]{:S(2)}, u32[]{:S(2)}) collective-permute-start(f32[2,8,128,128]{2,3,1,0:T(8,128)S(1)} %slice_add_fusion.1), channel_id=1, source_target_pairs={{0,8},{2,10},{4,12},{6,14},{8,0},{10,2},{12,4},{14,6},{16,24},{18,... | collective-permute-start | bytes 3145736 | tf_op jit(solution)/shard_map/ppermute | solution.py:26
  505.0 9.1 %collective-permute-start.11 = (bf16[1,8,128,128]{2,3,1,0:T(8,128)(2,1)S(1)}, bf16[1,8,128,128]{2,3,1,0:T(8,128)(2,1)S(1)}, u32[]{:S(2)}, u32[]{:S(2)}) collective-permute-start(bf16[1,8,128,128]{2,3,1,0:T(8,128)(2,1)S(1)} %slice_add_fusion.2), channel_id=1, source_target_pairs={{0,16},{2,18},{4,20},{6,22},{8,24},{10,26},{12,28},{14,30},{16,0},... | collective-permute-start | bytes 786440 | tf_op jit(solution)/shard_map/ppermute | solution.py:26
  (45 other events, 328.7 us)
where the time goes:
time: 524 us; the launch traced here: 521 us
  waiting for transfers between devices  139 us (27%)
  matrix products  128 us (24%)
  blocking collectives  77 us (15%)
  local copies, waits for them, and re-layouts  74.6 us (14%)
  starting transfers between devices  53.9 us (10%)
  other arithmetic  35.6 us (7%)
  loops' own time  11.3 us (2%)
    ppermute x8, waiting for transfers between devices, from_partner(): lax.ppermute(shard, axis, [(i, i ^ 1 << bit) for i in range(lax.axis_size...  139 us
    dot_general x78, matrix products, contract(): jnp.einsum(pattern, left_side, right_side, preferred_element_type=jnp.flo...  128 us
    psum x1, blocking collectives, shards(): table_grad, gain_grad = lax.psum((table_part, gain_part), 'seq')  71.9 us
    ppermute x8, starting transfers between devices, from_partner(): lax.ppermute(shard, axis, [(i, i ^ 1 << bit) for i in range(lax.axis_size...  31.3 us
    ppermute x8, starting transfers between devices, shifted(): return lax.ppermute(block, axis, route)  22.6 us
    unnamed x121, local copies, waits for them, and re-layouts  19.4 us
  transfers between devices with their start and end apart: 16, of which 5 were waited for; matrix products, arithmetic and copies ran while one was open for 22% of the time, Pallas kernels for 0%

commit v1 on v0

--- a/solution.py
+++ b/solution.py
@@ -1,8 +1,11 @@
+import functools
 import math
 
 import jax
 import jax.numpy as jnp
 from jax import lax
+from jax.experimental import pallas as pl
+from jax.experimental.pallas import tpu as pltpu
 from jax.sharding import PartitionSpec as P
 
 H = 16
@@ -123,7 +126,7 @@
     return (jnp.concatenate(query_grad, axis=0), key_grad, value_grad)
 
 
-def shards(
+def wide_shards(
     query_rows, key_rows, value_rows, norm_gain, level_table, level_index, window_length, out_grad
 ):
     heads_here, tok_here, head_dim = query_rows.shape
@@ -266,6 +269,611 @@
     )
 
 
+f32 = jnp.float32
+bf16 = jnp.bfloat16
+index_rows = 16
+
+
+def dot_nn(left, right):
+    return lax.dot_general(left, right, (((1,), (0,)), ((), ())), preferred_element_type=f32)
+
+
+def dot_nt(left, right):
+    return lax.dot_general(left, right, (((1,), (1,)), ((), ())), preferred_element_type=f32)
+
+
+def dot_tn(left, right):
+    return lax.dot_general(left, right, (((0,), (0,)), ((), ())), preferred_element_type=f32)
+
+
+def level_scale(level_no, head_dim):
+    return 1.0 / math.sqrt(BLOCK * 2 ** max(level_no - 1, 0) * head_dim)
+
+
+def lane_indices(index_block):
+    rows = index_block.astype(f32)
+    return jnp.concatenate([rows[:8], rows[8:]], axis=1)
+
+
+def lane_weights(indices, table_ref):
+    weights = jnp.zeros(indices.shape, f32)
+    wide = indices.shape[1] // table_ref.shape[-1]
+    for row_no in range(TABLE_ROWS):
+        row = jnp.concatenate([table_ref[0, row_no]] * wide, axis=1)
+        weights = jnp.where(indices == row_no, row, weights)
+    return weights
+
+
+def columns_of(lanes):
+    return jnp.transpose(lanes)
+
+
+def positions(rows):
+    row_pos = lax.broadcasted_iota(jnp.int32, (rows, rows), 0)
+    col_pos = lax.broadcasted_iota(jnp.int32, (rows, rows), 1)
+    return row_pos, col_pos
+
+
+def leaf_bits(row_pos, col_pos):
+    shift = BLOCK.bit_length() - 1
+    return (row_pos >> shift) ^ (col_pos >> shift)
+
+
+def diagonal_factor(query_pos, key_pos, picked, window_scale, near_levels, head_dim):
+    apart = leaf_bits(query_pos, key_pos)
+    factor = picked(0) * level_scale(0, head_dim)
+    for level_no in range(1, near_levels + 1):
+        factor = jnp.where(
+            apart >= 2 ** (level_no - 1), picked(level_no) * level_scale(level_no, head_dim), factor
+        )
+    return jnp.where(query_pos >= key_pos, factor + window_scale, 0.0)
+
+
+def fill(target, first_ref, second_ref):
+    count, rows, _ = first_ref.shape
+    for block_no in range(count):
+        target[pl.ds(block_no * rows, rows)] = first_ref[block_no]
+        target[pl.ds((count + block_no) * rows, rows)] = second_ref[block_no]
+
+
+def summary_kernel(key_ref, value_ref, near_ref, total_ref, *, near_levels):
+    group, _, head_dim = key_ref.shape
+    parts = [dot_tn(key_ref[block_no], value_ref[block_no]) for block_no in range(group)]
+    total_ref[0] = functools.reduce(lambda a, b: a + b, parts)
+    for block_no in range(group):
+        for bit_no in range(group.bit_length() - 1):
+            if block_no >> bit_no & 1:
+                first = (block_no >> bit_no << bit_no) - 2**bit_no
+                lower = functools.reduce(lambda a, b: a + b, parts[first : first + 2**bit_no])
+                scale = level_scale(near_levels + 1 + bit_no, head_dim)
+                near_ref[0, block_no, bit_no] = (lower * scale).astype(bf16)
+            else:
+                near_ref[0, block_no, bit_no] = jnp.zeros((head_dim, head_dim), bf16)
+
+
+def forward_kernel(
+    length_ref, scale_ref, query_ref, grad_ref, key_ref, value_ref, key_prev_ref, value_prev_ref,
+    index_ref, table_ref, gain_ref, near_ref, far_ref,
+    mixed_ref, stat_ref, key_all, value_all, *, near_levels,
+):
+    block_no = pl.program_id(0)
+    head_no = pl.program_id(1)
+    group, rows, head_dim = key_ref.shape
+
+    @pl.when(block_no == 0)
+    def _():
+        fill(key_all.at[head_no], key_prev_ref, key_ref)
+        fill(value_all.at[head_no], value_prev_ref, value_ref)
+
+    query = query_ref[0]
+    span = length_ref[head_no]
+    window_scale = scale_ref[head_no]
+    row_pos, col_pos = positions(rows)
+    offset = row_pos - col_pos
+    start = pl.multiple_of(block_no * rows, rows)
+    total = jnp.zeros((rows, head_dim), f32)
+    for piece_no in range(group):
+        key_part = key_all[head_no, pl.ds(start + piece_no * rows, rows)]
+        value_part = value_all[head_no, pl.ds(start + piece_no * rows, rows)]
+        distance = (group - piece_no) * rows
+        scores = dot_nt(query, key_part)
+        if distance + rows > WINDOW // 2:
+            scores = jnp.where(offset < span - distance, scores, 0.0)
+        total = total + dot_nn(scores.astype(bf16), value_part)
+    weights = columns_of(lane_weights(lane_indices(index_ref[0]), table_ref))
+
+    def picked(level_no):
+        return weights[:, level_no : level_no + 1]
+
+    factor = diagonal_factor(row_pos, col_pos, picked, window_scale, near_levels, head_dim)
+    key_part = key_all[head_no, pl.ds(start + group * rows, rows)]
+    value_part = value_all[head_no, pl.ds(start + group * rows, rows)]
+    prob = (dot_nt(query, key_part) * factor).astype(bf16)
+    mixed = dot_nn(prob, value_part) + window_scale * total
+    for bit_no in range(group.bit_length() - 1):
+        mixed = mixed + picked(near_levels + 1 + bit_no) * dot_nn(query, near_ref[0, 0, bit_no])
+    mixed = mixed + picked(LEVELS - 1) * dot_nn(query, far_ref[0])
+    mixed_ref[0] = mixed
+    scaled = grad_ref[0].astype(f32) * gain_ref[0]
+    ones = jnp.ones((8, head_dim), bf16)
+    squares = dot_nt(ones, (mixed * mixed).astype(bf16))
+    crosses = dot_nt(ones, (scaled * mixed).astype(bf16))
+    stats = jnp.where(lax.broadcasted_iota(jnp.int32, squares.shape, 0) < 4, squares, crosses)
+
+    @pl.when(head_no == 0)
+    def _():
+        stat_ref[0] = stats
+
+    @pl.when(head_no > 0)
+    def _():
+        stat_ref[0] = stat_ref[0] + stats
+
+
+def norm_kernel(mixed_ref, grad_ref, stat_ref, gain_ref, out_ref, low_ref, gain_part_ref, *, width):
+    block_no = pl.program_id(1)
+    stats = columns_of(stat_ref[0])
+    inv_rms = lax.rsqrt(stats[:, 0:1] / width + epsilon)
+    pull = inv_rms * inv_rms * inv_rms * stats[:, 4:5] / width
+    mixed = mixed_ref[0]
+    grad = grad_ref[0].astype(f32)
+    gain = gain_ref[0]
+    normed = mixed * inv_rms
+    out_ref[0] = (normed * gain).astype(bf16)
+    low_ref[0] = (grad * gain * inv_rms - mixed * pull).astype(bf16)
+    part = jnp.sum(grad * normed, axis=0, keepdims=True)
+
+    @pl.when(block_no == 0)
+    def _():
+        gain_part_ref[0] = part
+
+    @pl.when(block_no > 0)
+    def _():
+        gain_part_ref[0] = gain_part_ref[0] + part
+
+
+def query_kernel(
+    length_ref, scale_ref, query_ref, low_ref, key_ref, value_ref, key_prev_ref, value_prev_ref,
+    index_ref, table_ref, near_ref, far_ref,
+    query_grad_ref, table_part_ref, near_grad_ref, far_grad_ref, key_all, value_all, *, near_levels,
+):
+    head_no = pl.program_id(0)
+    block_no = pl.program_id(1)
+    group, rows, head_dim = key_ref.shape
+
+    @pl.when(block_no == 0)
+    def _():
+        fill(key_all, key_prev_ref, key_ref)
+        fill(value_all, value_prev_ref, value_ref)
+
+    query = query_ref[0]
+    low = low_ref[0]
+    span = length_ref[head_no]
+    window_scale = scale_ref[head_no]
+    row_pos, col_pos = positions(rows)
+    offset = row_pos - col_pos
+    start = pl.multiple_of(block_no * rows, rows)
+    total = jnp.zeros((rows, head_dim), f32)
+    for piece_no in range(group):
+        key_part = key_all[pl.ds(start + piece_no * rows, rows)]
+        value_part = value_all[pl.ds(start + piece_no * rows, rows)]
+        distance = (group - piece_no) * rows
+        scores = dot_nt(low, value_part)
+        if distance + rows > WINDOW // 2:
+            scores = jnp.where(offset < span - distance, scores, 0.0)
+        total = total + dot_nn(scores.astype(bf16), key_part)
+    indices = lane_indices(index_ref[0])
+    weights = columns_of(lane_weights(indices, table_ref))
+
+    def picked(level_no):
+        return weights[:, level_no : level_no + 1]
+
+    factor = diagonal_factor(row_pos, col_pos, picked, window_scale, near_levels, head_dim)
+    key_part = key_all[pl.ds(start + group * rows, rows)]
+    value_part = value_all[pl.ds(start + group * rows, rows)]
+    prob_grad = dot_nt(low, value_part)
+    result = dot_nn((prob_grad * factor).astype(bf16), key_part) + window_scale * total
+    pairs = jnp.where(row_pos >= col_pos, dot_nt(query, key_part) * prob_grad, 0.0).astype(bf16)
+    leaf_count = rows // BLOCK
+    leaf_row = lax.broadcasted_iota(jnp.int32, (8, rows), 0)
+    leaf_col = lax.broadcasted_iota(jnp.int32, (8, rows), 1) // BLOCK
+    leaf_sums = dot_nt((leaf_row == leaf_col).astype(bf16), pairs)
+    level_rows = [jnp.zeros((1, rows), f32) for _ in range(LEVELS)]
+    own_leaf = leaf_col[:1]
+    for leaf_no in range(leaf_count):
+        leaf_sum = leaf_sums[leaf_no : leaf_no + 1]
+        apart = own_leaf ^ leaf_no
+        level_rows[0] = level_rows[0] + jnp.where(apart == 0, leaf_sum, 0.0)
+        for level_no in range(1, near_levels + 1):
+            here = (apart >> (level_no - 1)) == 1
+            level_rows[level_no] = level_rows[level_no] + jnp.where(here, leaf_sum, 0.0)
+    for level_no in range(near_levels + 1):
+        level_rows[level_no] = level_rows[level_no] * level_scale(level_no, head_dim)
+    ones = jnp.ones((8, head_dim), bf16)
+    query_wide = query.astype(f32)
+    low_wide = low.astype(f32)
+    states = [near_ref[0, 0, bit_no] for bit_no in range(group.bit_length() - 1)] + [far_ref[0]]
+    for state_no, state in enumerate(states):
+        level_no = near_levels + 1 + state_no
+        back = dot_nt(low, state)
+        result = result + picked(level_no) * back
+        level_rows[level_no] = dot_nt(ones, (query_wide * back).astype(bf16))[:1]
+        upstream = (picked(level_no) * low_wide).astype(bf16)
+        outer = dot_tn(query, upstream)
+        if state_no < len(states) - 1:
+            near_grad_ref[0, 0, state_no] = outer
+        else:
+            @pl.when(block_no == 0)
+            def _():
+                far_grad_ref[0] = outer
+
+            @pl.when(block_no > 0)
+            def _():
+                far_grad_ref[0] = far_grad_ref[0] + outer
+    query_grad_ref[0] = result.astype(bf16)
+    blank = jnp.zeros((8 - LEVELS, rows), f32)
+    weight_grad = jnp.concatenate(level_rows + [blank], axis=0)
+    lanes = table_part_ref.shape[-1]
+
+    @pl.when(block_no == 0)
+    def _():
+        table_part_ref[...] = jnp.zeros(table_part_ref.shape, f32)
+
+    for row_no in range(TABLE_ROWS):
+        chosen = jnp.where(indices == row_no, weight_grad, 0.0)
+        folded = functools.reduce(
+            lambda a, b: a + b, [chosen[:, i : i + lanes] for i in range(0, rows, lanes)]
+        )
+        table_part_ref[0, row_no] = table_part_ref[0, row_no] + folded
+
+
+def key_kernel(
+    length_ref, scale_ref, key_ref, value_ref, query_ref, low_ref, query_next_ref, low_next_ref,
+    index_ref, table_ref, near_grad_ref, far_grad_ref,
+    key_grad_ref, value_grad_ref, query_all, low_all, *, near_levels,
+):
+    head_no = pl.program_id(0)
+    block_no = pl.program_id(1)
+    group, rows, head_dim = query_ref.shape
+
+    @pl.when(block_no == 0)
+    def _():
+        fill(query_all, query_ref, query_next_ref)
+        fill(low_all, low_ref, low_next_ref)
+
+    key = key_ref[0]
+    value = value_ref[0]
+    span = length_ref[head_no]
+    window_scale = scale_ref[head_no]
+    row_pos, col_pos = positions(rows)
+    offset = col_pos - row_pos
+    start = pl.multiple_of(block_no * rows, rows)
+    key_total = jnp.zeros((rows, head_dim), f32)
+    value_total = jnp.zeros((rows, head_dim), f32)
+    for piece_no in range(1, group + 1):
+        query_part = query_all[pl.ds(start + piece_no * rows, rows)]
+        low_part = low_all[pl.ds(start + piece_no * rows, rows)]
+        distance = piece_no * rows
+        prob = dot_nt(key, query_part)
+        prob_grad = dot_nt(value, low_part)
+        if distance + rows > WINDOW // 2:
+            inside = offset < span - distance
+            prob = jnp.where(inside, prob, 0.0)
+            prob_grad = jnp.where(inside, prob_grad, 0.0)
+        value_total = value_total + dot_nn(prob.astype(bf16), low_part)
+        key_total = key_total + dot_nn(prob_grad.astype(bf16), query_part)
+    weights = lane_weights(lane_indices(index_ref[0]), table_ref)
+
+    def picked(level_no):
+        return weights[level_no : level_no + 1]
+
+    factor = diagonal_factor(col_pos, row_pos, picked, window_scale, near_levels, head_dim)
+    query_part = query_all[pl.ds(start, rows)]
+    low_part = low_all[pl.ds(start, rows)]
+    prob = (dot_nt(key, query_part) * factor).astype(bf16)
+    prob_grad = (dot_nt(value, low_part) * factor).astype(bf16)
+    state = far_grad_ref[0]
+    for bit_no in range(group.bit_length() - 1):
+        first = (block_no >> bit_no | 1) << bit_no
+        scale = jnp.where(
+            block_no >> bit_no & 1 == 0, level_scale(near_levels + 1 + bit_no, head_dim), 0.0
+        )
+        for step_no in range(2**bit_no):
+            state = state + near_grad_ref[0, first + step_no, bit_no] * scale
+    state = state.astype(bf16)
+    value_grad = dot_nn(prob, low_part) + window_scale * value_total + dot_nn(key, state)
+    key_grad = dot_nn(prob_grad, query_part) + window_scale * key_total + dot_nt(value, state)
+    value_grad_ref[0] = value_grad.astype(bf16)
+    key_grad_ref[0] = key_grad.astype(bf16)
+
+
+def grouped_shards(
+    query_rows, key_rows, value_rows, norm_gain, level_table, level_index, window_length, out_grad
+):
+    heads_here, rows, head_dim = query_rows.shape
+    group = WINDOW // rows
+    heads = heads_here // group
+    group_bits = group.bit_length() - 1
+    near_levels = (rows // BLOCK).bit_length() - 1
+    seq_count = lax.axis_size("seq")
+    chunk_bits = (seq_count // group).bit_length() - 1
+    seq_index = lax.axis_index("seq")
+    member = seq_index & (group - 1)
+    width = float(heads_here * lax.axis_size("head") * head_dim)
+
+    def swapped(shard, bits):
+        return lax.ppermute(shard, "seq", [(i, i ^ bits) for i in range(seq_count)])
+
+    def regrouped(payload):
+        pieces = [
+            swapped(lax.dynamic_index_in_dim(payload, member ^ bits, 0), bits)
+            for bits in range(1, group)
+        ]
+        own = lax.dynamic_index_in_dim(payload, member, 0)
+        result = lax.dynamic_update_slice_in_dim(jnp.zeros_like(payload), own, member, 0)
+        for bits in range(1, group):
+            result = lax.dynamic_update_slice_in_dim(result, pieces[bits - 1], member ^ bits, 0)
+        return result
+
+    def by_member(tensor):
+        return tensor.reshape(group, heads * rows, head_dim)
+
+    index_pad = jnp.pad(level_index.astype(bf16), ((0, 0), (0, 8 - LEVELS)))
+    index_pack = index_pad.reshape(rows // 128, 128, 8).transpose(0, 2, 1).reshape(index_rows, 128)
+    index_pack = jnp.broadcast_to(index_pack[None], (group, index_rows, 128))
+    pair = regrouped(jnp.concatenate([by_member(key_rows), by_member(value_rows)], axis=1))
+    rest = regrouped(
+        jnp.concatenate([by_member(query_rows), by_member(out_grad), index_pack], axis=1)
+    )
+    pair_prev = shifted(pair, "seq", group)
+    query_next = shifted(rest[:, : heads * rows], "seq", -group)
+
+    first_head = member * heads
+    table = lax.dynamic_slice_in_dim(level_table, first_head, heads, 1)
+    table = jnp.pad(table.transpose(1, 0, 2), ((0, 0), (0, 0), (0, 8 - LEVELS)))
+    table = jnp.broadcast_to(table[..., None], (heads, TABLE_ROWS, 8, 128))
+    gain = lax.dynamic_slice_in_dim(norm_gain, first_head, heads, 0)[:, None, :]
+    length = lax.dynamic_slice_in_dim(window_length, first_head, heads, 0)
+    scale = lax.rsqrt((head_dim * length).astype(f32))
+
+    smem = pl.BlockSpec(memory_space=pltpu.SMEM)
+    state_shape = (head_dim, head_dim)
+    chunk_shape = (group, heads * rows, head_dim)
+    near_shape = (heads, group, group_bits) + state_shape
+
+    def whole(first, head_of):
+        return pl.BlockSpec(
+            (group, rows, head_dim), lambda *pos: (0, first * heads + head_of(pos), 0)
+        )
+
+    def piece(first, head_of, block_of):
+        return pl.BlockSpec(
+            (1, rows, head_dim), lambda *pos: (block_of(pos), first * heads + head_of(pos), 0)
+        )
+
+    def per_head(shape, head_of):
+        return pl.BlockSpec((1,) + shape, lambda *pos: (head_of(pos),) + (0,) * len(shape))
+
+    def per_block(shape, head_of, block_of):
+        return pl.BlockSpec(
+            (1, 1) + shape, lambda *pos: (head_of(pos), block_of(pos)) + (0,) * len(shape)
+        )
+
+    def index_spec(block_of):
+        return pl.BlockSpec(
+            (1, index_rows, 128),
+            lambda *pos: (block_of(pos), 2 * heads * rows // index_rows, 0),
+        )
+
+    def axis0(pos):
+        return pos[0]
+
+    def axis1(pos):
+        return pos[1]
+
+    near, total = pl.pallas_call(
+        functools.partial(summary_kernel, near_levels=near_levels),
+        grid=(heads,),
+        in_specs=[whole(0, axis0), whole(1, axis0)],
+        out_specs=[
+            per_head((group, group_bits) + state_shape, axis0),
+            per_head(state_shape, axis0),
+        ],
+        out_shape=[
+            jax.ShapeDtypeStruct(near_shape, bf16),
+            jax.ShapeDtypeStruct((heads,) + state_shape, f32),
+        ],
+        name="summaries",
+    )(pair, pair)
+    far = jnp.zeros((heads,) + state_shape, f32)
+    running = total
+    for bit_no in range(chunk_bits):
+        partner = swapped(running.astype(bf16), group << bit_no).astype(f32)
+        upper = seq_index // group >> bit_no & 1 == 1
+        far_scale = level_scale(near_levels + group_bits + 1 + bit_no, head_dim)
+        far = far + jnp.where(upper, partner * far_scale, 0.0)
+        running = running + partner
+    far = far.astype(bf16)
+
+    mixed, stats = pl.pallas_call(
+        functools.partial(forward_kernel, near_levels=near_levels),
+        grid=(group, heads),
+        in_specs=[
+            smem,
+            smem,
+            piece(0, axis1, axis0),
+            piece(1, axis1, axis0),
+            whole(0, axis1),
+            whole(1, axis1),
+            whole(0, axis1),
+            whole(1, axis1),
+            index_spec(axis0),
+            per_head((TABLE_ROWS, 8, 128), axis1),
+            per_head((1, head_dim), axis1),
+            per_block((group_bits,) + state_shape, axis1, axis0),
+            per_head(state_shape, axis1),
+        ],
+        out_specs=[
+            piece(0, axis1, axis0),
+            pl.BlockSpec((1, 8, rows), lambda *pos: (pos[0], 0, 0)),
+        ],
+        out_shape=[
+            jax.ShapeDtypeStruct(chunk_shape, f32),
+            jax.ShapeDtypeStruct((group, 8, rows), f32),
+        ],
+        scratch_shapes=[
+            pltpu.VMEM((heads, 2 * group * rows, head_dim), bf16),
+            pltpu.VMEM((heads, 2 * group * rows, head_dim), bf16),
+        ],
+        name="forward",
+    )(length, scale, rest, rest, pair, pair, pair_prev, pair_prev, rest, table, gain, near, far)
+
+    for bit_no in range(group_bits):
+        stats = stats + swapped(stats, 1 << bit_no)
+    head_count = lax.axis_size("head")
+    part = stats
+    for step_no in range(1, head_count):
+        turn = [(i, (i + step_no) % head_count) for i in range(head_count)]
+        stats = stats + lax.ppermute(part, "head", turn)
+
+    layer_out, low, gain_part = pl.pallas_call(
+        functools.partial(norm_kernel, width=width),
+        grid=(heads, group),
+        in_specs=[
+            piece(0, axis0, axis1),
+            piece(1, axis0, axis1),
+            pl.BlockSpec((1, 8, rows), lambda *pos: (pos[1], 0, 0)),
+            per_head((1, head_dim), axis0),
+        ],
+        out_specs=[
+            piece(0, axis0, axis1),
+            piece(0, axis0, axis1),
+            per_head((1, head_dim), axis0),
+        ],
+        out_shape=[
+            jax.ShapeDtypeStruct(chunk_shape, bf16),
+            jax.ShapeDtypeStruct(chunk_shape, bf16),
+            jax.ShapeDtypeStruct((heads, 1, head_dim), f32),
+        ],
+        name="norm",
+    )(mixed, rest, stats, gain)
+    low_next = shifted(low, "seq", -group)
+
+    query_grad, table_part, near_grad, far_part = pl.pallas_call(
+        functools.partial(query_kernel, near_levels=near_levels),
+        grid=(heads, group),
+        in_specs=[
+            smem,
+            smem,
+            piece(0, axis0, axis1),
+            piece(0, axis0, axis1),
+            whole(0, axis0),
+            whole(1, axis0),
+            whole(0, axis0),
+            whole(1, axis0),
+            index_spec(axis1),
+            per_head((TABLE_ROWS, 8, 128), axis0),
+            per_block((group_bits,) + state_shape, axis0, axis1),
+            per_head(state_shape, axis0),
+        ],
+        out_specs=[
+            piece(0, axis0, axis1),
+            per_head((TABLE_ROWS, 8, 128), axis0),
+            per_block((group_bits,) + state_shape, axis0, axis1),
+            per_head(state_shape, axis0),
+        ],
+        out_shape=[
+            jax.ShapeDtypeStruct(chunk_shape, bf16),
+            jax.ShapeDtypeStruct((heads, TABLE_ROWS, 8, 128), f32),
+            jax.ShapeDtypeStruct(near_shape, f32),
+            jax.ShapeDtypeStruct((heads,) + state_shape, f32),
+        ],
+        scratch_shapes=[
+            pltpu.VMEM((2 * group * rows, head_dim), bf16),
+            pltpu.VMEM((2 * group * rows, head_dim), bf16),
+        ],
+        name="query_side",
+    )(length, scale, rest, low, pair, pair, pair_prev, pair_prev, rest, table, near, far)
+
+    table_sum = jnp.sum(table_part, axis=-1)
+    table_sum = jnp.pad(table_sum, ((0, 0), (0, 0), (0, head_dim - 8)))
+    running = jnp.concatenate([far_part, table_sum, gain_part], axis=1)
+    far_grad = jnp.zeros((heads,) + state_shape, f32)
+    for bit_no in range(chunk_bits):
+        partner = swapped(running, group << bit_no)
+        lower = seq_index // group >> bit_no & 1 == 0
+        far_scale = level_scale(near_levels + group_bits + 1 + bit_no, head_dim)
+        far_grad = far_grad + jnp.where(lower, partner[:, :head_dim] * far_scale, 0.0)
+        running = running + partner
+    small = running[:, head_dim:]
+
+    key_grad, value_grad = pl.pallas_call(
+        functools.partial(key_kernel, near_levels=near_levels),
+        grid=(heads, group),
+        in_specs=[
+            smem,
+            smem,
+            piece(0, axis0, axis1),
+            piece(1, axis0, axis1),
+            whole(0, axis0),
+            whole(0, axis0),
+            whole(0, axis0),
+            whole(0, axis0),
+            index_spec(axis1),
+            per_head((TABLE_ROWS, 8, 128), axis0),
+            per_head((group, group_bits) + state_shape, axis0),
+            per_head(state_shape, axis0),
+        ],
+        out_specs=[piece(0, axis0, axis1), piece(0, axis0, axis1)],
+        out_shape=[jax.ShapeDtypeStruct(chunk_shape, bf16)] * 2,
+        scratch_shapes=[
+            pltpu.VMEM((2 * group * rows, head_dim), bf16),
+            pltpu.VMEM((2 * group * rows, head_dim), bf16),
+        ],
+        name="key_side",
+    )(
+        length, scale, pair, pair, rest, low, query_next, low_next, rest, table, near_grad, far_grad
+    )
+
+    half = heads * rows
+    first_out = regrouped(jnp.concatenate([layer_out, query_grad], axis=1))
+    last_out = regrouped(jnp.concatenate([key_grad, value_grad], axis=1))
+    small = regrouped(jnp.broadcast_to(small[None], (group,) + small.shape))
+    small = small.reshape((heads_here,) + small.shape[2:])
+
+    def by_head(payload):
+        return payload.reshape(query_rows.shape)
+
+    return (
+        by_head(first_out[:, :half]),
+        by_head(first_out[:, half:]),
+        by_head(last_out[:, :half]),
+        by_head(last_out[:, half:]),
+        small[:, :TABLE_ROWS, :LEVELS].transpose(1, 0, 2),
+        small[:, TABLE_ROWS],
+    )
+
+
+def fits_groups(heads_here, rows, seq_count):
+    group = WINDOW // rows
+    levels_fit = (WINDOW // BLOCK).bit_length() + 1 == LEVELS
+    return (
+        group * rows == WINDOW
+        and rows == 2 * 128
+        and group == 1 << (group.bit_length() - 1)
+        and heads_here % group == 0
+        and seq_count % group == 0
+        and seq_count == 1 << (seq_count.bit_length() - 1)
+        and levels_fit
+    )
+
+
+def shards(query_rows, *others):
+    heads_here, rows, _ = query_rows.shape
+    if fits_groups(heads_here, rows, lax.axis_size("seq")):
+        return grouped_shards(query_rows, *others)
+    return wide_shards(query_rows, *others)
+
+
 def solution(mesh):
     placed = (
         P("head", "seq", None),

time: 524 us -> 177 us (0.34)
  matrix products: 128 us -> 0 us
  blocking collectives: 77 us -> 0 us
  waiting for transfers between devices: 139 us -> 64.3 us
  local copies, waits for them, and re-layouts: 74.6 us -> 18.1 us
  Pallas kernels: 0 us -> 44.3 us
  other arithmetic: 35.6 us -> 8.01 us
  starting transfers between devices: 53.9 us -> 39.8 us
  loops' own time: 11.3 us -> 0 us
    dot_general x80 -> x0, matrix products: 128 us -> none  [the longest x78 128 us: contract(): jnp.einsum(pattern, left_side, right_side, preferred_element_type=jnp.flo...]
    psum x3 -> x0, blocking collectives: 77 us -> none  [the longest x1 71.9 us: shards(): table_grad, gain_grad = lax.psum((table_part, gain_part), 'seq')]
    ppermute x8 -> x22, waiting for transfers between devices: 139 us -> 64.3 us  [the longest x21 63.1 us: swapped(): return lax.ppermute(shard, 'seq', [(i, i ^ bits) for i in range(seq_count)])]
    pallas_call x0 -> x5, Pallas kernels: none -> 44.3 us  [the longest x1 12.6 us: grouped_shards(): pl.pallas_call(functools.partial(query_kernel, near_levels=near_levels),...]
    reshape x10 -> x0, local copies, waits for them, and re-layouts: 24.3 us -> none  [the longest x2 5.64 us: level_grads(): jnp.stack([value_low, blank], axis=2).reshape(full_shape)]
    ppermute x8 -> x3, starting transfers between devices: 22.6 us -> 6.25 us  [shifted(): return lax.ppermute(block, axis, route)]
    unnamed x121 -> x42, local copies, waits for them, and re-layouts: 19.4 us -> 5.19 us
    another operation x9 -> x3, local copies, waits for them, and re-layouts: 12.5 us -> 0.41 us  [the longest x2 4.25 us: level_area(): jnp.stack([jnp.zeros_like(upper_half), upper_half], axis=2)]
  transfers between devices with their start and end apart: 16 -> 25, of which waited for: 5 -> 13; matrix products, arithmetic and copies ran while one was open for 22% -> 8% of each run, Pallas kernels for 0% -> 1%
where the time goes in v1:
time: 177 us; the launch traced here: 176 us
  waiting for transfers between devices  64.3 us (36%)
  Pallas kernels  44.3 us (25%)
  starting transfers between devices  39.8 us (22%)
  local copies, waits for them, and re-layouts  18.1 us (10%)
  other arithmetic  8.01 us (5%)
    ppermute x21, waiting for transfers between devices, swapped(): return lax.ppermute(shard, 'seq', [(i, i ^ bits) for i in range(seq_count)])  63.1 us
    ppermute x21, starting transfers between devices, swapped(): return lax.ppermute(shard, 'seq', [(i, i ^ bits) for i in range(seq_count)])  33.5 us
    pallas_call x1, Pallas kernels, grouped_shards(): pl.pallas_call(functools.partial(query_kernel, near_levels=near_levels),...  12.6 us
    pallas_call x1, Pallas kernels, grouped_shards(): pl.pallas_call(functools.partial(key_kernel, near_levels=near_levels), gr...  12.1 us
    pallas_call x1, Pallas kernels, grouped_shards(): pl.pallas_call(functools.partial(forward_kernel, near_levels=near_levels)...  10.8 us
    pallas_call x1, Pallas kernels, grouped_shards(): pl.pallas_call(functools.partial(norm_kernel, width=width), grid=(heads,...  6.5 us
    ppermute x3, starting transfers between devices, shifted(): return lax.ppermute(block, axis, route)  6.25 us
    dynamic_update_slice x15, local copies, waits for them, and re-layouts, regrouped(): lax.dynamic_update_slice_in_dim(result, pieces[bits - 1], member ^ bits, 0)  5.25 us
  transfers between devices with their start and end apart: 25, of which 13 were waited for; matrix products, arithmetic and copies ran while one was open for 8% of the time, Pallas kernels for 1%

profile of v1, /device:TPU:0, one launch (start us, length us, event | category | flops | bytes accessed | tf_op | source)
XLA Modules:
  0.0 175.6 jit_solution(4235575963457404920)
XLA Ops:
  2.8 3.0 %collective-permute-start.3 = (bf16[1,1024,128]{2,1,0:T(8,128)(2,1)}, bf16[1,1024,128]{2,1,0:T(8,128)(2,1)}, u32[]{:S(2)}, u32[]{:S(2)}) collective-permute-start(bf16[1,1024,128]{2,1,0:T(8,128)(2,1)} %get-tuple-element.58), channel_id=1, source_target_pairs={{0,2},{2,0},{4,6},{6,4},{8,10},{10,8},{12,14},{14,12},{16,18},{18,... | collective-permute-start | bytes 786440 | tf_op jit(solution)/shard_map/ppermute | solution.py:604
  7.6 2.0 %collective-permute-start = (bf16[1,1040,128]{2,1,0:T(8,128)(2,1)S(1)}, bf16[1,1040,128]{2,1,0:T(8,128)(2,1)S(1)}, u32[]{:S(2)}, u32[]{:S(2)}) collective-permute-start(bf16[1,1040,128]{2,1,0:T(8,128)(2,1)S(1)} %get-tuple-element.42), channel_id=1, source_target_pairs={{0,2},{2,0},{4,6},{6,4},{8,10},{10,8},{12,14},{14,12},{16,18},{18,... | collective-permute-start | bytes 798728 | tf_op jit(solution)/shard_map/ppermute | solution.py:604
  13.2 2.9 %collective-permute-start.2 = (bf16[1,1040,128]{2,1,0:T(8,128)(2,1)S(1)}, bf16[1,1040,128]{2,1,0:T(8,128)(2,1)}, u32[]{:S(2)}, u32[]{:S(2)}) collective-permute-start(bf16[1,1040,128]{2,1,0:T(8,128)(2,1)S(1)} %get-tuple-element.40), channel_id=1, source_target_pairs={{0,6},{2,4},{4,2},{6,0},{8,14},{10,12},{12,10},{14,8},{16,22},{18,... | collective-permute-start | bytes 798728 | tf_op jit(solution)/shard_map/ppermute | solution.py:604
  17.2 3.7 %collective-permute-done.4 = bf16[1,1024,128]{2,1,0:T(8,128)(2,1)} collective-permute-done((bf16[1,1024,128]{2,1,0:T(8,128)(2,1)}, bf16[1,1024,128]{2,1,0:T(8,128)(2,1)}, u32[]{:S(2)}, u32[]{:S(2)}) %collective-permute-start.4) | collective-permute-done | bytes 262176 | tf_op jit(solution)/shard_map/ppermute | solution.py:604
  23.8 2.3 %summaries.1 = (bf16[2,4,2,128,128]{4,3,2,1,0:T(8,128)(2,1)}, f32[2,128,128]{2,1,0:T(8,128)}) custom-call(bf16[4,1024,128]{2,1,0:T(8,128)(2,1)} %copy-done.2, bf16[4,1024,128]{2,1,0:T(8,128)(2,1)} %copy-done.2), custom_call_target="tpu_custom_call" | custom-call | tf_op jit(solution)/shard_map/summaries/pallas_call | solution.py:673
  26.1 3.7 %collective-permute-start.6 = (bf16[4,1024,128]{2,1,0:T(8,128)(2,1)}, bf16[4,1024,128]{2,1,0:T(8,128)(2,1)S(1)}, u32[]{:S(2)}, u32[]{:S(2)}) collective-permute-start(bf16[4,1024,128]{2,1,0:T(8,128)(2,1)} %copy-done.2), channel_id=1, source_target_pairs={{0,8},{2,10},{4,12},{6,14},{8,16},{10,18},{12,20},{14,22},{16,24},... | collective-permute-start | bytes 3145736 | tf_op jit(solution)/shard_map/ppermute | solution.py:25
  30.7 1.6 collective-permute-start.7
  32.4 18.6 %collective-permute-done.7 = bf16[2,128,128]{2,1,0:T(8,128)(2,1)S(1)} collective-permute-done((bf16[2,128,128]{2,1,0:T(8,128)(2,1)S(1)}, bf16[2,128,128]{2,1,0:T(8,128)(2,1)S(1)}, u32[]{:S(2)}, u32[]{:S(2)}) %collective-permute-start.7) | collective-permute-done | bytes 65568 | tf_op jit(solution)/shard_map/ppermute | solution.py:604
  51.0 2.7 %collective-permute-start.8 = (bf16[2,128,128]{2,1,0:T(8,128)(2,1)S(1)}, bf16[2,128,128]{2,1,0:T(8,128)(2,1)S(1)}, u32[]{:S(2)}, u32[]{:S(2)}) collective-permute-start(bf16[2,128,128]{2,1,0:T(8,128)(2,1)S(1)} %fusion.10), channel_id=1, source_target_pairs={{0,16},{2,18},{4,20},{6,22},{8,24},{10,26},{12,28},{14,30},{16,0},... | collective-permute-start | bytes 196616 | tf_op jit(solution)/shard_map/ppermute | solution.py:604
  54.6 1.6 collective-permute-done.8
  57.9 10.8 %forward.1 = (f32[4,512,128]{2,1,0:T(8,128)}, f32[4,8,256]{2,1,0:T(8,128)}) custom-call(s32[2]{0:T(128)} %get-tuple-element.39.length_ref, f32[2]{0:T(128)} %get-tuple-element.38.scale_ref, bf16[4,1040,128]{2,1,0:T(8,128)(2,1)} %copy-done.1, bf16[4,1040,128]{2,1,0:T(8,128)(2,1)} %copy-done.1, bf16[4,1024,128]{2,1,0:T(8,128)(2,1)} %copy-done.2, ...), custom_call_target="tpu_custom_call" | custom-call | tf_op jit(solution)/shard_map/forward/pallas_call | solution.py:697
  69.8 3.1 %collective-permute-done.9 = f32[4,8,256]{2,1,0:T(8,128)S(1)} collective-permute-done((f32[4,8,256]{2,1,0:T(8,128)}, f32[4,8,256]{2,1,0:T(8,128)S(1)}, u32[]{:S(2)}, u32[]{:S(2)}) %collective-permute-start.9) | collective-permute-done | bytes 32800 | tf_op jit(solution)/shard_map/ppermute | solution.py:604
  74.1 3.4 %collective-permute-done.10 = f32[4,8,256]{2,1,0:T(8,128)S(1)} collective-permute-done((f32[4,8,256]{2,1,0:T(8,128)S(1)}, f32[4,8,256]{2,1,0:T(8,128)S(1)}, u32[]{:S(2)}, u32[]{:S(2)}) %collective-permute-start.10) | collective-permute-done | bytes 32800 | tf_op jit(solution)/shard_map/ppermute | solution.py:604
  79.4 6.5 %norm.1 = (bf16[4,512,128]{2,1,0:T(8,128)(2,1)}, bf16[4,512,128]{2,1,0:T(8,128)(2,1)}, f32[2,1,128]{2,1,0:T(1,128)}) custom-call(f32[4,512,128]{2,1,0:T(8,128)} %get-tuple-element.21.mixed_ref, bf16[4,1040,128]{2,1,0:T(8,128)(2,1)} %copy-done.1, f32[4,8,256]{2,1,0:T(8,128)} %add.96.stat_ref, f32[2,1,128]{2,1,0:T(1,128)} %bitcast.35), custom_call_target="tpu_custom_call" | custom-call | tf_op jit(solution)/shard_map/norm/pallas_call | solution.py:738
  85.9 12.6 %query_side.1 = (bf16[4,512,128]{2,1,0:T(8,128)(2,1)}, f32[2,16,8,128]{3,2,1,0:T(8,128)}, f32[2,4,2,128,128]{4,3,2,1,0:T(8,128)}, f32[2,128,128]{2,1,0:T(8,128)}) custom-call(s32[2]{0:T(128)} %get-tuple-element.39.length_ref, f32[2]{0:T(128)} %get-tuple-element.38.scale_ref, bf16[4,1040,128]{2,1,0:T(8,128)(2,1)} %copy-done.1, ...), custom_call_target="tpu_custom_call" | custom-call | tf_op jit(solution)/shard_map/query_side/pallas_call | solution.py:761
  99.6 1.6 fusion.5
  101.2 2.5 %collective-permute-start.17 = (f32[2,145,128]{2,1,0:T(8,128)}, f32[2,145,128]{2,1,0:T(8,128)S(1)}, u32[]{:S(2)}, u32[]{:S(2)}) collective-permute-start(f32[2,145,128]{2,1,0:T(8,128)} %fusion.5), channel_id=1, source_target_pairs={{0,8},{2,10},{4,12},{6,14},{8,0},{10,2},{12,4},{14,6},{16,24},{18,... | collective-permute-start | bytes 445448 | tf_op jit(solution)/shard_map/ppermute | solution.py:604
  113.2 3.6 %collective-permute-start.18 = (f32[2,145,128]{2,1,0:T(8,128)S(1)}, f32[2,145,128]{2,1,0:T(8,128)S(1)}, u32[]{:S(2)}, u32[]{:S(2)}) collective-permute-start(f32[2,145,128]{2,1,0:T(8,128)S(1)} %fusion.16), channel_id=1, source_target_pairs={{0,16},{2,18},{4,20},{6,22},{8,24},{10,26},{12,28},{14,30},{16,0},... | collective-permute-start | bytes 445448 | tf_op jit(solution)/shard_map/ppermute | solution.py:604
  117.8 5.2 %collective-permute-done.13 = bf16[1,1024,128]{2,1,0:T(8,128)(2,1)S(1)} collective-permute-done((bf16[1,1024,128]{2,1,0:T(8,128)(2,1)S(1)}, bf16[1,1024,128]{2,1,0:T(8,128)(2,1)S(1)}, u32[]{:S(2)}, u32[]{:S(2)}) %collective-permute-start.13) | collective-permute-done | bytes 262176 | tf_op jit(solution)/shard_map/ppermute | solution.py:604
  124.1 16.5 %collective-permute-done.18 = f32[2,145,128]{2,1,0:T(8,128)S(1)} collective-permute-done((f32[2,145,128]{2,1,0:T(8,128)S(1)}, f32[2,145,128]{2,1,0:T(8,128)S(1)}, u32[]{:S(2)}, u32[]{:S(2)}) %collective-permute-start.18) | collective-permute-done | bytes 148512 | tf_op jit(solution)/shard_map/ppermute | solution.py:604
  142.5 1.7 collective-permute-start.24
  148.2 12.1 %key_side.1 = (bf16[4,512,128]{2,1,0:T(8,128)(2,1)}, bf16[4,512,128]{2,1,0:T(8,128)(2,1)}) custom-call(s32[2]{0:T(128)} %get-tuple-element.39.length_ref, f32[2]{0:T(128)} %get-tuple-element.38.scale_ref, bf16[4,1024,128]{2,1,0:T(8,128)(2,1)} %copy-done.2, bf16[4,1024,128]{2,1,0:T(8,128)(2,1)} %copy-done.2, bf16[4,1040,128]{2,1,0:T(8,128)(2,1)} %copy-done.1, ...), custom_call_target="tpu_custom_call" | custom-call | tf_op jit(solution)/shard_map/key_side/pallas_call | solution.py:809
  166.7 3.5 %collective-permute-done.19 = bf16[1,1024,128]{2,1,0:T(8,128)(2,1)S(1)} collective-permute-done((bf16[1,1024,128]{2,1,0:T(8,128)(2,1)S(1)}, bf16[1,1024,128]{2,1,0:T(8,128)(2,1)S(1)}, u32[]{:S(2)}, u32[]{:S(2)}) %collective-permute-start.19) | collective-permute-done | bytes 262176 | tf_op jit(solution)/shard_map/ppermute | solution.py:604
  170.3 4.1 %collective-permute-done.20 = bf16[1,1024,128]{2,1,0:T(8,128)(2,1)S(1)} collective-permute-done((bf16[1,1024,128]{2,1,0:T(8,128)(2,1)S(1)}, bf16[1,1024,128]{2,1,0:T(8,128)(2,1)S(1)}, u32[]{:S(2)}, u32[]{:S(2)}) %collective-permute-start.20) | collective-permute-done | bytes 262176 | tf_op jit(solution)/shard_map/ppermute | solution.py:604
  (125 shorter events, 45.2 us)
Async XLA Ops:
  2.8 10.5 %collective-permute-start.3 = (bf16[1,1024,128]{2,1,0:T(8,128)(2,1)}, bf16[1,1024,128]{2,1,0:T(8,128)(2,1)}, u32[]{:S(2)}, u32[]{:S(2)}) collective-permute-start(bf16[1,1024,128]{2,1,0:T(8,128)(2,1)} %get-tuple-element.58), channel_id=1, source_target_pairs={{0,2},{2,0},{4,6},{6,4},{8,10},{10,8},{12,14},{14,12},{16,18},{18,... | collective-permute-start | bytes 786440 | tf_op jit(solution)/shard_map/ppermute | solution.py:604
  5.7 15.1 %collective-permute-start.4 = (bf16[1,1024,128]{2,1,0:T(8,128)(2,1)}, bf16[1,1024,128]{2,1,0:T(8,128)(2,1)}, u32[]{:S(2)}, u32[]{:S(2)}) collective-permute-start(bf16[1,1024,128]{2,1,0:T(8,128)(2,1)} %get-tuple-element.59), channel_id=1, source_target_pairs={{0,4},{2,6},{4,0},{6,2},{8,12},{10,14},{12,8},{14,10},{16,20},{18,... | collective-permute-start | bytes 786440 | tf_op jit(solution)/shard_map/ppermute | solution.py:604
  7.2 14.6 %collective-permute-start.5 = (bf16[1,1024,128]{2,1,0:T(8,128)(2,1)}, bf16[1,1024,128]{2,1,0:T(8,128)(2,1)}, u32[]{:S(2)}, u32[]{:S(2)}) collective-permute-start(bf16[1,1024,128]{2,1,0:T(8,128)(2,1)} %get-tuple-element.56), channel_id=1, source_target_pairs={{0,6},{2,4},{4,2},{6,0},{8,14},{10,12},{12,10},{14,8},{16,22},{18,... | collective-permute-start | bytes 786440 | tf_op jit(solution)/shard_map/ppermute | solution.py:604
  7.6 24.6 %collective-permute-start = (bf16[1,1040,128]{2,1,0:T(8,128)(2,1)S(1)}, bf16[1,1040,128]{2,1,0:T(8,128)(2,1)S(1)}, u32[]{:S(2)}, u32[]{:S(2)}) collective-permute-start(bf16[1,1040,128]{2,1,0:T(8,128)(2,1)S(1)} %get-tuple-element.42), channel_id=1, source_target_pairs={{0,2},{2,0},{4,6},{6,4},{8,10},{10,8},{12,14},{14,12},{16,18},{18,... | collective-permute-start | bytes 798728 | tf_op jit(solution)/shard_map/ppermute | solution.py:604
  9.7 22.6 %collective-permute-start.1 = (bf16[1,1040,128]{2,1,0:T(8,128)(2,1)S(1)}, bf16[1,1040,128]{2,1,0:T(8,128)(2,1)S(1)}, u32[]{:S(2)}, u32[]{:S(2)}) collective-permute-start(bf16[1,1040,128]{2,1,0:T(8,128)(2,1)S(1)} %get-tuple-element.41), channel_id=1, source_target_pairs={{0,4},{2,6},{4,0},{6,2},{8,12},{10,14},{12,8},{14,10},{16,20},{18,... | collective-permute-start | bytes 798728 | tf_op jit(solution)/shard_map/ppermute | solution.py:604
  13.2 40.4 %collective-permute-start.2 = (bf16[1,1040,128]{2,1,0:T(8,128)(2,1)S(1)}, bf16[1,1040,128]{2,1,0:T(8,128)(2,1)}, u32[]{:S(2)}, u32[]{:S(2)}) collective-permute-start(bf16[1,1040,128]{2,1,0:T(8,128)(2,1)S(1)} %get-tuple-element.40), channel_id=1, source_target_pairs={{0,6},{2,4},{4,2},{6,0},{8,14},{10,12},{12,10},{14,8},{16,22},{18,... | collective-permute-start | bytes 798728 | tf_op jit(solution)/shard_map/ppermute | solution.py:604
  26.1 30.8 %collective-permute-start.6 = (bf16[4,1024,128]{2,1,0:T(8,128)(2,1)}, bf16[4,1024,128]{2,1,0:T(8,128)(2,1)S(1)}, u32[]{:S(2)}, u32[]{:S(2)}) collective-permute-start(bf16[4,1024,128]{2,1,0:T(8,128)(2,1)} %copy-done.2), channel_id=1, source_target_pairs={{0,8},{2,10},{4,12},{6,14},{8,16},{10,18},{12,20},{14,22},{16,24},... | collective-permute-start | bytes 3145736 | tf_op jit(solution)/shard_map/ppermute | solution.py:25
  30.7 20.3 %collective-permute-start.7 = (bf16[2,128,128]{2,1,0:T(8,128)(2,1)S(1)}, bf16[2,128,128]{2,1,0:T(8,128)(2,1)S(1)}, u32[]{:S(2)}, u32[]{:S(2)}) collective-permute-start(bf16[2,128,128]{2,1,0:T(8,128)(2,1)S(1)} %convert_element_type.29), channel_id=1, source_target_pairs={{0,8},{2,10},{4,12},{6,14},{8,0},{10,2},{12,4},{14,6},{16,24},{18,... | collective-permute-start | bytes 196616 | tf_op jit(solution)/shard_map/ppermute | solution.py:604
  51.0 5.2 %collective-permute-start.8 = (bf16[2,128,128]{2,1,0:T(8,128)(2,1)S(1)}, bf16[2,128,128]{2,1,0:T(8,128)(2,1)S(1)}, u32[]{:S(2)}, u32[]{:S(2)}) collective-permute-start(bf16[2,128,128]{2,1,0:T(8,128)(2,1)S(1)} %fusion.10), channel_id=1, source_target_pairs={{0,16},{2,18},{4,20},{6,22},{8,24},{10,26},{12,28},{14,30},{16,0},... | collective-permute-start | bytes 196616 | tf_op jit(solution)/shard_map/ppermute | solution.py:604
  68.7 4.2 %collective-permute-start.9 = (f32[4,8,256]{2,1,0:T(8,128)}, f32[4,8,256]{2,1,0:T(8,128)S(1)}, u32[]{:S(2)}, u32[]{:S(2)}) collective-permute-start(f32[4,8,256]{2,1,0:T(8,128)} %get-tuple-element.22), channel_id=1, source_target_pairs={{0,2},{2,0},{4,6},{6,4},{8,10},{10,8},{12,14},{14,12},{16,18},{18,... | collective-permute-start | bytes 98312 | tf_op jit(solution)/shard_map/ppermute | solution.py:604
  73.6 3.9 %collective-permute-start.10 = (f32[4,8,256]{2,1,0:T(8,128)S(1)}, f32[4,8,256]{2,1,0:T(8,128)S(1)}, u32[]{:S(2)}, u32[]{:S(2)}) collective-permute-start(f32[4,8,256]{2,1,0:T(8,128)S(1)} %add.94), channel_id=1, source_target_pairs={{0,4},{2,6},{4,0},{6,2},{8,12},{10,14},{12,8},{14,10},{16,20},{18,... | collective-permute-start | bytes 98312 | tf_op jit(solution)/shard_map/ppermute | solution.py:604
  101.2 9.3 %collective-permute-start.17 = (f32[2,145,128]{2,1,0:T(8,128)}, f32[2,145,128]{2,1,0:T(8,128)S(1)}, u32[]{:S(2)}, u32[]{:S(2)}) collective-permute-start(f32[2,145,128]{2,1,0:T(8,128)} %fusion.5), channel_id=1, source_target_pairs={{0,8},{2,10},{4,12},{6,14},{8,0},{10,2},{12,4},{14,6},{16,24},{18,... | collective-permute-start | bytes 445448 | tf_op jit(solution)/shard_map/ppermute | solution.py:604
  104.8 8.5 %collective-permute-start.12 = (bf16[1,1024,128]{2,1,0:T(8,128)(2,1)}, bf16[1,1024,128]{2,1,0:T(8,128)(2,1)}, u32[]{:S(2)}, u32[]{:S(2)}) collective-permute-start(bf16[1,1024,128]{2,1,0:T(8,128)(2,1)} %get-tuple-element.54), channel_id=1, source_target_pairs={{0,2},{2,0},{4,6},{6,4},{8,10},{10,8},{12,14},{14,12},{16,18},{18,... | collective-permute-start | bytes 786440 | tf_op jit(solution)/shard_map/ppermute | solution.py:604
  106.9 40.3 %collective-permute-start.15 = (bf16[4,512,128]{2,1,0:T(8,128)(2,1)S(1)}, bf16[4,512,128]{2,1,0:T(8,128)(2,1)S(1)}, u32[]{:S(2)}, u32[]{:S(2)}) collective-permute-start(bf16[4,512,128]{2,1,0:T(8,128)(2,1)S(1)} %slice.42), channel_id=1, source_target_pairs={{8,0},{10,2},{12,4},{14,6},{16,8},{18,10},{20,12},{22,14},{24,16},... | collective-permute-start | bytes 1572872 | tf_op jit(solution)/shard_map/ppermute | solution.py:25
  108.2 39.0 %collective-permute-start.16 = (bf16[4,512,128]{2,1,0:T(8,128)(2,1)S(1)}, bf16[4,512,128]{2,1,0:T(8,128)(2,1)S(1)}, u32[]{:S(2)}, u32[]{:S(2)}) collective-permute-start(bf16[4,512,128]{2,1,0:T(8,128)(2,1)S(1)} %copy-done.4), channel_id=1, source_target_pairs={{8,0},{10,2},{12,4},{14,6},{16,8},{18,10},{20,12},{22,14},{24,16},... | collective-permute-start | bytes 1572872 | tf_op jit(solution)/shard_map/ppermute | solution.py:25
  109.5 13.5 %collective-permute-start.13 = (bf16[1,1024,128]{2,1,0:T(8,128)(2,1)S(1)}, bf16[1,1024,128]{2,1,0:T(8,128)(2,1)S(1)}, u32[]{:S(2)}, u32[]{:S(2)}) collective-permute-start(bf16[1,1024,128]{2,1,0:T(8,128)(2,1)S(1)} %get-tuple-element.53), channel_id=1, source_target_pairs={{0,4},{2,6},{4,0},{6,2},{8,12},{10,14},{12,8},{14,10},{16,20},{18,... | collective-permute-start | bytes 786440 | tf_op jit(solution)/shard_map/ppermute | solution.py:604
  110.5 12.5 %collective-permute-start.14 = (bf16[1,1024,128]{2,1,0:T(8,128)(2,1)S(1)}, bf16[1,1024,128]{2,1,0:T(8,128)(2,1)S(1)}, u32[]{:S(2)}, u32[]{:S(2)}) collective-permute-start(bf16[1,1024,128]{2,1,0:T(8,128)(2,1)S(1)} %get-tuple-element.52), channel_id=1, source_target_pairs={{0,6},{2,4},{4,2},{6,0},{8,14},{10,12},{12,10},{14,8},{16,22},{18,... | collective-permute-start | bytes 786440 | tf_op jit(solution)/shard_map/ppermute | solution.py:604
  113.2 27.5 %collective-permute-start.18 = (f32[2,145,128]{2,1,0:T(8,128)S(1)}, f32[2,145,128]{2,1,0:T(8,128)S(1)}, u32[]{:S(2)}, u32[]{:S(2)}) collective-permute-start(f32[2,145,128]{2,1,0:T(8,128)S(1)} %fusion.16), channel_id=1, source_target_pairs={{0,16},{2,18},{4,20},{6,22},{8,24},{10,26},{12,28},{14,30},{16,0},... | collective-permute-start | bytes 445448 | tf_op jit(solution)/shard_map/ppermute | solution.py:604
  140.7 4.2 %collective-permute-start.22 = (f32[1,2,17,128]{3,2,1,0:T(8,128)S(1)}, f32[1,2,17,128]{3,2,1,0:T(8,128)S(1)}, u32[]{:S(2)}, u32[]{:S(2)}) collective-permute-start(f32[1,2,17,128]{3,2,1,0:T(8,128)S(1)} %fusion.14), channel_id=1, source_target_pairs={{0,2},{2,0},{4,6},{6,4},{8,10},{10,8},{12,14},{14,12},{16,18},{18,... | collective-permute-start | bytes 52232 | tf_op jit(solution)/shard_map/ppermute | solution.py:604
  142.0 3.8 %collective-permute-start.23 = (f32[1,2,17,128]{3,2,1,0:T(8,128)S(1)}, f32[1,2,17,128]{3,2,1,0:T(8,128)S(1)}, u32[]{:S(2)}, u32[]{:S(2)}) collective-permute-start(f32[1,2,17,128]{3,2,1,0:T(8,128)S(1)} %fusion.14), channel_id=1, source_target_pairs={{0,4},{2,6},{4,0},{6,2},{8,12},{10,14},{12,8},{14,10},{16,20},{18,... | collective-permute-start | bytes 52232 | tf_op jit(solution)/shard_map/ppermute | solution.py:604
  142.5 4.7 %collective-permute-start.24 = (f32[1,2,17,128]{3,2,1,0:T(8,128)S(1)}, f32[1,2,17,128]{3,2,1,0:T(8,128)S(1)}, u32[]{:S(2)}, u32[]{:S(2)}) collective-permute-start(f32[1,2,17,128]{3,2,1,0:T(8,128)S(1)} %fusion.14), channel_id=1, source_target_pairs={{0,6},{2,4},{4,2},{6,0},{8,14},{10,12},{12,10},{14,8},{16,22},{18,... | collective-permute-start | bytes 52232 | tf_op jit(solution)/shard_map/ppermute | solution.py:604
  161.8 8.4 %collective-permute-start.19 = (bf16[1,1024,128]{2,1,0:T(8,128)(2,1)S(1)}, bf16[1,1024,128]{2,1,0:T(8,128)(2,1)S(1)}, u32[]{:S(2)}, u32[]{:S(2)}) collective-permute-start(bf16[1,1024,128]{2,1,0:T(8,128)(2,1)S(1)} %get-tuple-element.48), channel_id=1, source_target_pairs={{0,2},{2,0},{4,6},{6,4},{8,10},{10,8},{12,14},{14,12},{16,18},{18,... | collective-permute-start | bytes 786440 | tf_op jit(solution)/shard_map/ppermute | solution.py:604
  163.4 11.0 %collective-permute-start.20 = (bf16[1,1024,128]{2,1,0:T(8,128)(2,1)S(1)}, bf16[1,1024,128]{2,1,0:T(8,128)(2,1)S(1)}, u32[]{:S(2)}, u32[]{:S(2)}) collective-permute-start(bf16[1,1024,128]{2,1,0:T(8,128)(2,1)S(1)} %get-tuple-element.47), channel_id=1, source_target_pairs={{0,4},{2,6},{4,0},{6,2},{8,12},{10,14},{12,8},{14,10},{16,20},{18,... | collective-permute-start | bytes 786440 | tf_op jit(solution)/shard_map/ppermute | solution.py:604
  164.2 10.3 %collective-permute-start.21 = (bf16[1,1024,128]{2,1,0:T(8,128)(2,1)S(1)}, bf16[1,1024,128]{2,1,0:T(8,128)(2,1)S(1)}, u32[]{:S(2)}, u32[]{:S(2)}) collective-permute-start(bf16[1,1024,128]{2,1,0:T(8,128)(2,1)S(1)} %get-tuple-element.46), channel_id=1, source_target_pairs={{0,6},{2,4},{4,2},{6,0},{8,14},{10,12},{12,10},{14,8},{16,22},{18,... | collective-permute-start | bytes 786440 | tf_op jit(solution)/shard_map/ppermute | solution.py:604
  (20 other events, 115.8 us)

commit v2 on v0

--- a/solution.py
+++ b/solution.py
@@ -1,9 +1,13 @@
+import functools
 import math
 
 import jax
 import jax.numpy as jnp
 from jax import lax
+from jax.experimental import pallas as pl
+from jax.experimental.pallas import tpu as pltpu
 from jax.sharding import PartitionSpec as P
+
 
 H = 16
 BLOCK = 64
@@ -123,7 +127,7 @@
     return (jnp.concatenate(query_grad, axis=0), key_grad, value_grad)
 
 
-def shards(
+def wide_shards(
     query_rows, key_rows, value_rows, norm_gain, level_table, level_index, window_length, out_grad
 ):
     heads_here, tok_here, head_dim = query_rows.shape
@@ -192,7 +196,7 @@
     )
     gain_part = jnp.sum(grad_full * mixed * inv_rms[None, :, None], axis=1)
     grad_low = mixed_grad.astype(jnp.bfloat16)
-    columns = [jnp.zeros((heads_here, tok_here), jnp.float32) for column_no in range(LEVELS)]
+    columns = [jnp.zeros((heads_here, tok_here), jnp.float32) for _ in range(LEVELS)]
     for level_no in range(len(area_list)):
         column_no = min(level_no, LEVELS - 1)
         columns[column_no] = columns[column_no] + jnp.sum(mixed_grad * area_list[level_no], axis=2)
@@ -266,6 +270,687 @@
     )
 
 
+f32 = jnp.float32
+bf16 = jnp.bfloat16
+index_rows = 16
+kernel_vmem = 20 * 2**20
+
+
+def dot_nn(left, right):
+    return lax.dot_general(left, right, (((1,), (0,)), ((), ())), preferred_element_type=f32)
+
+
+def dot_nt(left, right):
+    return lax.dot_general(left, right, (((1,), (1,)), ((), ())), preferred_element_type=f32)
+
+
+def dot_tn(left, right):
+    return lax.dot_general(left, right, (((0,), (0,)), ((), ())), preferred_element_type=f32)
+
+
+def added(parts):
+    return functools.reduce(lambda a, b: a + b, parts)
+
+
+def level_scale(level_no, head_dim):
+    return 1.0 / math.sqrt(BLOCK * 2 ** max(level_no - 1, 0) * head_dim)
+
+
+def lane_indices(index_block):
+    rows = index_block.astype(f32)
+    return jnp.concatenate([rows[:8], rows[8:]], axis=1)
+
+
+def lane_weights(indices, table_ref):
+    weights = jnp.zeros(indices.shape, f32)
+    wide = indices.shape[1] // table_ref.shape[-1]
+    for row_no in range(TABLE_ROWS):
+        row = jnp.concatenate([table_ref[0, row_no]] * wide, axis=1)
+        weights = jnp.where(indices == row_no, row, weights)
+    return weights
+
+
+def positions(rows, cols):
+    row_pos = lax.broadcasted_iota(jnp.int32, (rows, cols), 0)
+    col_pos = lax.broadcasted_iota(jnp.int32, (rows, cols), 1)
+    return row_pos, col_pos
+
+
+def diagonal_factor(query_pos, key_pos, picked, window_scale, near_levels, head_dim):
+    shift = BLOCK.bit_length() - 1
+    apart = (query_pos >> shift) ^ (key_pos >> shift)
+    factor = picked(0) * level_scale(0, head_dim) + window_scale
+    for level_no in range(1, near_levels + 1):
+        factor = jnp.where(
+            apart >= 2 ** (level_no - 1),
+            picked(level_no) * level_scale(level_no, head_dim) + window_scale,
+            factor,
+        )
+    return jnp.where(query_pos >= key_pos, factor, 0.0)
+
+
+def place(target, first_block, piece_refs, member):
+    rows = piece_refs[0].shape[0]
+    for bits, piece_ref in enumerate(piece_refs):
+        start = pl.multiple_of((first_block + (member ^ bits)) * rows, rows)
+        target[pl.ds(start, rows)] = piece_ref[...]
+
+
+def copy_all(pairs, semaphore):
+    copies = [pltpu.make_async_copy(a, b, semaphore.at[i]) for i, (a, b) in enumerate(pairs)]
+    for copy in copies:
+        copy.start()
+    for copy in copies:
+        copy.wait()
+
+
+def pack_kernel(member_ref, *refs, group, extra):
+    *refs, semaphore = refs
+    sources, pieces = refs[:-group], refs[-group:]
+    heads = sources[0].shape[0] // group
+    rows = sources[0].shape[1]
+    pairs = []
+    for bits, piece in enumerate(pieces):
+        for source_no, source in enumerate(sources[: len(sources) - extra]):
+            for head_no in range(heads):
+                first = (source_no * heads + head_no) * rows
+                block = source.at[(member_ref[0] ^ bits) * heads + head_no]
+                pairs.append((block, piece.at[pl.ds(first, rows)]))
+        if extra:
+            first = (len(sources) - 1) * heads * rows
+            pairs.append((sources[-1], piece.at[pl.ds(first, sources[-1].shape[0])]))
+    copy_all(pairs, semaphore)
+
+
+def arrange_kernel(member_ref, *refs, group):
+    pieces, targets = refs[:group], refs[group:]
+    for bits, piece in enumerate(pieces):
+        first = 0
+        for target in targets:
+            count = target.shape[1]
+            target[member_ref[0] ^ bits] = piece[first : first + count]
+            first += count
+
+
+def unpack_kernel(member_ref, *refs, group, head_stride, kind_stride):
+    *refs, semaphore = refs
+    pieces, outs = refs[:group], refs[group:]
+    heads = outs[0].shape[0] // group
+    rows = outs[0].shape[1]
+    pairs = []
+    for bits, piece in enumerate(pieces):
+        for head_no in range(heads):
+            for kind, out in enumerate(outs):
+                first = (head_no * head_stride + kind * kind_stride) * rows
+                target = out.at[(member_ref[0] ^ bits) * heads + head_no]
+                pairs.append((piece.at[pl.ds(first, rows)], target))
+    copy_all(pairs, semaphore)
+
+
+def window_reach(span, rows):
+    whole = span // rows
+    return whole, span - whole * rows
+
+
+def window_state(blocks, whole, steps):
+    state = blocks[0]
+    for step_no in range(1, steps):
+        state = state + blocks[step_no] * jnp.where(whole > step_no + 1, 1.0, 0.0)
+    return state
+
+
+def summary_kernel(member_ref, *refs, group, near_levels):
+    key_refs, value_refs = refs[:group], refs[group : 2 * group]
+    near_ref, block_ref, total_ref = refs[2 * group : 2 * group + 3]
+    key_all, value_all = refs[2 * group + 3 :]
+    rows, head_dim = key_refs[0].shape
+    member = member_ref[0]
+    place(key_all, 0, key_refs, member)
+    place(value_all, 0, value_refs, member)
+    parts = [
+        dot_tn(key_all[i * rows : (i + 1) * rows], value_all[i * rows : (i + 1) * rows])
+        for i in range(group)
+    ]
+    total_ref[0] = added(parts)
+    for block_no in range(group):
+        block_ref[0, block_no] = parts[block_no]
+        for bit_no in range(group.bit_length() - 1):
+            if block_no >> bit_no & 1:
+                first = (block_no >> bit_no << bit_no) - 2**bit_no
+                scale = level_scale(near_levels + 1 + bit_no, head_dim)
+                lower = added(parts[first : first + 2**bit_no]) * scale
+                near_ref[0, block_no, bit_no] = lower.astype(bf16)
+            else:
+                near_ref[0, block_no, bit_no] = jnp.zeros((head_dim, head_dim), bf16)
+
+
+def load_window(member, own_refs, prev_refs, target):
+    group = len(own_refs)
+    rows, head_dim = own_refs[0].shape
+    target[:rows] = jnp.zeros((rows, head_dim), bf16)
+    place(target, 1, prev_refs, member)
+    place(target, 1 + group, own_refs, member)
+
+
+def forward_kernel(member_ref, length_ref, scale_ref, last_scale_ref, *refs, group, near_levels):
+    key_refs, value_refs = refs[:group], refs[group : 2 * group]
+    key_prev, value_prev = refs[2 * group : 3 * group], refs[3 * group : 4 * group]
+    (
+        query_ref, grad_ref, index_ref, table_ref, gain_ref, near_ref, block_ref, far_ref,
+        mixed_ref, stat_ref, state_ref, far_out_ref, key_all, value_all,
+    ) = refs[4 * group :]
+    head_no = pl.program_id(0)
+    _, rows, head_dim = query_ref.shape
+    member = member_ref[0]
+    load_window(member, key_refs, key_prev, key_all)
+    load_window(member, value_refs, value_prev, value_all)
+    whole, part = window_reach(length_ref[head_no], rows)
+    window_scale = scale_ref[head_no]
+    blocks = [
+        dot_tn(key_all[i * rows : (i + 1) * rows], value_all[i * rows : (i + 1) * rows])
+        for i in range(1, group + 1)
+    ]
+    far = (far_ref[0] + added(blocks) * last_scale_ref[0]).astype(bf16)
+    far_out_ref[0] = far
+    blocks = blocks[1:] + [block_ref[0, i] for i in range(group - 1)]
+    stat_rows = []
+    row_pos, col_pos = positions(rows, rows)
+    edge_row, edge_col = positions(rows, 2 * rows)
+    edge_mask = edge_row - edge_col < part - rows
+    ones = jnp.ones((8, head_dim), bf16)
+    for block_no in range(group):
+        query = query_ref[block_no]
+        start = pl.multiple_of((block_no + group - whole) * rows, rows)
+        scores = dot_nt(query, key_all[pl.ds(start, 2 * rows)])
+        edge = jnp.where(edge_mask, scores, 0.0).astype(bf16)
+        total = dot_nn(edge, value_all[pl.ds(start, 2 * rows)])
+        recent = blocks[block_no : block_no + group - 1][::-1]
+        state = window_state(recent, whole, group - 1) * window_scale
+        state = state.astype(bf16)
+        state_ref[0, block_no] = state
+        weights = jnp.transpose(lane_weights(lane_indices(index_ref[block_no]), table_ref))
+
+        def picked(level_no):
+            return weights[:, level_no : level_no + 1]
+
+        factor = diagonal_factor(row_pos, col_pos, picked, window_scale, near_levels, head_dim)
+        own = slice((1 + group + block_no) * rows, (2 + group + block_no) * rows)
+        prob = (dot_nt(query, key_all[own]) * factor).astype(bf16)
+        mixed = dot_nn(prob, value_all[own]) + window_scale * total + dot_nn(query, state)
+        for bit_no in range(group.bit_length() - 1):
+            if block_no >> bit_no & 1:
+                area = dot_nn(query, near_ref[0, block_no, bit_no])
+                mixed = mixed + picked(near_levels + 1 + bit_no) * area
+        mixed = mixed + picked(LEVELS - 1) * dot_nn(query, far)
+        mixed_ref[block_no] = mixed
+        scaled = grad_ref[block_no].astype(f32) * gain_ref[0]
+        stat_rows.append(dot_nt(ones, (mixed * mixed).astype(bf16))[:1])
+        stat_rows.append(dot_nt(ones, (scaled * mixed).astype(bf16))[:1])
+    stats = jnp.concatenate(stat_rows, axis=0)
+
+    @pl.when(head_no == 0)
+    def _():
+        stat_ref[...] = stats
+
+    @pl.when(head_no > 0)
+    def _():
+        stat_ref[...] = stat_ref[...] + stats
+
+
+def norm_kernel(member_ref, mixed_ref, grad_ref, gain_ref, *refs, group, width):
+    stat_refs, out_refs = refs[:group], refs[group : 2 * group]
+    low_ref, gain_part_ref, out_all = refs[2 * group :]
+    gain = gain_ref[0]
+    stats = jnp.transpose(added([stat_ref[...] for stat_ref in stat_refs]))
+    parts = []
+    for block_no in range(group):
+        inv_rms = lax.rsqrt(stats[:, 2 * block_no : 2 * block_no + 1] / width + epsilon)
+        pull = inv_rms * inv_rms * inv_rms * stats[:, 2 * block_no + 1 : 2 * block_no + 2] / width
+        mixed = mixed_ref[block_no]
+        grad = grad_ref[block_no].astype(f32)
+        normed = mixed * inv_rms
+        out_all[block_no] = (normed * gain).astype(bf16)
+        low_ref[block_no] = (grad * gain * inv_rms - mixed * pull).astype(bf16)
+        parts.append(jnp.sum(grad * normed, axis=0, keepdims=True))
+    gain_part_ref[0] = added(parts)
+    for bits, out_ref in enumerate(out_refs):
+        out_ref[...] = out_all[member_ref[0] ^ bits]
+
+
+def far_grad_kernel(query_ref, low_ref, index_ref, table_ref, far_grad_ref):
+    parts = []
+    for block_no in range(query_ref.shape[0]):
+        weights = jnp.transpose(lane_weights(lane_indices(index_ref[block_no]), table_ref))
+        low = weights[:, LEVELS - 1 : LEVELS] * low_ref[block_no].astype(f32)
+        parts.append(dot_tn(query_ref[block_no], low.astype(bf16)))
+    far_grad_ref[0] = added(parts).astype(bf16)
+
+
+def query_kernel(member_ref, length_ref, scale_ref, *refs, group, near_levels):
+    key_refs, value_refs = refs[:group], refs[group : 2 * group]
+    key_prev, value_prev = refs[2 * group : 3 * group], refs[3 * group : 4 * group]
+    (
+        query_ref, low_ref, index_ref, table_ref, near_ref, state_ref, far_ref, gain_part_ref,
+    ) = refs[4 * group : 4 * group + 8]
+    out_refs = refs[5 * group + 8 : 6 * group + 8]
+    near_grad_ref, sums_ref, key_all, value_all, out_all = refs[6 * group + 8 :]
+    head_no = pl.program_id(0)
+    _, rows, head_dim = query_ref.shape
+    member = member_ref[0]
+    load_window(member, key_refs, key_prev, key_all)
+    load_window(member, value_refs, value_prev, value_all)
+    whole, part = window_reach(length_ref[head_no], rows)
+    window_scale = scale_ref[head_no]
+    row_pos, col_pos = positions(rows, rows)
+    edge_row, edge_col = positions(rows, 2 * rows)
+    edge_mask = edge_row - edge_col < part - rows
+    ones = jnp.ones((8, head_dim), bf16)
+    leaf_row = lax.broadcasted_iota(jnp.int32, (8, rows), 0)
+    leaf_col = lax.broadcasted_iota(jnp.int32, (8, rows), 1) >> (BLOCK.bit_length() - 1)
+    leaf_pick = jnp.where(leaf_row == leaf_col, 1.0, 0.0).astype(bf16)
+    own_leaf = leaf_col[:1]
+    lanes = table_ref.shape[-1]
+    table_parts = [jnp.zeros((8, lanes), f32) for _ in range(TABLE_ROWS)]
+    for block_no in range(group):
+        query = query_ref[block_no]
+        low = low_ref[block_no]
+        start = pl.multiple_of((block_no + group - whole) * rows, rows)
+        scores = dot_nt(low, value_all[pl.ds(start, 2 * rows)])
+        edge = jnp.where(edge_mask, scores, 0.0).astype(bf16)
+        total = dot_nn(edge, key_all[pl.ds(start, 2 * rows)])
+        indices = lane_indices(index_ref[block_no])
+        weights = jnp.transpose(lane_weights(indices, table_ref))
+
+        def picked(level_no):
+            return weights[:, level_no : level_no + 1]
+
+        factor = diagonal_factor(row_pos, col_pos, picked, window_scale, near_levels, head_dim)
+        own = slice((1 + group + block_no) * rows, (2 + group + block_no) * rows)
+        prob_grad = dot_nt(low, value_all[own])
+        result = dot_nn((prob_grad * factor).astype(bf16), key_all[own])
+        result = result + window_scale * total + dot_nt(low, state_ref[0, block_no])
+        scores = dot_nt(query, key_all[own])
+        pairs = jnp.where(row_pos >= col_pos, scores * prob_grad, 0.0).astype(bf16)
+        leaf_sums = dot_nt(leaf_pick, pairs)
+        level_rows = [jnp.zeros((1, rows), f32) for _ in range(8)]
+        for leaf_no in range(rows // BLOCK):
+            leaf_sum = leaf_sums[leaf_no : leaf_no + 1]
+            apart = own_leaf ^ leaf_no
+            level_rows[0] = level_rows[0] + jnp.where(apart == 0, leaf_sum, 0.0)
+            for level_no in range(1, near_levels + 1):
+                here = (apart >> (level_no - 1)) == 1
+                level_rows[level_no] = level_rows[level_no] + jnp.where(here, leaf_sum, 0.0)
+        for level_no in range(near_levels + 1):
+            level_rows[level_no] = level_rows[level_no] * level_scale(level_no, head_dim)
+        query_wide = query.astype(f32)
+        low_wide = low.astype(f32)
+        for level_no in range(near_levels + 1, LEVELS):
+            bit_no = level_no - near_levels - 1
+            last = level_no == LEVELS - 1
+            if not last and not block_no >> bit_no & 1:
+                continue
+            back = dot_nt(low, far_ref[0] if last else near_ref[0, block_no, bit_no])
+            result = result + picked(level_no) * back
+            level_rows[level_no] = dot_nt(ones, (query_wide * back).astype(bf16))[:1]
+            if not last:
+                upstream = (picked(level_no) * low_wide).astype(bf16)
+                near_grad_ref[0, block_no, bit_no] = dot_tn(query, upstream)
+        out_all[block_no] = result.astype(bf16)
+        weight_grad = jnp.concatenate(level_rows, axis=0)
+        for row_no in range(TABLE_ROWS):
+            chosen = jnp.where(indices == row_no, weight_grad, 0.0)
+            folded = added([chosen[:, i : i + lanes] for i in range(0, rows, lanes)])
+            table_parts[row_no] = table_parts[row_no] + folded
+    table_part = jnp.concatenate(table_parts, axis=0)
+    table_high = table_part.astype(bf16)
+    table_low = (table_part - table_high.astype(f32)).astype(bf16)
+    lane_sums = dot_nt(ones, table_high) + dot_nt(ones, table_low)
+    for bits, out_ref in enumerate(out_refs):
+        out_ref[...] = out_all[member ^ bits]
+    heads = pl.num_programs(0)
+    row_no = lax.broadcasted_iota(jnp.int32, sums_ref.shape, 0)
+    first = (member * heads + head_no) * 2
+
+    @pl.when(head_no == 0)
+    def _():
+        sums_ref[...] = jnp.zeros(sums_ref.shape, f32)
+
+    sums = jnp.where(row_no == first, lane_sums[:1], sums_ref[...])
+    sums_ref[...] = jnp.where(row_no == first + 1, gain_part_ref[0], sums)
+
+
+def key_kernel(member_ref, length_ref, scale_ref, *refs, group, near_levels):
+    key_refs, value_refs = refs[:group], refs[group : 2 * group]
+    (
+        query_ref, low_ref, query_next_ref, low_next_ref, index_ref, table_ref, near_grad_ref,
+        far_grad_ref,
+    ) = refs[2 * group : 2 * group + 8]
+    out_refs = refs[2 * group + 8 : 3 * group + 8]
+    key_all, value_all, query_all, low_all, out_all = refs[3 * group + 8 :]
+    head_no = pl.program_id(0)
+    _, rows, head_dim = query_ref.shape
+    member = member_ref[0]
+    place(key_all, 0, key_refs, member)
+    place(value_all, 0, value_refs, member)
+    for target, first_ref, second_ref in (
+        (query_all, query_ref, query_next_ref),
+        (low_all, low_ref, low_next_ref),
+    ):
+        for i in range(group):
+            target[i * rows : (i + 1) * rows] = first_ref[i]
+            target[(group + i) * rows : (group + i + 1) * rows] = second_ref[i]
+        target[2 * group * rows :] = jnp.zeros((rows, head_dim), bf16)
+    whole, part = window_reach(length_ref[head_no], rows)
+    window_scale = scale_ref[head_no]
+    blocks = [
+        dot_tn(query_all[i * rows : (i + 1) * rows], low_all[i * rows : (i + 1) * rows])
+        for i in range(1, 2 * group - 1)
+    ]
+    row_pos, col_pos = positions(rows, rows)
+    edge_row, edge_col = positions(rows, 2 * rows)
+    edge_mask = edge_col - edge_row < part
+    for block_no in range(group):
+        own = slice(block_no * rows, (block_no + 1) * rows)
+        key = key_all[own]
+        value = value_all[own]
+        start = pl.multiple_of((block_no + whole) * rows, rows)
+        query_part = query_all[pl.ds(start, 2 * rows)]
+        low_part = low_all[pl.ds(start, 2 * rows)]
+        prob = jnp.where(edge_mask, dot_nt(key, query_part), 0.0).astype(bf16)
+        prob_grad = jnp.where(edge_mask, dot_nt(value, low_part), 0.0).astype(bf16)
+        value_total = dot_nn(prob, low_part)
+        key_total = dot_nn(prob_grad, query_part)
+        weights = lane_weights(lane_indices(index_ref[block_no]), table_ref)
+
+        def picked(level_no):
+            return weights[level_no : level_no + 1]
+
+        factor = diagonal_factor(col_pos, row_pos, picked, window_scale, near_levels, head_dim)
+        prob = (dot_nt(key, query_all[own]) * factor).astype(bf16)
+        prob_grad = (dot_nt(value, low_all[own]) * factor).astype(bf16)
+        state = window_state(blocks[block_no : block_no + group - 1], whole, group - 1)
+        state = state * window_scale + far_grad_ref[0]
+        for bit_no in range(group.bit_length() - 1):
+            if not block_no >> bit_no & 1:
+                first = (block_no >> bit_no | 1) << bit_no
+                upper = [near_grad_ref[0, first + i, bit_no] for i in range(2**bit_no)]
+                state = state + added(upper) * level_scale(near_levels + 1 + bit_no, head_dim)
+        state = state.astype(bf16)
+        value_grad = dot_nn(prob, low_all[own]) + window_scale * value_total + dot_nn(key, state)
+        key_grad = dot_nn(prob_grad, query_all[own]) + window_scale * key_total
+        key_grad = key_grad + dot_nt(value, state)
+        out_all[block_no, :rows] = key_grad.astype(bf16)
+        out_all[block_no, rows:] = value_grad.astype(bf16)
+    for bits, out_ref in enumerate(out_refs):
+        out_ref[...] = out_all[member ^ bits]
+
+
+def grouped_shards(
+    query_rows, key_rows, value_rows, norm_gain, level_table, level_index, window_length, out_grad
+):
+    heads_here, rows, head_dim = query_rows.shape
+    group = WINDOW // rows
+    heads = heads_here // group
+    group_bits = group.bit_length() - 1
+    near_levels = (rows // BLOCK).bit_length() - 1
+    seq_count = lax.axis_size("seq")
+    chunk_bits = (seq_count // group).bit_length() - 1
+    seq_index = lax.axis_index("seq")
+    member = seq_index & (group - 1)
+    member_arg = member.astype(jnp.int32).reshape(1)
+    head_count = lax.axis_size("head")
+    width = float(heads_here * head_count * head_dim)
+
+    def swapped(shard, bits):
+        return lax.ppermute(shard, "seq", [(i, i ^ bits) for i in range(seq_count)])
+
+    def moved(shard, distance):
+        return shifted(shard, "seq", distance)
+
+    def exchanged(pieces):
+        return list(pieces[:1]) + [swapped(pieces[bits], bits) for bits in range(1, group)]
+
+    smem = pl.BlockSpec(memory_space=pltpu.SMEM)
+    vmem = pl.BlockSpec(memory_space=pltpu.VMEM)
+    hbm = pl.BlockSpec(memory_space=pltpu.HBM)
+
+    def whole_call(kernel, in_specs, outs, copies, *args):
+        return pl.pallas_call(
+            kernel,
+            in_specs=in_specs,
+            out_specs=[spec for spec, _, _ in outs],
+            out_shape=[jax.ShapeDtypeStruct(shape, dtype) for _, shape, dtype in outs],
+            scratch_shapes=[pltpu.SemaphoreType.DMA((copies,))] if copies else [],
+            compiler_params=pltpu.CompilerParams(vmem_limit_bytes=kernel_vmem),
+        )(*args)
+
+    piece_shape = (2 * heads * rows, head_dim)
+    rest_shape = (2 * heads * rows + index_rows, head_dim)
+    chunk_shape = (group, heads * rows, head_dim)
+    index_shape = (group, index_rows, head_dim)
+    pair = whole_call(
+        functools.partial(pack_kernel, group=group, extra=0),
+        [smem, hbm, hbm], [(vmem, piece_shape, bf16)] * group, 2 * heads * group,
+        member_arg, key_rows, value_rows,
+    )
+    index_pad = jnp.pad(level_index.astype(bf16), ((0, 0), (0, 8 - LEVELS)))
+    index_pack = index_pad.reshape(rows // 128, 128, 8).transpose(0, 2, 1).reshape(index_rows, 128)
+    rest = whole_call(
+        functools.partial(pack_kernel, group=group, extra=1),
+        [smem, hbm, hbm, hbm], [(vmem, rest_shape, bf16)] * group, (2 * heads + 1) * group,
+        member_arg, query_rows, out_grad, index_pack,
+    )
+    pair = exchanged(pair)
+    pair_prev = [moved(piece, group) for piece in pair]
+    rest = exchanged(rest)
+    query, grad, index = whole_call(
+        functools.partial(arrange_kernel, group=group), [smem] + [vmem] * group,
+        [(vmem, chunk_shape, bf16), (vmem, chunk_shape, bf16), (vmem, index_shape, bf16)], 0,
+        member_arg, *rest,
+    )
+    query_next = moved(query, -group)
+
+    first_head = member * heads
+    table = lax.dynamic_slice_in_dim(level_table, first_head, heads, 1)
+    table = jnp.pad(table.transpose(1, 0, 2), ((0, 0), (0, 0), (0, 8 - LEVELS)))
+    table = jnp.broadcast_to(table[..., None], (heads, TABLE_ROWS, 8, 128))
+    gain = lax.dynamic_slice_in_dim(norm_gain, first_head, heads, 0)[:, None, :]
+    length = lax.dynamic_slice_in_dim(window_length, first_head, heads, 0)
+    scale = lax.rsqrt((head_dim * length).astype(f32))
+
+    chunk_no = seq_index // group
+
+    def far_scale(other):
+        apart = chunk_no ^ other
+        result = jnp.full((), level_scale(near_levels + group_bits + 1, head_dim), f32)
+        for bit_no in range(1, chunk_bits):
+            scale_here = level_scale(near_levels + group_bits + 1 + bit_no, head_dim)
+            result = jnp.where(apart >= 1 << bit_no, scale_here, result)
+        return result
+
+    state_shape = (head_dim, head_dim)
+    states_shape = (heads,) + state_shape
+    near_shape = (heads, group, group_bits) + state_shape
+    block_states = (heads, group) + state_shape
+
+    def whole(first):
+        return pl.BlockSpec((group, rows, head_dim), lambda h: (0, first * heads + h, 0))
+
+    def each(first):
+        return [pl.BlockSpec((rows, head_dim), lambda h: (first * heads + h, 0))] * group
+
+    def per_head(shape):
+        return pl.BlockSpec((1,) + shape[1:], lambda h: (h,) + (0,) * (len(shape) - 1))
+
+    def fixed(shape):
+        return pl.BlockSpec(shape, lambda h: (0,) * len(shape))
+
+    index_spec = fixed(index_shape)
+    table_spec = per_head(table.shape)
+    stat_shape = (2 * group, rows)
+
+    def run(kernel, cost, in_specs, outs, scratch, aliases, *args):
+        return pl.pallas_call(
+            kernel,
+            grid=(heads,),
+            in_specs=in_specs,
+            out_specs=[spec for spec, _, _ in outs],
+            out_shape=[jax.ShapeDtypeStruct(shape, dtype) for _, shape, dtype in outs],
+            scratch_shapes=[pltpu.VMEM(shape, bf16) for shape in scratch],
+            input_output_aliases=aliases,
+            cost_estimate=pl.CostEstimate(
+                flops=int(cost * 1e9), transcendentals=0, bytes_accessed=4 * 2**20
+            ),
+            compiler_params=pltpu.CompilerParams(vmem_limit_bytes=kernel_vmem),
+        )(*args)
+
+    sizes = dict(group=group, near_levels=near_levels)
+    chunk_rows = (group * rows, head_dim)
+    window_rows = ((2 * group + 1) * rows, head_dim)
+    results = (group, rows, head_dim)
+    near, block_sums, total = run(
+        functools.partial(summary_kernel, **sizes), 0.5,
+        [smem] + each(0) + each(1),
+        [
+            (per_head(near_shape), near_shape, bf16),
+            (per_head(block_states), block_states, f32),
+            (per_head(states_shape), states_shape, f32),
+        ],
+        [chunk_rows] * 2, {}, member_arg, *pair, *pair,
+    )
+    total = total.astype(bf16)
+    far = jnp.zeros(states_shape, f32)
+    for step_no in range(2, 1 << chunk_bits):
+        other = moved(total, step_no * group).astype(f32)
+        far = far + other * far_scale(chunk_no - step_no)
+    last_scale = far_scale(chunk_no - 1).reshape(1)
+    far_spec = per_head(states_shape)
+
+    mixed, stats, states, far = run(
+        functools.partial(forward_kernel, **sizes), 3,
+        [smem] * 4 + each(0) + each(1) + each(0) + each(1)
+        + [
+            whole(0), whole(0), index_spec, table_spec, per_head(gain.shape),
+            per_head(near_shape), per_head(block_states), far_spec,
+        ],
+        [
+            (whole(0), chunk_shape, f32),
+            (fixed(stat_shape), stat_shape, f32),
+            (per_head(block_states), block_states, bf16),
+            (far_spec, states_shape, bf16),
+        ],
+        [window_rows] * 2, {},
+        member_arg, length, scale, last_scale, *pair, *pair, *pair_prev, *pair_prev,
+        query, grad, index, table, gain, near, block_sums, far,
+    )
+
+    part = stats
+    for step_no in range(1, head_count):
+        turn = [(i, (i + step_no) % head_count) for i in range(head_count)]
+        stats = stats + lax.ppermute(part, "head", turn)
+    stat_parts = [stats] + [swapped(stats, bits) for bits in range(1, group)]
+
+    out_pieces = [(each(0)[0], piece_shape, bf16)] * group
+    *first_out, low, gain_part = run(
+        functools.partial(norm_kernel, group=group, width=width), 0.6,
+        [smem, whole(0), whole(0), per_head(gain.shape)] + [fixed(stat_shape)] * group,
+        out_pieces + [(whole(0), chunk_shape, bf16), (per_head(gain.shape), gain.shape, f32)],
+        [results], {}, member_arg, mixed, grad, gain, *stat_parts,
+    )
+    low_next = moved(low, -group)
+    (far_part,) = run(
+        far_grad_kernel, 0.3,
+        [whole(0), whole(0), index_spec, table_spec], [(far_spec, states_shape, bf16)],
+        [], {}, query, low, index, table,
+    )
+    far_grad = jnp.zeros(states_shape, f32)
+    for step_no in range(1, 1 << chunk_bits):
+        other = moved(far_part, -step_no * group).astype(f32)
+        far_grad = far_grad + other * far_scale(chunk_no + step_no)
+
+    args = (
+        member_arg, length, scale, *pair, *pair, *pair_prev, *pair_prev,
+        query, low, index, table, near, states, far, gain_part, *first_out,
+    )
+    sums_shape = (2 * heads_here, head_dim)
+    *first_out, near_grad, sums = run(
+        functools.partial(query_kernel, **sizes), 3,
+        [smem] * 3 + each(0) + each(1) + each(0) + each(1)
+        + [
+            whole(0), whole(0), index_spec, table_spec, per_head(near_shape),
+            per_head(block_states), far_spec, per_head(gain.shape),
+        ]
+        + [pl.BlockSpec(memory_space=pl.ANY)] * group,
+        [(each(1)[0], piece_shape, bf16)] * group
+        + [(per_head(near_shape), near_shape, f32), (fixed(sums_shape), sums_shape, f32)],
+        [window_rows] * 2 + [results],
+        {len(args) - group + bits: bits for bits in range(group)}, *args,
+    )
+    first_out = exchanged(first_out)
+
+    pair_out = pl.BlockSpec((2 * rows, head_dim), lambda h: (h, 0))
+    last_out = run(
+        functools.partial(key_kernel, **sizes), 4,
+        [smem] * 3 + each(0) + each(1)
+        + [
+            whole(0), whole(0), whole(0), whole(0), index_spec, table_spec,
+            per_head(near_shape), far_spec,
+        ],
+        [(pair_out, piece_shape, bf16)] * group,
+        [chunk_rows] * 2 + [window_rows] * 2 + [(group, 2 * rows, head_dim)], {},
+        member_arg, length, scale, *pair, *pair,
+        query, low, query_next, low_next, index, table, near_grad, far_grad,
+    )
+    last_out = exchanged(last_out)
+
+    for step_no in range(chunk_bits + group_bits):
+        bit_no = (step_no + group_bits) % (chunk_bits + group_bits)
+        sums = sums + swapped(sums, 1 << bit_no)
+    sums = sums.reshape(heads_here, 2, head_dim)
+    table_grad = sums[:, 0].reshape(heads_here, TABLE_ROWS, 8)[:, :, :LEVELS]
+
+    def unpacked(pieces, head_stride, kind_stride):
+        return whole_call(
+            functools.partial(
+                unpack_kernel, group=group, head_stride=head_stride, kind_stride=kind_stride
+            ),
+            [smem] + [vmem] * group, [(hbm, query_rows.shape, bf16)] * 2,
+            2 * heads * group, member_arg, *pieces,
+        )
+
+    layer_out, query_grad = unpacked(first_out, 1, heads)
+    key_grad, value_grad = unpacked(last_out, 2, 1)
+    return (
+        layer_out,
+        query_grad,
+        key_grad,
+        value_grad,
+        table_grad.transpose(1, 0, 2),
+        sums[:, 1],
+    )
+
+
+def fits_groups(heads_here, rows, seq_count):
+    group = WINDOW // rows
+    levels_fit = (WINDOW // BLOCK).bit_length() + 1 == LEVELS
+    return (
+        group * rows == WINDOW
+        and rows == 2 * 128
+        and group == 1 << (group.bit_length() - 1)
+        and heads_here % group == 0
+        and seq_count % group == 0
+        and seq_count == 1 << (seq_count.bit_length() - 1)
+        and levels_fit
+    )
+
+
+def shards(query_rows, *others):
+    heads_here, rows, _ = query_rows.shape
+    if fits_groups(heads_here, rows, lax.axis_size("seq")):
+        return grouped_shards(query_rows, *others)
+    return wide_shards(query_rows, *others)
+
+
 def solution(mesh):
     placed = (
         P("head", "seq", None),

time: 524 us -> 133 us (0.25)
  matrix products: 128 us -> 0 us
  waiting for transfers between devices: 139 us -> 35.3 us
  blocking collectives: 77 us -> 0 us
  local copies, waits for them, and re-layouts: 74.6 us -> 7.21 us
  other arithmetic: 35.6 us -> 0.88 us
  Pallas kernels: 0 us -> 32.6 us
  loops' own time: 11.3 us -> 0 us
    dot_general x80 -> x0, matrix products: 128 us -> none  [the longest x78 128 us: contract(): jnp.einsum(pattern, left_side, right_side, preferred_element_type=jnp.flo...]
    ppermute x8 -> x20, waiting for transfers between devices: 139 us -> 24.5 us  [the longest x19 23.4 us: swapped(): return lax.ppermute(shard, 'seq', [(i, i ^ bits) for i in range(seq_count)])]
    psum x3 -> x0, blocking collectives: 77 us -> none  [the longest x1 71.9 us: shards(): table_grad, gain_grad = lax.psum((table_part, gain_part), 'seq')]
    pallas_call x0 -> x11, Pallas kernels: none -> 32.6 us  [the longest x6 26.4 us: run(): pl.pallas_call(kernel, grid=(heads,), in_specs=in_specs, out_specs=[spec...]
    reshape x10 -> x1, local copies, waits for them, and re-layouts: 24.3 us -> 0.01 us  [grouped_shards(): index_pad.reshape(rows // 128, 128, 8).transpose(0, 2, 1)]
    unnamed x121 -> x30, local copies, waits for them, and re-layouts: 19.4 us -> 5.73 us
    another operation x9 -> x1, local copies, waits for them, and re-layouts: 12.5 us -> 0.08 us  [grouped_shards(): table_grad = sums[:, 0].reshape(heads_here, TABLE_ROWS, 8)[:, :, :LEVELS]]
    another operation x2 -> x0, loops' own time: 11.3 us -> none  [the longest x1 5.67 us: shards(): lax.map(lambda head_items: window_back_head(head_items[0], head_items[1],...]
  transfers between devices with their start and end apart: 16 -> 31, of which waited for: 5 -> 14; matrix products, arithmetic and copies ran while one was open for 22% -> 2% of each run, Pallas kernels for 0% -> 17%
where the time goes in v2:
time: 133 us
  starting transfers between devices  55.6 us (42%)
  waiting for transfers between devices  35.3 us (27%)
  Pallas kernels  32.6 us (25%)
  local copies, waits for them, and re-layouts  7.21 us (5%)
    ppermute x19, starting transfers between devices, swapped(): return lax.ppermute(shard, 'seq', [(i, i ^ bits) for i in range(seq_count)])  29.2 us
    pallas_call x6, Pallas kernels, run(): pl.pallas_call(kernel, grid=(heads,), in_specs=in_specs, out_specs=[spec...  26.4 us
    ppermute x11, starting transfers between devices, shifted(): return lax.ppermute(block, axis, route)  26.4 us
    ppermute x19, waiting for transfers between devices, swapped(): return lax.ppermute(shard, 'seq', [(i, i ^ bits) for i in range(seq_count)])  23.4 us
    ppermute x11, waiting for transfers between devices, shifted(): return lax.ppermute(block, axis, route)  10.8 us
    pallas_call x5, Pallas kernels, whole_call(): pl.pallas_call(kernel, in_specs=in_specs, out_specs=[spec for spec, _, _...  6.14 us
    unnamed x30, local copies, waits for them, and re-layouts  5.73 us
  transfers between devices with their start and end apart: 31, of which 14 were waited for; matrix products, arithmetic and copies ran while one was open for 2% of the time, Pallas kernels for 17%

profile of v2, /device:TPU:0, one launch (start us, length us, event | category | flops | bytes accessed | tf_op | source)
XLA Modules:
  0.0 132.8 jit_solution(9127521096199429040)
XLA Ops:
  4.3 3.0 %collective-permute-start = (bf16[1024,128]{1,0:T(8,128)(2,1)S(1)}, bf16[1024,128]{1,0:T(8,128)(2,1)S(1)}, u32[]{:S(2)}, u32[]{:S(2)}) collective-permute-start(bf16[1024,128]{1,0:T(8,128)(2,1)S(1)} %get-tuple-element.45), channel_id=1, source_target_pairs={{0,2},{2,0},{4,6},{6,4},{8,10},{10,8},{12,14},{14,12},{16,18},{18,... | collective-permute-start | bytes 786440 | tf_op jit(solution)/shard_map/ppermute | solution.py:705
  9.5 2.4 %shard_map.128 = (bf16[1040,128]{1,0:T(8,128)(2,1)S(1)}, bf16[1040,128]{1,0:T(8,128)(2,1)}, bf16[1040,128]{1,0:T(8,128)(2,1)}, bf16[1040,128]{1,0:T(8,128)(2,1)S(1)}) custom-call(s32[1]{0:T(128)} %bitcast.member_ref, bf16[8,256,128]{2,1,0:T(8,128)(2,1)S(1)} %copy-done.3, bf16[8,256,128]{2,1,0:T(8,128)(2,1)S(1)} %copy-done.4, ...), custom_call_target="tpu_custom_call" | custom-call | tf_op jit(solution)/shard_map/pallas_call | solution.py:718
  11.9 2.0 %collective-permute-start.7 = (bf16[1040,128]{1,0:T(8,128)(2,1)}, bf16[1040,128]{1,0:T(8,128)(2,1)S(1)}, u32[]{:S(2)}, u32[]{:S(2)}) collective-permute-start(bf16[1040,128]{1,0:T(8,128)(2,1)} %get-tuple-element.49), channel_id=1, source_target_pairs={{0,2},{2,0},{4,6},{6,4},{8,10},{10,8},{12,14},{14,12},{16,18},{18,... | collective-permute-start | bytes 798728 | tf_op jit(solution)/shard_map/ppermute | solution.py:705
  15.5 1.9 %collective-permute-start.9 = (bf16[1040,128]{1,0:T(8,128)(2,1)S(1)}, bf16[1040,128]{1,0:T(8,128)(2,1)S(1)}, u32[]{:S(2)}, u32[]{:S(2)}) collective-permute-start(bf16[1040,128]{1,0:T(8,128)(2,1)S(1)} %get-tuple-element.51), channel_id=1, source_target_pairs={{0,6},{2,4},{4,2},{6,0},{8,14},{10,12},{12,10},{14,8},{16,22},{18,... | collective-permute-start | bytes 798728 | tf_op jit(solution)/shard_map/ppermute | solution.py:705
  17.4 3.7 %collective-permute-done.1.refs_2_.refs_6_ = bf16[1024,128]{1,0:T(8,128)(2,1)S(1)} collective-permute-done((bf16[1024,128]{1,0:T(8,128)(2,1)S(1)}, bf16[1024,128]{1,0:T(8,128)(2,1)S(1)}, u32[]{:S(2)}, u32[]{:S(2)}) %collective-permute-start.1) | collective-permute-done | bytes 262176 | tf_op jit(solution)/shard_map/ppermute | solution.py:705
  21.1 3.9 %collective-permute-start.3 = (bf16[1024,128]{1,0:T(8,128)(2,1)S(1)}, bf16[1024,128]{1,0:T(8,128)(2,1)}, u32[]{:S(2)}, u32[]{:S(2)}) collective-permute-start(bf16[1024,128]{1,0:T(8,128)(2,1)S(1)} %get-tuple-element.44.refs_0_.refs_4_), channel_id=1, source_target_pairs={{0,8},{2,10},{4,12},{6,14},{8,16},{10,18},{12,20},{14,22},{16,24},... | collective-permute-start | bytes 786440 | tf_op jit(solution)/shard_map/ppermute | solution.py:26
  27.3 3.8 %collective-permute-start.10 = (bf16[2,128,128]{2,1,0:T(8,128)(2,1)S(1)}, bf16[2,128,128]{2,1,0:T(8,128)(2,1)S(1)}, u32[]{:S(2)}, u32[]{:S(2)}) collective-permute-start(bf16[2,128,128]{2,1,0:T(8,128)(2,1)S(1)} %convert_element_type.30), channel_id=1, source_target_pairs={{0,16},{2,18},{4,20},{6,22},{8,24},{10,26},{12,28},{14,30},{1,17},... | collective-permute-start | bytes 196616 | tf_op jit(solution)/shard_map/ppermute | solution.py:26
  32.5 3.8 %collective-permute-start.4 = (bf16[1024,128]{1,0:T(8,128)(2,1)S(1)}, bf16[1024,128]{1,0:T(8,128)(2,1)}, u32[]{:S(2)}, u32[]{:S(2)}) collective-permute-start(bf16[1024,128]{1,0:T(8,128)(2,1)S(1)} %collective-permute-done.refs_1_.refs_5_), channel_id=1, source_target_pairs={{0,8},{2,10},{4,12},{6,14},{8,16},{10,18},{12,20},{14,22},{16,24},... | collective-permute-start | bytes 786440 | tf_op jit(solution)/shard_map/ppermute | solution.py:26
  36.3 2.8 %collective-permute-start.5 = (bf16[1024,128]{1,0:T(8,128)(2,1)S(1)}, bf16[1024,128]{1,0:T(8,128)(2,1)S(1)}, u32[]{:S(2)}, u32[]{:S(2)}) collective-permute-start(bf16[1024,128]{1,0:T(8,128)(2,1)S(1)} %collective-permute-done.1.refs_2_.refs_6_), channel_id=1, source_target_pairs={{0,8},{2,10},{4,12},{6,14},{8,16},{10,18},{12,20},{14,22},{16,24},... | collective-permute-start | bytes 786440 | tf_op jit(solution)/shard_map/ppermute | solution.py:26
  39.1 4.2 %collective-permute-start.6 = (bf16[1024,128]{1,0:T(8,128)(2,1)S(1)}, bf16[1024,128]{1,0:T(8,128)(2,1)}, u32[]{:S(2)}, u32[]{:S(2)}) collective-permute-start(bf16[1024,128]{1,0:T(8,128)(2,1)S(1)} %collective-permute-done.2.refs_3_.refs_7_), channel_id=1, source_target_pairs={{0,8},{2,10},{4,12},{6,14},{8,16},{10,18},{12,20},{14,22},{16,24},... | collective-permute-start | bytes 786440 | tf_op jit(solution)/shard_map/ppermute | solution.py:26
  44.2 2.3 %collective-permute-done.5.refs_10_.refs_14_ = bf16[1024,128]{1,0:T(8,128)(2,1)S(1)} collective-permute-done((bf16[1024,128]{1,0:T(8,128)(2,1)S(1)}, bf16[1024,128]{1,0:T(8,128)(2,1)S(1)}, u32[]{:S(2)}, u32[]{:S(2)}) %collective-permute-start.5) | collective-permute-done | bytes 262176 | tf_op jit(solution)/shard_map/ppermute | solution.py:26
  46.5 2.8 %collective-permute-done.6.refs_11_.refs_15_ = bf16[1024,128]{1,0:T(8,128)(2,1)} collective-permute-done((bf16[1024,128]{1,0:T(8,128)(2,1)S(1)}, bf16[1024,128]{1,0:T(8,128)(2,1)}, u32[]{:S(2)}, u32[]{:S(2)}) %collective-permute-start.6) | collective-permute-done | bytes 262176 | tf_op jit(solution)/shard_map/ppermute | solution.py:26
  49.5 7.3 %shard_map.131 = (f32[4,512,128]{2,1,0:T(8,128)S(1)}, f32[8,256]{1,0:T(8,128)S(1)}, bf16[2,4,128,128]{3,2,1,0:T(8,128)(2,1)S(1)}, bf16[2,128,128]{2,1,0:T(8,128)(2,1)S(1)}) custom-call(s32[1]{0:T(128)} %bitcast.member_ref, s32[2]{0:T(128)S(1)} %get-tuple-element.89.length_ref, f32[2]{0:T(128)S(1)} %get-tuple-element.88.scale_ref, f32[1]{0:T(128)} %bitcast.4.last_scale_ref, ...), custom_call_target="tpu_custom_call" | custom-call | flops 3000000000 | bytes 4194304 | tf_op jit(solution)/shard_map/pallas_call | solution.py:793
  59.0 2.1 %collective-permute-start.14 = (f32[8,256]{1,0:T(8,128)S(1)}, f32[8,256]{1,0:T(8,128)S(1)}, u32[]{:S(2)}, u32[]{:S(2)}) collective-permute-start(f32[8,256]{1,0:T(8,128)S(1)} %add.48.refs_0_), channel_id=1, source_target_pairs={{0,4},{2,6},{4,0},{6,2},{8,12},{10,14},{12,8},{14,10},{16,20},{18,... | collective-permute-start | bytes 24584 | tf_op jit(solution)/shard_map/ppermute | solution.py:705
  62.9 2.8 %collective-permute-done.15.refs_3_ = f32[8,256]{1,0:T(8,128)S(1)} collective-permute-done((f32[8,256]{1,0:T(8,128)S(1)}, f32[8,256]{1,0:T(8,128)S(1)}, u32[]{:S(2)}, u32[]{:S(2)}) %collective-permute-start.15) | collective-permute-done | bytes 8224 | tf_op jit(solution)/shard_map/ppermute | solution.py:705
  68.8 8.5 %shard_map.133 = (bf16[1024,128]{1,0:T(8,128)(2,1)S(1)}, bf16[1024,128]{1,0:T(8,128)(2,1)}, bf16[1024,128]{1,0:T(8,128)(2,1)}, bf16[1024,128]{1,0:T(8,128)(2,1)}...) custom-call(s32[1]{0:T(128)} %bitcast.member_ref, ...), custom_call_target="tpu_custom_call", output_to_operand_aliasing={{0}: (27, {}), {1}: (28, {}), {2}: (29, {}), {3}: (30, {})} | custom-call | flops 3000000000 | bytes 4194304 | tf_op jit(solution)/shard_map/pallas_call | solution.py:793
  77.3 3.3 %collective-permute-start.27 = (f32[16,128]{1,0:T(8,128)S(1)}, f32[16,128]{1,0:T(8,128)S(1)}, u32[]{:S(2)}, u32[]{:S(2)}) collective-permute-start(f32[16,128]{1,0:T(8,128)S(1)} %get-tuple-element.81), channel_id=1, source_target_pairs={{0,8},{2,10},{4,12},{6,14},{8,0},{10,2},{12,4},{14,6},{16,24},{18,... | collective-permute-start | bytes 24584 | tf_op jit(solution)/shard_map/ppermute | solution.py:705
  80.6 8.2 %collective-permute-done.27 = f32[16,128]{1,0:T(8,128)S(1)} collective-permute-done((f32[16,128]{1,0:T(8,128)S(1)}, f32[16,128]{1,0:T(8,128)S(1)}, u32[]{:S(2)}, u32[]{:S(2)}) %collective-permute-start.27) | collective-permute-done | bytes 8224 | tf_op jit(solution)/shard_map/ppermute | solution.py:705
  88.9 2.8 %collective-permute-start.28 = (f32[16,128]{1,0:T(8,128)S(1)}, f32[16,128]{1,0:T(8,128)S(1)}, u32[]{:S(2)}, u32[]{:S(2)}) collective-permute-start(f32[16,128]{1,0:T(8,128)S(1)} %add.54), channel_id=1, source_target_pairs={{0,16},{2,18},{4,20},{6,22},{8,24},{10,26},{12,28},{14,30},{16,0},... | collective-permute-start | bytes 24584 | tf_op jit(solution)/shard_map/ppermute | solution.py:705
  94.7 2.4 %collective-permute-done.29 = f32[16,128]{1,0:T(8,128)S(1)} collective-permute-done((f32[16,128]{1,0:T(8,128)S(1)}, f32[16,128]{1,0:T(8,128)S(1)}, u32[]{:S(2)}, u32[]{:S(2)}) %collective-permute-start.29) | collective-permute-done | bytes 8224 | tf_op jit(solution)/shard_map/ppermute | solution.py:705
  104.1 2.0 %collective-permute-done.21 = bf16[2,128,128]{2,1,0:T(8,128)(2,1)S(1)} collective-permute-done((bf16[2,128,128]{2,1,0:T(8,128)(2,1)S(1)}, bf16[2,128,128]{2,1,0:T(8,128)(2,1)S(1)}, u32[]{:S(2)}, u32[]{:S(2)}) %collective-permute-start.21) | collective-permute-done | bytes 65568 | tf_op jit(solution)/shard_map/ppermute | solution.py:26
  108.8 2.9 %collective-permute-done.23 = bf16[2,128,128]{2,1,0:T(8,128)(2,1)S(1)} collective-permute-done((bf16[2,128,128]{2,1,0:T(8,128)(2,1)S(1)}, bf16[2,128,128]{2,1,0:T(8,128)(2,1)S(1)}, u32[]{:S(2)}, u32[]{:S(2)}) %collective-permute-start.23) | collective-permute-done | bytes 65568 | tf_op jit(solution)/shard_map/ppermute | solution.py:26
  114.2 6.8 %shard_map.136 = (bf16[1024,128]{1,0:T(8,128)(2,1)S(1)}, bf16[1024,128]{1,0:T(8,128)(2,1)}, bf16[1024,128]{1,0:T(8,128)(2,1)}, bf16[1024,128]{1,0:T(8,128)(2,1)}) custom-call(s32[1]{0:T(128)} %bitcast.member_ref, s32[2]{0:T(128)S(1)} %get-tuple-element.89.length_ref, f32[2]{0:T(128)S(1)} %get-tuple-element.88.scale_ref, ...), custom_call_target="tpu_custom_call" | custom-call | flops 4000000000 | bytes 4194304 | tf_op jit(solution)/shard_map/pallas_call | solution.py:793
  127.6 2.7 %collective-permute-done.25.refs_2_ = bf16[1024,128]{1,0:T(8,128)(2,1)S(1)} collective-permute-done((bf16[1024,128]{1,0:T(8,128)(2,1)}, bf16[1024,128]{1,0:T(8,128)(2,1)S(1)}, u32[]{:S(2)}, u32[]{:S(2)}) %collective-permute-start.25) | collective-permute-done | bytes 262176 | tf_op jit(solution)/shard_map/ppermute | solution.py:705
  (97 shorter events, 43.1 us)
Async XLA Ops:
  4.3 11.2 %collective-permute-start = (bf16[1024,128]{1,0:T(8,128)(2,1)S(1)}, bf16[1024,128]{1,0:T(8,128)(2,1)S(1)}, u32[]{:S(2)}, u32[]{:S(2)}) collective-permute-start(bf16[1024,128]{1,0:T(8,128)(2,1)S(1)} %get-tuple-element.45), channel_id=1, source_target_pairs={{0,2},{2,0},{4,6},{6,4},{8,10},{10,8},{12,14},{14,12},{16,18},{18,... | collective-permute-start | bytes 786440 | tf_op jit(solution)/shard_map/ppermute | solution.py:705
  7.3 13.8 %collective-permute-start.1 = (bf16[1024,128]{1,0:T(8,128)(2,1)S(1)}, bf16[1024,128]{1,0:T(8,128)(2,1)S(1)}, u32[]{:S(2)}, u32[]{:S(2)}) collective-permute-start(bf16[1024,128]{1,0:T(8,128)(2,1)S(1)} %get-tuple-element.46), channel_id=1, source_target_pairs={{0,4},{2,6},{4,0},{6,2},{8,12},{10,14},{12,8},{14,10},{16,20},{18,... | collective-permute-start | bytes 786440 | tf_op jit(solution)/shard_map/ppermute | solution.py:705
  8.8 16.3 %collective-permute-start.2 = (bf16[1024,128]{1,0:T(8,128)(2,1)S(1)}, bf16[1024,128]{1,0:T(8,128)(2,1)S(1)}, u32[]{:S(2)}, u32[]{:S(2)}) collective-permute-start(bf16[1024,128]{1,0:T(8,128)(2,1)S(1)} %get-tuple-element.47), channel_id=1, source_target_pairs={{0,6},{2,4},{4,2},{6,0},{8,14},{10,12},{12,10},{14,8},{16,22},{18,... | collective-permute-start | bytes 786440 | tf_op jit(solution)/shard_map/ppermute | solution.py:705
  11.9 19.3 %collective-permute-start.7 = (bf16[1040,128]{1,0:T(8,128)(2,1)}, bf16[1040,128]{1,0:T(8,128)(2,1)S(1)}, u32[]{:S(2)}, u32[]{:S(2)}) collective-permute-start(bf16[1040,128]{1,0:T(8,128)(2,1)} %get-tuple-element.49), channel_id=1, source_target_pairs={{0,2},{2,0},{4,6},{6,4},{8,10},{10,8},{12,14},{14,12},{16,18},{18,... | collective-permute-start | bytes 798728 | tf_op jit(solution)/shard_map/ppermute | solution.py:705
  14.0 18.6 %collective-permute-start.8 = (bf16[1040,128]{1,0:T(8,128)(2,1)}, bf16[1040,128]{1,0:T(8,128)(2,1)S(1)}, u32[]{:S(2)}, u32[]{:S(2)}) collective-permute-start(bf16[1040,128]{1,0:T(8,128)(2,1)} %get-tuple-element.50), channel_id=1, source_target_pairs={{0,4},{2,6},{4,0},{6,2},{8,12},{10,14},{12,8},{14,10},{16,20},{18,... | collective-permute-start | bytes 798728 | tf_op jit(solution)/shard_map/ppermute | solution.py:705
  15.5 20.8 %collective-permute-start.9 = (bf16[1040,128]{1,0:T(8,128)(2,1)S(1)}, bf16[1040,128]{1,0:T(8,128)(2,1)S(1)}, u32[]{:S(2)}, u32[]{:S(2)}) collective-permute-start(bf16[1040,128]{1,0:T(8,128)(2,1)S(1)} %get-tuple-element.51), channel_id=1, source_target_pairs={{0,6},{2,4},{4,2},{6,0},{8,14},{10,12},{12,10},{14,8},{16,22},{18,... | collective-permute-start | bytes 798728 | tf_op jit(solution)/shard_map/ppermute | solution.py:705
  21.1 23.1 %collective-permute-start.3 = (bf16[1024,128]{1,0:T(8,128)(2,1)S(1)}, bf16[1024,128]{1,0:T(8,128)(2,1)}, u32[]{:S(2)}, u32[]{:S(2)}) collective-permute-start(bf16[1024,128]{1,0:T(8,128)(2,1)S(1)} %get-tuple-element.44.refs_0_.refs_4_), channel_id=1, source_target_pairs={{0,8},{2,10},{4,12},{6,14},{8,16},{10,18},{12,20},{14,22},{16,24},... | collective-permute-start | bytes 786440 | tf_op jit(solution)/shard_map/ppermute | solution.py:26
  27.3 11.8 %collective-permute-start.10 = (bf16[2,128,128]{2,1,0:T(8,128)(2,1)S(1)}, bf16[2,128,128]{2,1,0:T(8,128)(2,1)S(1)}, u32[]{:S(2)}, u32[]{:S(2)}) collective-permute-start(bf16[2,128,128]{2,1,0:T(8,128)(2,1)S(1)} %convert_element_type.30), channel_id=1, source_target_pairs={{0,16},{2,18},{4,20},{6,22},{8,24},{10,26},{12,28},{14,30},{1,17},... | collective-permute-start | bytes 196616 | tf_op jit(solution)/shard_map/ppermute | solution.py:26
  31.2 12.9 %collective-permute-start.11 = (bf16[2,128,128]{2,1,0:T(8,128)(2,1)S(1)}, bf16[2,128,128]{2,1,0:T(8,128)(2,1)S(1)}, u32[]{:S(2)}, u32[]{:S(2)}) collective-permute-start(bf16[2,128,128]{2,1,0:T(8,128)(2,1)S(1)} %convert_element_type.30), channel_id=1, source_target_pairs={{0,24},{2,26},{4,28},{6,30},{1,25},{3,27},{5,29},{7,31}} | collective-permute-start | bytes 196616 | tf_op jit(solution)/shard_map/ppermute | solution.py:26
  32.5 11.7 %collective-permute-start.4 = (bf16[1024,128]{1,0:T(8,128)(2,1)S(1)}, bf16[1024,128]{1,0:T(8,128)(2,1)}, u32[]{:S(2)}, u32[]{:S(2)}) collective-permute-start(bf16[1024,128]{1,0:T(8,128)(2,1)S(1)} %collective-permute-done.refs_1_.refs_5_), channel_id=1, source_target_pairs={{0,8},{2,10},{4,12},{6,14},{8,16},{10,18},{12,20},{14,22},{16,24},... | collective-permute-start | bytes 786440 | tf_op jit(solution)/shard_map/ppermute | solution.py:26
  36.3 10.3 %collective-permute-start.5 = (bf16[1024,128]{1,0:T(8,128)(2,1)S(1)}, bf16[1024,128]{1,0:T(8,128)(2,1)S(1)}, u32[]{:S(2)}, u32[]{:S(2)}) collective-permute-start(bf16[1024,128]{1,0:T(8,128)(2,1)S(1)} %collective-permute-done.1.refs_2_.refs_6_), channel_id=1, source_target_pairs={{0,8},{2,10},{4,12},{6,14},{8,16},{10,18},{12,20},{14,22},{16,24},... | collective-permute-start | bytes 786440 | tf_op jit(solution)/shard_map/ppermute | solution.py:26
  39.1 10.3 %collective-permute-start.6 = (bf16[1024,128]{1,0:T(8,128)(2,1)S(1)}, bf16[1024,128]{1,0:T(8,128)(2,1)}, u32[]{:S(2)}, u32[]{:S(2)}) collective-permute-start(bf16[1024,128]{1,0:T(8,128)(2,1)S(1)} %collective-permute-done.2.refs_3_.refs_7_), channel_id=1, source_target_pairs={{0,8},{2,10},{4,12},{6,14},{8,16},{10,18},{12,20},{14,22},{16,24},... | collective-permute-start | bytes 786440 | tf_op jit(solution)/shard_map/ppermute | solution.py:26
  61.6 51.4 %collective-permute-start.19 = (bf16[4,512,128]{2,1,0:T(8,128)(2,1)S(1)}, bf16[4,512,128]{2,1,0:T(8,128)(2,1)}, u32[]{:S(2)}, u32[]{:S(2)}) collective-permute-start(bf16[4,512,128]{2,1,0:T(8,128)(2,1)S(1)} %get-tuple-element.52.refs_16_.query_ref.refs_8_), channel_id=1, source_target_pairs={{8,0},{10,2},{12,4},{14,6},{16,8},{18,10},{20,12},{22,14},{24,16},... | collective-permute-start | bytes 1572872 | tf_op jit(solution)/shard_map/ppermute | solution.py:26
  67.5 45.4 %collective-permute-start.20 = (bf16[4,512,128]{2,1,0:T(8,128)(2,1)S(1)}, bf16[4,512,128]{2,1,0:T(8,128)(2,1)}, u32[]{:S(2)}, u32[]{:S(2)}) collective-permute-start(bf16[4,512,128]{2,1,0:T(8,128)(2,1)S(1)} %get-tuple-element.60.refs_17_.low_ref.refs_9_), channel_id=1, source_target_pairs={{8,0},{10,2},{12,4},{14,6},{16,8},{18,10},{20,12},{22,14},{24,16},... | collective-permute-start | bytes 1572872 | tf_op jit(solution)/shard_map/ppermute | solution.py:26
  77.3 11.5 %collective-permute-start.27 = (f32[16,128]{1,0:T(8,128)S(1)}, f32[16,128]{1,0:T(8,128)S(1)}, u32[]{:S(2)}, u32[]{:S(2)}) collective-permute-start(f32[16,128]{1,0:T(8,128)S(1)} %get-tuple-element.81), channel_id=1, source_target_pairs={{0,8},{2,10},{4,12},{6,14},{8,0},{10,2},{12,4},{14,6},{16,24},{18,... | collective-permute-start | bytes 24584 | tf_op jit(solution)/shard_map/ppermute | solution.py:705
  99.9 6.2 %collective-permute-start.21 = (bf16[2,128,128]{2,1,0:T(8,128)(2,1)S(1)}, bf16[2,128,128]{2,1,0:T(8,128)(2,1)S(1)}, u32[]{:S(2)}, u32[]{:S(2)}) collective-permute-start(bf16[2,128,128]{2,1,0:T(8,128)(2,1)S(1)} %shard_map.135), channel_id=1, source_target_pairs={{8,0},{10,2},{12,4},{14,6},{16,8},{18,10},{20,12},{22,14},{24,16},... | collective-permute-start | bytes 196616 | tf_op jit(solution)/shard_map/ppermute | solution.py:26
  101.2 7.1 %collective-permute-start.22 = (bf16[2,128,128]{2,1,0:T(8,128)(2,1)S(1)}, bf16[2,128,128]{2,1,0:T(8,128)(2,1)S(1)}, u32[]{:S(2)}, u32[]{:S(2)}) collective-permute-start(bf16[2,128,128]{2,1,0:T(8,128)(2,1)S(1)} %shard_map.135), channel_id=1, source_target_pairs={{16,0},{18,2},{20,4},{22,6},{24,8},{26,10},{28,12},{30,14},{17,1},... | collective-permute-start | bytes 196616 | tf_op jit(solution)/shard_map/ppermute | solution.py:26
  102.5 9.1 %collective-permute-start.23 = (bf16[2,128,128]{2,1,0:T(8,128)(2,1)S(1)}, bf16[2,128,128]{2,1,0:T(8,128)(2,1)S(1)}, u32[]{:S(2)}, u32[]{:S(2)}) collective-permute-start(bf16[2,128,128]{2,1,0:T(8,128)(2,1)S(1)} %shard_map.135), channel_id=1, source_target_pairs={{24,0},{26,2},{28,4},{30,6},{25,1},{27,3},{29,5},{31,7}} | collective-permute-start | bytes 196616 | tf_op jit(solution)/shard_map/ppermute | solution.py:26
  106.1 17.2 %collective-permute-start.16 = (bf16[1024,128]{1,0:T(8,128)(2,1)}, bf16[1024,128]{1,0:T(8,128)(2,1)S(1)}, u32[]{:S(2)}, u32[]{:S(2)}) collective-permute-start(bf16[1024,128]{1,0:T(8,128)(2,1)} %get-tuple-element.69), channel_id=1, source_target_pairs={{0,2},{2,0},{4,6},{6,4},{8,10},{10,8},{12,14},{14,12},{16,18},{18,... | collective-permute-start | bytes 786440 | tf_op jit(solution)/shard_map/ppermute | solution.py:705
  108.3 17.6 %collective-permute-start.17 = (bf16[1024,128]{1,0:T(8,128)(2,1)}, bf16[1024,128]{1,0:T(8,128)(2,1)S(1)}, u32[]{:S(2)}, u32[]{:S(2)}) collective-permute-start(bf16[1024,128]{1,0:T(8,128)(2,1)} %get-tuple-element.70), channel_id=1, source_target_pairs={{0,4},{2,6},{4,0},{6,2},{8,12},{10,14},{12,8},{14,10},{16,20},{18,... | collective-permute-start | bytes 786440 | tf_op jit(solution)/shard_map/ppermute | solution.py:705
  111.7 14.2 %collective-permute-start.18 = (bf16[1024,128]{1,0:T(8,128)(2,1)}, bf16[1024,128]{1,0:T(8,128)(2,1)S(1)}, u32[]{:S(2)}, u32[]{:S(2)}) collective-permute-start(bf16[1024,128]{1,0:T(8,128)(2,1)} %get-tuple-element.71), channel_id=1, source_target_pairs={{0,6},{2,4},{4,2},{6,0},{8,14},{10,12},{12,10},{14,8},{16,22},{18,... | collective-permute-start | bytes 786440 | tf_op jit(solution)/shard_map/ppermute | solution.py:705
  121.0 6.6 %collective-permute-start.24 = (bf16[1024,128]{1,0:T(8,128)(2,1)}, bf16[1024,128]{1,0:T(8,128)(2,1)S(1)}, u32[]{:S(2)}, u32[]{:S(2)}) collective-permute-start(bf16[1024,128]{1,0:T(8,128)(2,1)} %get-tuple-element.76), channel_id=1, source_target_pairs={{0,2},{2,0},{4,6},{6,4},{8,10},{10,8},{12,14},{14,12},{16,18},{18,... | collective-permute-start | bytes 786440 | tf_op jit(solution)/shard_map/ppermute | solution.py:705
  121.8 8.5 %collective-permute-start.25 = (bf16[1024,128]{1,0:T(8,128)(2,1)}, bf16[1024,128]{1,0:T(8,128)(2,1)S(1)}, u32[]{:S(2)}, u32[]{:S(2)}) collective-permute-start(bf16[1024,128]{1,0:T(8,128)(2,1)} %get-tuple-element.77), channel_id=1, source_target_pairs={{0,4},{2,6},{4,0},{6,2},{8,12},{10,14},{12,8},{14,10},{16,20},{18,... | collective-permute-start | bytes 786440 | tf_op jit(solution)/shard_map/ppermute | solution.py:705
  123.3 8.3 %collective-permute-start.26 = (bf16[1024,128]{1,0:T(8,128)(2,1)}, bf16[1024,128]{1,0:T(8,128)(2,1)S(1)}, u32[]{:S(2)}, u32[]{:S(2)}) collective-permute-start(bf16[1024,128]{1,0:T(8,128)(2,1)} %get-tuple-element.78), channel_id=1, source_target_pairs={{0,6},{2,4},{4,2},{6,0},{8,14},{10,12},{12,10},{14,8},{16,22},{18,... | collective-permute-start | bytes 786440 | tf_op jit(solution)/shard_map/ppermute | solution.py:705
  (21 other events, 130.8 us)

commit v3 on v2

--- a/solution.py
+++ b/solution.py
@@ -273,7 +273,7 @@
 f32 = jnp.float32
 bf16 = jnp.bfloat16
 index_rows = 16
-kernel_vmem = 20 * 2**20
+kernel_vmem = 16 * 2**20
 
 
 def dot_nn(left, right):
@@ -363,13 +363,13 @@
 
 
 def arrange_kernel(member_ref, *refs, group):
-    pieces, targets = refs[:group], refs[group:]
+    pieces, (query_ref, grad_ref) = refs[:group], refs[group:]
+    count = grad_ref.shape[1]
     for bits, piece in enumerate(pieces):
-        first = 0
-        for target in targets:
-            count = target.shape[1]
-            target[member_ref[0] ^ bits] = piece[first : first + count]
-            first += count
+        block_no = member_ref[0] ^ bits
+        query_ref[block_no, :count] = piece[:count]
+        query_ref[block_no, count:] = piece[2 * count :]
+        grad_ref[block_no] = piece[count : 2 * count]
 
 
 def unpack_kernel(member_ref, *refs, group, head_stride, kind_stride):
@@ -411,7 +411,7 @@
         dot_tn(key_all[i * rows : (i + 1) * rows], value_all[i * rows : (i + 1) * rows])
         for i in range(group)
     ]
-    total_ref[0] = added(parts)
+    total_ref[0] = added(parts).astype(bf16)
     for block_no in range(group):
         block_ref[0, block_no] = parts[block_no]
         for bit_no in range(group.bit_length() - 1):
@@ -432,13 +432,18 @@
     place(target, 1 + group, own_refs, member)
 
 
-def forward_kernel(member_ref, length_ref, scale_ref, last_scale_ref, *refs, group, near_levels):
+def forward_kernel(
+    member_ref, length_ref, scale_ref, far_scale_ref, *refs, group, chunks, near_levels
+):
     key_refs, value_refs = refs[:group], refs[group : 2 * group]
     key_prev, value_prev = refs[2 * group : 3 * group], refs[3 * group : 4 * group]
     (
-        query_ref, grad_ref, index_ref, table_ref, gain_ref, near_ref, block_ref, far_ref,
+        query_ref, grad_ref, index_ref, table_ref, gain_ref, near_ref, block_ref,
+    ) = refs[4 * group : 4 * group + 7]
+    far_refs = refs[4 * group + 7 : 4 * group + chunks + 5]
+    (
         mixed_ref, stat_ref, state_ref, far_out_ref, key_all, value_all,
-    ) = refs[4 * group :]
+    ) = refs[4 * group + chunks + 5 :]
     head_no = pl.program_id(0)
     _, rows, head_dim = query_ref.shape
     member = member_ref[0]
@@ -450,7 +455,10 @@
         dot_tn(key_all[i * rows : (i + 1) * rows], value_all[i * rows : (i + 1) * rows])
         for i in range(1, group + 1)
     ]
-    far = (far_ref[0] + added(blocks) * last_scale_ref[0]).astype(bf16)
+    far = added(blocks) * far_scale_ref[0]
+    for step_no, far_ref in enumerate(far_refs):
+        far = far + far_ref[0].astype(f32) * far_scale_ref[step_no + 1]
+    far = far.astype(bf16)
     far_out_ref[0] = far
     blocks = blocks[1:] + [block_ref[0, i] for i in range(group - 1)]
     stat_rows = []
@@ -498,8 +506,8 @@
 
 
 def norm_kernel(member_ref, mixed_ref, grad_ref, gain_ref, *refs, group, width):
-    stat_refs, out_refs = refs[:group], refs[group : 2 * group]
-    low_ref, gain_part_ref, out_all = refs[2 * group :]
+    stat_refs, out_refs = refs[:2], refs[2 : 2 + group]
+    low_ref, gain_part_ref, out_all = refs[2 + group :]
     gain = gain_ref[0]
     stats = jnp.transpose(added([stat_ref[...] for stat_ref in stat_refs]))
     parts = []
@@ -517,13 +525,18 @@
         out_ref[...] = out_all[member_ref[0] ^ bits]
 
 
-def far_grad_kernel(query_ref, low_ref, index_ref, table_ref, far_grad_ref):
+def last_level_outer(query_ref, low_ref, index_ref, table_ref):
     parts = []
     for block_no in range(query_ref.shape[0]):
         weights = jnp.transpose(lane_weights(lane_indices(index_ref[block_no]), table_ref))
         low = weights[:, LEVELS - 1 : LEVELS] * low_ref[block_no].astype(f32)
         parts.append(dot_tn(query_ref[block_no], low.astype(bf16)))
-    far_grad_ref[0] = added(parts).astype(bf16)
+    return added(parts)
+
+
+def far_grad_kernel(query_ref, low_ref, index_ref, table_ref, far_grad_ref):
+    outer = last_level_outer(query_ref, low_ref, index_ref, table_ref)
+    far_grad_ref[0] = outer.astype(bf16)
 
 
 def query_kernel(member_ref, length_ref, scale_ref, *refs, group, near_levels):
@@ -551,6 +564,7 @@
     own_leaf = leaf_col[:1]
     lanes = table_ref.shape[-1]
     table_parts = [jnp.zeros((8, lanes), f32) for _ in range(TABLE_ROWS)]
+    near_grads = [[] for _ in range(group)]
     for block_no in range(group):
         query = query_ref[block_no]
         low = low_ref[block_no]
@@ -594,7 +608,10 @@
             level_rows[level_no] = dot_nt(ones, (query_wide * back).astype(bf16))[:1]
             if not last:
                 upstream = (picked(level_no) * low_wide).astype(bf16)
-                near_grad_ref[0, block_no, bit_no] = dot_tn(query, upstream)
+                outer = dot_tn(query, upstream) * level_scale(level_no, head_dim)
+                first = ((block_no >> bit_no) - 1) << bit_no
+                for lower_no in range(first, first + 2**bit_no):
+                    near_grads[lower_no].append(outer)
         out_all[block_no] = result.astype(bf16)
         weight_grad = jnp.concatenate(level_rows, axis=0)
         for row_no in range(TABLE_ROWS):
@@ -607,6 +624,8 @@
     lane_sums = dot_nt(ones, table_high) + dot_nt(ones, table_low)
     for bits, out_ref in enumerate(out_refs):
         out_ref[...] = out_all[member ^ bits]
+    for lower_no in range(group - 1):
+        near_grad_ref[0, lower_no] = added(near_grads[lower_no])
     heads = pl.num_programs(0)
     row_no = lax.broadcasted_iota(jnp.int32, sums_ref.shape, 0)
     first = (member * heads + head_no) * 2
@@ -619,14 +638,17 @@
     sums_ref[...] = jnp.where(row_no == first + 1, gain_part_ref[0], sums)
 
 
-def key_kernel(member_ref, length_ref, scale_ref, *refs, group, near_levels):
+def key_kernel(
+    member_ref, length_ref, scale_ref, far_scale_ref, *refs, group, chunks, near_levels
+):
     key_refs, value_refs = refs[:group], refs[group : 2 * group]
     (
-        query_ref, low_ref, query_next_ref, low_next_ref, index_ref, table_ref, near_grad_ref,
-        far_grad_ref,
+        query_ref, low_ref, query_next_ref, low_next_ref, index_ref, index_next_ref, table_ref,
+        near_grad_ref,
     ) = refs[2 * group : 2 * group + 8]
-    out_refs = refs[2 * group + 8 : 3 * group + 8]
-    key_all, value_all, query_all, low_all, out_all = refs[3 * group + 8 :]
+    far_refs = refs[2 * group + 8 : 2 * group + chunks + 6]
+    out_refs = refs[2 * group + chunks + 6 : 3 * group + chunks + 6]
+    key_all, value_all, query_all, low_all, out_all = refs[3 * group + chunks + 6 :]
     head_no = pl.program_id(0)
     _, rows, head_dim = query_ref.shape
     member = member_ref[0]
@@ -646,6 +668,10 @@
         dot_tn(query_all[i * rows : (i + 1) * rows], low_all[i * rows : (i + 1) * rows])
         for i in range(1, 2 * group - 1)
     ]
+    far_grad = last_level_outer(query_next_ref, low_next_ref, index_next_ref, table_ref)
+    far_grad = far_grad * far_scale_ref[chunks - 1]
+    for step_no, far_ref in enumerate(far_refs):
+        far_grad = far_grad + far_ref[0].astype(f32) * far_scale_ref[chunks + step_no]
     row_pos, col_pos = positions(rows, rows)
     edge_row, edge_col = positions(rows, 2 * rows)
     edge_mask = edge_col - edge_row < part
@@ -669,12 +695,9 @@
         prob = (dot_nt(key, query_all[own]) * factor).astype(bf16)
         prob_grad = (dot_nt(value, low_all[own]) * factor).astype(bf16)
         state = window_state(blocks[block_no : block_no + group - 1], whole, group - 1)
-        state = state * window_scale + far_grad_ref[0]
-        for bit_no in range(group.bit_length() - 1):
-            if not block_no >> bit_no & 1:
-                first = (block_no >> bit_no | 1) << bit_no
-                upper = [near_grad_ref[0, first + i, bit_no] for i in range(2**bit_no)]
-                state = state + added(upper) * level_scale(near_levels + 1 + bit_no, head_dim)
+        state = state * window_scale + far_grad
+        if block_no < group - 1:
+            state = state + near_grad_ref[0, block_no]
         state = state.astype(bf16)
         value_grad = dot_nn(prob, low_all[own]) + window_scale * value_total + dot_nn(key, state)
         key_grad = dot_nn(prob_grad, query_all[own]) + window_scale * key_total
@@ -694,12 +717,33 @@
     group_bits = group.bit_length() - 1
     near_levels = (rows // BLOCK).bit_length() - 1
     seq_count = lax.axis_size("seq")
-    chunk_bits = (seq_count // group).bit_length() - 1
+    chunks = seq_count // group
+    chunk_bits = chunks.bit_length() - 1
     seq_index = lax.axis_index("seq")
     member = seq_index & (group - 1)
     member_arg = member.astype(jnp.int32).reshape(1)
     head_count = lax.axis_size("head")
     width = float(heads_here * head_count * head_dim)
+
+    first_head = member * heads
+    table = lax.dynamic_slice_in_dim(level_table, first_head, heads, 1)
+    table = jnp.pad(table.transpose(1, 0, 2), ((0, 0), (0, 0), (0, 8 - LEVELS)))
+    gain = lax.dynamic_slice_in_dim(norm_gain, first_head, heads, 0)[:, None, :]
+    length = lax.dynamic_slice_in_dim(window_length, first_head, heads, 0)
+    scale = lax.rsqrt((head_dim * length).astype(f32))
+    chunk_no = (seq_index >> group_bits).astype(jnp.int32)
+    steps = lax.broadcasted_iota(jnp.int32, (2 * chunks - 2,), 0)
+    steps = jnp.where(steps < chunks - 1, -1 - steps, steps - chunks + 2)
+    apart = chunk_no ^ (chunk_no + steps)
+    far_scale = jnp.full(apart.shape, level_scale(near_levels + group_bits + 1, head_dim), f32)
+    for bit_no in range(1, chunk_bits):
+        scale_here = level_scale(near_levels + group_bits + 1 + bit_no, head_dim)
+        far_scale = jnp.where(apart >= 1 << bit_no, scale_here, far_scale)
+    early_member = member_arg
+    member_arg, length, scale, far_scale, gain, table = lax.optimization_barrier(
+        (member_arg, length, scale, far_scale, gain, table)
+    )
+    table = jnp.broadcast_to(table[..., None], (heads, TABLE_ROWS, 8, 128))
 
     def swapped(shard, bits):
         return lax.ppermute(shard, "seq", [(i, i ^ bits) for i in range(seq_count)])
@@ -724,14 +768,17 @@
             compiler_params=pltpu.CompilerParams(vmem_limit_bytes=kernel_vmem),
         )(*args)
 
+    def in_hbm(tensor):
+        return pltpu.with_memory_space_constraint(tensor, pltpu.HBM)
+
     piece_shape = (2 * heads * rows, head_dim)
     rest_shape = (2 * heads * rows + index_rows, head_dim)
     chunk_shape = (group, heads * rows, head_dim)
-    index_shape = (group, index_rows, head_dim)
+    query_shape = (group, heads * rows + index_rows, head_dim)
     pair = whole_call(
         functools.partial(pack_kernel, group=group, extra=0),
         [smem, hbm, hbm], [(vmem, piece_shape, bf16)] * group, 2 * heads * group,
-        member_arg, key_rows, value_rows,
+        early_member, in_hbm(key_rows), in_hbm(value_rows),
     )
     index_pad = jnp.pad(level_index.astype(bf16), ((0, 0), (0, 8 - LEVELS)))
     index_pack = index_pad.reshape(rows // 128, 128, 8).transpose(0, 2, 1).reshape(index_rows, 128)
@@ -743,35 +790,18 @@
     pair = exchanged(pair)
     pair_prev = [moved(piece, group) for piece in pair]
     rest = exchanged(rest)
-    query, grad, index = whole_call(
+    query, grad = whole_call(
         functools.partial(arrange_kernel, group=group), [smem] + [vmem] * group,
-        [(vmem, chunk_shape, bf16), (vmem, chunk_shape, bf16), (vmem, index_shape, bf16)], 0,
+        [(vmem, query_shape, bf16), (vmem, chunk_shape, bf16)], 0,
         member_arg, *rest,
     )
     query_next = moved(query, -group)
-
-    first_head = member * heads
-    table = lax.dynamic_slice_in_dim(level_table, first_head, heads, 1)
-    table = jnp.pad(table.transpose(1, 0, 2), ((0, 0), (0, 0), (0, 8 - LEVELS)))
-    table = jnp.broadcast_to(table[..., None], (heads, TABLE_ROWS, 8, 128))
-    gain = lax.dynamic_slice_in_dim(norm_gain, first_head, heads, 0)[:, None, :]
-    length = lax.dynamic_slice_in_dim(window_length, first_head, heads, 0)
-    scale = lax.rsqrt((head_dim * length).astype(f32))
-
-    chunk_no = seq_index // group
-
-    def far_scale(other):
-        apart = chunk_no ^ other
-        result = jnp.full((), level_scale(near_levels + group_bits + 1, head_dim), f32)
-        for bit_no in range(1, chunk_bits):
-            scale_here = level_scale(near_levels + group_bits + 1 + bit_no, head_dim)
-            result = jnp.where(apart >= 1 << bit_no, scale_here, result)
-        return result
 
     state_shape = (head_dim, head_dim)
     states_shape = (heads,) + state_shape
     near_shape = (heads, group, group_bits) + state_shape
     block_states = (heads, group) + state_shape
+    lower_shape = (heads, group - 1) + state_shape
 
     def whole(first):
         return pl.BlockSpec((group, rows, head_dim), lambda h: (0, first * heads + h, 0))
@@ -785,7 +815,9 @@
     def fixed(shape):
         return pl.BlockSpec(shape, lambda h: (0,) * len(shape))
 
-    index_spec = fixed(index_shape)
+    index_spec = pl.BlockSpec(
+        (group, index_rows, head_dim), lambda h: (0, heads * rows // index_rows, 0)
+    )
     table_spec = per_head(table.shape)
     stat_shape = (2 * group, rows)
 
@@ -814,25 +846,21 @@
         [
             (per_head(near_shape), near_shape, bf16),
             (per_head(block_states), block_states, f32),
-            (per_head(states_shape), states_shape, f32),
+            (per_head(states_shape), states_shape, bf16),
         ],
         [chunk_rows] * 2, {}, member_arg, *pair, *pair,
     )
-    total = total.astype(bf16)
-    far = jnp.zeros(states_shape, f32)
-    for step_no in range(2, 1 << chunk_bits):
-        other = moved(total, step_no * group).astype(f32)
-        far = far + other * far_scale(chunk_no - step_no)
-    last_scale = far_scale(chunk_no - 1).reshape(1)
+    far = [moved(total, step_no * group) for step_no in range(2, chunks)]
     far_spec = per_head(states_shape)
 
     mixed, stats, states, far = run(
-        functools.partial(forward_kernel, **sizes), 3,
+        functools.partial(forward_kernel, chunks=chunks, **sizes), 3,
         [smem] * 4 + each(0) + each(1) + each(0) + each(1)
         + [
             whole(0), whole(0), index_spec, table_spec, per_head(gain.shape),
-            per_head(near_shape), per_head(block_states), far_spec,
-        ],
+            per_head(near_shape), per_head(block_states),
+        ]
+        + [far_spec] * (chunks - 2),
         [
             (whole(0), chunk_shape, f32),
             (fixed(stat_shape), stat_shape, f32),
@@ -840,20 +868,22 @@
             (far_spec, states_shape, bf16),
         ],
         [window_rows] * 2, {},
-        member_arg, length, scale, last_scale, *pair, *pair, *pair_prev, *pair_prev,
-        query, grad, index, table, gain, near, block_sums, far,
+        member_arg, length, scale, far_scale, *pair, *pair, *pair_prev, *pair_prev,
+        query, grad, query, table, gain, near, block_sums, *far,
     )
 
     part = stats
     for step_no in range(1, head_count):
         turn = [(i, (i + step_no) % head_count) for i in range(head_count)]
         stats = stats + lax.ppermute(part, "head", turn)
-    stat_parts = [stats] + [swapped(stats, bits) for bits in range(1, group)]
+    for bit_no in range(group_bits - 1):
+        stats = stats + swapped(stats, 1 << bit_no)
+    stat_parts = [stats, swapped(stats, group >> 1)]
 
     out_pieces = [(each(0)[0], piece_shape, bf16)] * group
     *first_out, low, gain_part = run(
         functools.partial(norm_kernel, group=group, width=width), 0.6,
-        [smem, whole(0), whole(0), per_head(gain.shape)] + [fixed(stat_shape)] * group,
+        [smem, whole(0), whole(0), per_head(gain.shape)] + [fixed(stat_shape)] * 2,
         out_pieces + [(whole(0), chunk_shape, bf16), (per_head(gain.shape), gain.shape, f32)],
         [results], {}, member_arg, mixed, grad, gain, *stat_parts,
     )
@@ -861,16 +891,13 @@
     (far_part,) = run(
         far_grad_kernel, 0.3,
         [whole(0), whole(0), index_spec, table_spec], [(far_spec, states_shape, bf16)],
-        [], {}, query, low, index, table,
-    )
-    far_grad = jnp.zeros(states_shape, f32)
-    for step_no in range(1, 1 << chunk_bits):
-        other = moved(far_part, -step_no * group).astype(f32)
-        far_grad = far_grad + other * far_scale(chunk_no + step_no)
+        [], {}, query, low, query, table,
+    )
+    far_grad = [moved(far_part, -step_no * group) for step_no in range(2, chunks)]
 
     args = (
         member_arg, length, scale, *pair, *pair, *pair_prev, *pair_prev,
-        query, low, index, table, near, states, far, gain_part, *first_out,
+        query, low, query, table, near, states, far, gain_part, *first_out,
     )
     sums_shape = (2 * heads_here, head_dim)
     *first_out, near_grad, sums = run(
@@ -882,7 +909,7 @@
         ]
         + [pl.BlockSpec(memory_space=pl.ANY)] * group,
         [(each(1)[0], piece_shape, bf16)] * group
-        + [(per_head(near_shape), near_shape, f32), (fixed(sums_shape), sums_shape, f32)],
+        + [(per_head(lower_shape), lower_shape, f32), (fixed(sums_shape), sums_shape, f32)],
         [window_rows] * 2 + [results],
         {len(args) - group + bits: bits for bits in range(group)}, *args,
     )
@@ -890,22 +917,22 @@
 
     pair_out = pl.BlockSpec((2 * rows, head_dim), lambda h: (h, 0))
     last_out = run(
-        functools.partial(key_kernel, **sizes), 4,
-        [smem] * 3 + each(0) + each(1)
+        functools.partial(key_kernel, chunks=chunks, **sizes), 4,
+        [smem] * 4 + each(0) + each(1)
         + [
-            whole(0), whole(0), whole(0), whole(0), index_spec, table_spec,
-            per_head(near_shape), far_spec,
-        ],
+            whole(0), whole(0), whole(0), whole(0), index_spec, index_spec, table_spec,
+            per_head(lower_shape),
+        ]
+        + [far_spec] * (chunks - 2),
         [(pair_out, piece_shape, bf16)] * group,
         [chunk_rows] * 2 + [window_rows] * 2 + [(group, 2 * rows, head_dim)], {},
-        member_arg, length, scale, *pair, *pair,
-        query, low, query_next, low_next, index, table, near_grad, far_grad,
+        member_arg, length, scale, far_scale, *pair, *pair,
+        query, low, query_next, low_next, query, query_next, table, near_grad, *far_grad,
     )
     last_out = exchanged(last_out)
 
     for step_no in range(chunk_bits + group_bits):
-        bit_no = (step_no + group_bits) % (chunk_bits + group_bits)
-        sums = sums + swapped(sums, 1 << bit_no)
+        sums = sums + swapped(sums, 1 << step_no)
     sums = sums.reshape(heads_here, 2, head_dim)
     table_grad = sums[:, 0].reshape(heads_here, TABLE_ROWS, 8)[:, :, :LEVELS]
 
@@ -939,6 +966,7 @@
         and group == 1 << (group.bit_length() - 1)
         and heads_here % group == 0
         and seq_count % group == 0
+        and seq_count > 2 * group
         and seq_count == 1 << (seq_count.bit_length() - 1)
         and levels_fit
     )

time: 133 us -> 121 us (0.910)
  starting transfers between devices: 55.6 us -> 50.5 us
  local copies, waits for them, and re-layouts: 7.21 us -> 3.65 us
  waiting for transfers between devices: 35.3 us -> 33.7 us
    ppermute x11 -> x10, waiting for transfers between devices: 10.8 us -> 6.43 us  [shifted(): return lax.ppermute(block, axis, route)]
    ppermute x11 -> x10, starting transfers between devices: 26.4 us -> 22.6 us  [shifted(): return lax.ppermute(block, axis, route)]
    unnamed x30 -> x15, local copies, waits for them, and re-layouts: 5.73 us -> 2.08 us
    ppermute x19 -> x18, waiting for transfers between devices: 23.4 us -> 26.1 us  [swapped(): return lax.ppermute(shard, 'seq', [(i, i ^ bits) for i in range(seq_count)])]
    ppermute x19 -> x18, starting transfers between devices: 29.2 us -> 27.8 us  [swapped(): return lax.ppermute(shard, 'seq', [(i, i ^ bits) for i in range(seq_count)])]
  transfers between devices with their start and end apart: 31 -> 29, of which waited for: 14 -> 12; matrix products, arithmetic and copies ran while one was open for 2% -> 2% of each run, Pallas kernels for 17% -> 18%
where the time goes in v3:
time: 121 us; the launch traced here: 120 us
  starting transfers between devices  50.5 us (42%)
  waiting for transfers between devices  33.7 us (28%)
  Pallas kernels  31.4 us (26%)
  local copies, waits for them, and re-layouts  3.65 us (3%)
    ppermute x18, starting transfers between devices, swapped(): return lax.ppermute(shard, 'seq', [(i, i ^ bits) for i in range(seq_count)])  27.8 us
    ppermute x18, waiting for transfers between devices, swapped(): return lax.ppermute(shard, 'seq', [(i, i ^ bits) for i in range(seq_count)])  26.1 us
    pallas_call x6, Pallas kernels, run(): pl.pallas_call(kernel, grid=(heads,), in_specs=in_specs, out_specs=[spec...  26.1 us
    ppermute x10, starting transfers between devices, shifted(): return lax.ppermute(block, axis, route)  22.6 us
    ppermute x10, waiting for transfers between devices, shifted(): return lax.ppermute(block, axis, route)  6.43 us
    pallas_call x5, Pallas kernels, whole_call(): pl.pallas_call(kernel, in_specs=in_specs, out_specs=[spec for spec, _, _...  5.3 us
  transfers between devices with their start and end apart: 29, of which 12 were waited for; matrix products, arithmetic and copies ran while one was open for 2% of the time, Pallas kernels for 18%

profile of v3, /device:TPU:0, one launch (start us, length us, event | category | flops | bytes accessed | tf_op | source)
XLA Modules:
  0.0 120.4 jit_solution(1255055887535419752)
XLA Ops:
  2.1 3.0 %collective-permute-start = (bf16[1024,128]{1,0:T(8,128)(2,1)S(1)}, bf16[1024,128]{1,0:T(8,128)(2,1)S(1)}, u32[]{:S(2)}, u32[]{:S(2)}) collective-permute-start(bf16[1024,128]{1,0:T(8,128)(2,1)S(1)} %get-tuple-element.53), channel_id=1, source_target_pairs={{0,2},{2,0},{4,6},{6,4},{8,10},{10,8},{12,14},{14,12},{16,18},{18,... | collective-permute-start | bytes 786440 | tf_op jit(solution)/shard_map/ppermute | solution.py:749
  12.5 3.5 %collective-permute-start.3 = (bf16[1024,128]{1,0:T(8,128)(2,1)S(1)}, bf16[1024,128]{1,0:T(8,128)(2,1)S(1)}, u32[]{:S(2)}, u32[]{:S(2)}) collective-permute-start(bf16[1024,128]{1,0:T(8,128)(2,1)S(1)} %get-tuple-element.52.refs_0_.refs_4_), channel_id=1, source_target_pairs={{0,8},{2,10},{4,12},{6,14},{8,16},{10,18},{12,20},{14,22},{16,24},... | collective-permute-start | bytes 786440 | tf_op jit(solution)/shard_map/ppermute | solution.py:26
  18.1 7.4 %collective-permute-done.2.refs_3_.refs_7_ = bf16[1024,128]{1,0:T(8,128)(2,1)S(1)} collective-permute-done((bf16[1024,128]{1,0:T(8,128)(2,1)S(1)}, bf16[1024,128]{1,0:T(8,128)(2,1)S(1)}, u32[]{:S(2)}, u32[]{:S(2)}) %collective-permute-start.2) | collective-permute-done | bytes 262176 | tf_op jit(solution)/shard_map/ppermute | solution.py:749
  25.5 4.2 %collective-permute-start.4 = (bf16[1024,128]{1,0:T(8,128)(2,1)S(1)}, bf16[1024,128]{1,0:T(8,128)(2,1)}, u32[]{:S(2)}, u32[]{:S(2)}) collective-permute-start(bf16[1024,128]{1,0:T(8,128)(2,1)S(1)} %collective-permute-done.refs_1_.refs_5_), channel_id=1, source_target_pairs={{0,8},{2,10},{4,12},{6,14},{8,16},{10,18},{12,20},{14,22},{16,24},... | collective-permute-start | bytes 786440 | tf_op jit(solution)/shard_map/ppermute | solution.py:26
  29.7 3.5 %collective-permute-start.5 = (bf16[1024,128]{1,0:T(8,128)(2,1)S(1)}, bf16[1024,128]{1,0:T(8,128)(2,1)}, u32[]{:S(2)}, u32[]{:S(2)}) collective-permute-start(bf16[1024,128]{1,0:T(8,128)(2,1)S(1)} %collective-permute-done.1.refs_2_.refs_6_), channel_id=1, source_target_pairs={{0,8},{2,10},{4,12},{6,14},{8,16},{10,18},{12,20},{14,22},{16,24},... | collective-permute-start | bytes 786440 | tf_op jit(solution)/shard_map/ppermute | solution.py:26
  33.2 3.5 %collective-permute-start.6 = (bf16[1024,128]{1,0:T(8,128)(2,1)S(1)}, bf16[1024,128]{1,0:T(8,128)(2,1)}, u32[]{:S(2)}, u32[]{:S(2)}) collective-permute-start(bf16[1024,128]{1,0:T(8,128)(2,1)S(1)} %collective-permute-done.2.refs_3_.refs_7_), channel_id=1, source_target_pairs={{0,8},{2,10},{4,12},{6,14},{8,16},{10,18},{12,20},{14,22},{16,24},... | collective-permute-start | bytes 786440 | tf_op jit(solution)/shard_map/ppermute | solution.py:26
  40.1 5.7 %collective-permute-done.10.refs_23_ = bf16[2,128,128]{2,1,0:T(8,128)(2,1)S(1)} collective-permute-done((bf16[2,128,128]{2,1,0:T(8,128)(2,1)S(1)}, bf16[2,128,128]{2,1,0:T(8,128)(2,1)S(1)}, u32[]{:S(2)}, u32[]{:S(2)}) %collective-permute-start.10) | collective-permute-done | bytes 65568 | tf_op jit(solution)/shard_map/ppermute | solution.py:26
  46.6 7.4 %shard_map.131 = (f32[4,512,128]{2,1,0:T(8,128)S(1)}, f32[8,256]{1,0:T(8,128)S(1)}, bf16[2,4,128,128]{3,2,1,0:T(8,128)(2,1)S(1)}, bf16[2,128,128]{2,1,0:T(8,128)(2,1)S(1)}) custom-call(s32[1]{0:T(128)} %bitcast.member_ref, s32[2]{0:T(128)S(1)} %get-tuple-element.50.length_ref, f32[2]{0:T(128)S(1)} %get-tuple-element.51.scale_ref, ...), custom_call_target="tpu_custom_call" | custom-call | flops 3000000000 | bytes 4194304 | tf_op jit(solution)/shard_map/pallas_call | solution.py:825
  55.2 1.7 %collective-permute-start.13 = (f32[8,256]{1,0:T(8,128)S(1)}, f32[8,256]{1,0:T(8,128)S(1)}, u32[]{:S(2)}, u32[]{:S(2)}) collective-permute-start(f32[8,256]{1,0:T(8,128)S(1)} %add.43), channel_id=1, source_target_pairs={{0,2},{2,0},{4,6},{6,4},{8,10},{10,8},{12,14},{14,12},{16,18},{18,... | collective-permute-start | bytes 24584 | tf_op jit(solution)/shard_map/ppermute | solution.py:749
  56.9 2.0 %collective-permute-done.13 = f32[8,256]{1,0:T(8,128)S(1)} collective-permute-done((f32[8,256]{1,0:T(8,128)S(1)}, f32[8,256]{1,0:T(8,128)S(1)}, u32[]{:S(2)}, u32[]{:S(2)}) %collective-permute-start.13) | collective-permute-done | bytes 8224 | tf_op jit(solution)/shard_map/ppermute | solution.py:749
  62.5 1.9 %shard_map.132 = (bf16[1024,128]{1,0:T(8,128)(2,1)S(1)}, bf16[1024,128]{1,0:T(8,128)(2,1)S(1)}, bf16[1024,128]{1,0:T(8,128)(2,1)S(1)}, bf16[1024,128]{1,0:T(8,12...) custom-call(s32[1]{0:T(128)} %bitcast.member_ref, f32[4,512,128]{2,1,0:T(8,128)S(1)} %get-tuple-element.68.mixed_ref, ...), custom_call_target="tpu_custom_call" | custom-call | flops 600000000 | bytes 4194304 | tf_op jit(solution)/shard_map/pallas_call | solution.py:825
  69.9 8.4 %shard_map.133 = (bf16[1024,128]{1,0:T(8,128)(2,1)S(1)}, bf16[1024,128]{1,0:T(8,128)(2,1)S(1)}, bf16[1024,128]{1,0:T(8,128)(2,1)S(1)}, bf16[1024,128]{1,0:T(8,12...) custom-call(s32[1]{0:T(128)} %bitcast.member_ref, ...), custom_call_target="tpu_custom_call", output_to_operand_aliasing={{0}: (27, {}), {1}: (28, {}), {2}: (29, {}), {3}: (30, {})} | custom-call | flops 3000000000 | bytes 4194304 | tf_op jit(solution)/shard_map/pallas_call | solution.py:825
  78.3 1.7 %collective-permute-start.25 = (f32[16,128]{1,0:T(8,128)S(1)}, f32[16,128]{1,0:T(8,128)S(1)}, u32[]{:S(2)}, u32[]{:S(2)}) collective-permute-start(f32[16,128]{1,0:T(8,128)S(1)} %get-tuple-element.91), channel_id=1, source_target_pairs={{0,2},{2,0},{4,6},{6,4},{8,10},{10,8},{12,14},{14,12},{16,18},{18,... | collective-permute-start | bytes 24584 | tf_op jit(solution)/shard_map/ppermute | solution.py:749
  80.0 2.0 %collective-permute-done.25 = f32[16,128]{1,0:T(8,128)S(1)} collective-permute-done((f32[16,128]{1,0:T(8,128)S(1)}, f32[16,128]{1,0:T(8,128)S(1)}, u32[]{:S(2)}, u32[]{:S(2)}) %collective-permute-start.25) | collective-permute-done | bytes 8224 | tf_op jit(solution)/shard_map/ppermute | solution.py:749
  82.8 2.8 %collective-permute-done.26 = f32[16,128]{1,0:T(8,128)S(1)} collective-permute-done((f32[16,128]{1,0:T(8,128)S(1)}, f32[16,128]{1,0:T(8,128)S(1)}, u32[]{:S(2)}, u32[]{:S(2)}) %collective-permute-start.26) | collective-permute-done | bytes 8224 | tf_op jit(solution)/shard_map/ppermute | solution.py:749
  85.6 2.9 %collective-permute-start.27 = (f32[16,128]{1,0:T(8,128)S(1)}, f32[16,128]{1,0:T(8,128)S(1)}, u32[]{:S(2)}, u32[]{:S(2)}) collective-permute-start(f32[16,128]{1,0:T(8,128)S(1)} %add.46), channel_id=1, source_target_pairs={{0,8},{2,10},{4,12},{6,14},{8,0},{10,2},{12,4},{14,6},{16,24},{18,... | collective-permute-start | bytes 24584 | tf_op jit(solution)/shard_map/ppermute | solution.py:749
  88.6 1.6 %collective-permute-done.27 = f32[16,128]{1,0:T(8,128)S(1)} collective-permute-done((f32[16,128]{1,0:T(8,128)S(1)}, f32[16,128]{1,0:T(8,128)S(1)}, u32[]{:S(2)}, u32[]{:S(2)}) %collective-permute-start.27) | collective-permute-done | bytes 8224 | tf_op jit(solution)/shard_map/ppermute | solution.py:749
  90.2 4.2 %collective-permute-start.28 = (f32[16,128]{1,0:T(8,128)S(1)}, f32[16,128]{1,0:T(8,128)S(1)}, u32[]{:S(2)}, u32[]{:S(2)}) collective-permute-start(f32[16,128]{1,0:T(8,128)S(1)} %add.47), channel_id=1, source_target_pairs={{0,16},{2,18},{4,20},{6,22},{8,24},{10,26},{12,28},{14,30},{16,0},... | collective-permute-start | bytes 24584 | tf_op jit(solution)/shard_map/ppermute | solution.py:749
  94.4 1.6 %collective-permute-done.28 = f32[16,128]{1,0:T(8,128)S(1)} collective-permute-done((f32[16,128]{1,0:T(8,128)S(1)}, f32[16,128]{1,0:T(8,128)S(1)}, u32[]{:S(2)}, u32[]{:S(2)}) %collective-permute-start.28) | collective-permute-done | bytes 8224 | tf_op jit(solution)/shard_map/ppermute | solution.py:749
  96.0 1.7 %collective-permute-start.15 = (bf16[1024,128]{1,0:T(8,128)(2,1)S(1)}, bf16[1024,128]{1,0:T(8,128)(2,1)S(1)}, u32[]{:S(2)}, u32[]{:S(2)}) collective-permute-start(bf16[1024,128]{1,0:T(8,128)(2,1)S(1)} %get-tuple-element.79), channel_id=1, source_target_pairs={{0,2},{2,0},{4,6},{6,4},{8,10},{10,8},{12,14},{14,12},{16,18},{18,... | collective-permute-start | bytes 786440 | tf_op jit(solution)/shard_map/ppermute | solution.py:749
  99.5 6.4 %shard_map.136 = (bf16[1024,128]{1,0:T(8,128)(2,1)S(1)}, bf16[1024,128]{1,0:T(8,128)(2,1)S(1)}, bf16[1024,128]{1,0:T(8,128)(2,1)S(1)}, bf16[1024,128]{1,0:T(8,128)(2,1)S(1)}) custom-call(s32[1]{0:T(128)} %bitcast.member_ref, s32[2]{0:T(128)S(1)} %get-tuple-element.50.length_ref, f32[2]{0:T(128)S(1)} %get-tuple-element.51.scale_ref, ...), custom_call_target="tpu_custom_call" | custom-call | flops 4000000000 | bytes 4194304 | tf_op jit(solution)/shard_map/pallas_call | solution.py:825
  105.9 1.7 %collective-permute-start.22 = (bf16[1024,128]{1,0:T(8,128)(2,1)S(1)}, bf16[1024,128]{1,0:T(8,128)(2,1)S(1)}, u32[]{:S(2)}, u32[]{:S(2)}) collective-permute-start(bf16[1024,128]{1,0:T(8,128)(2,1)S(1)} %get-tuple-element.86), channel_id=1, source_target_pairs={{0,2},{2,0},{4,6},{6,4},{8,10},{10,8},{12,14},{14,12},{16,18},{18,... | collective-permute-start | bytes 786440 | tf_op jit(solution)/shard_map/ppermute | solution.py:749
  112.0 3.0 %collective-permute-done.22.refs_1_ = bf16[1024,128]{1,0:T(8,128)(2,1)S(1)} collective-permute-done((bf16[1024,128]{1,0:T(8,128)(2,1)S(1)}, bf16[1024,128]{1,0:T(8,128)(2,1)S(1)}, u32[]{:S(2)}, u32[]{:S(2)}) %collective-permute-start.22) | collective-permute-done | bytes 262176 | tf_op jit(solution)/shard_map/ppermute | solution.py:749
  115.0 4.1 %collective-permute-done.23.refs_2_ = bf16[1024,128]{1,0:T(8,128)(2,1)S(1)} collective-permute-done((bf16[1024,128]{1,0:T(8,128)(2,1)S(1)}, bf16[1024,128]{1,0:T(8,128)(2,1)S(1)}, u32[]{:S(2)}, u32[]{:S(2)}) %collective-permute-start.23) | collective-permute-done | bytes 262176 | tf_op jit(solution)/shard_map/ppermute | solution.py:749
  (78 shorter events, 33.5 us)
Async XLA Ops:
  2.1 13.9 %collective-permute-start = (bf16[1024,128]{1,0:T(8,128)(2,1)S(1)}, bf16[1024,128]{1,0:T(8,128)(2,1)S(1)}, u32[]{:S(2)}, u32[]{:S(2)}) collective-permute-start(bf16[1024,128]{1,0:T(8,128)(2,1)S(1)} %get-tuple-element.53), channel_id=1, source_target_pairs={{0,2},{2,0},{4,6},{6,4},{8,10},{10,8},{12,14},{14,12},{16,18},{18,... | collective-permute-start | bytes 786440 | tf_op jit(solution)/shard_map/ppermute | solution.py:749
  5.2 12.4 %collective-permute-start.1 = (bf16[1024,128]{1,0:T(8,128)(2,1)S(1)}, bf16[1024,128]{1,0:T(8,128)(2,1)S(1)}, u32[]{:S(2)}, u32[]{:S(2)}) collective-permute-start(bf16[1024,128]{1,0:T(8,128)(2,1)S(1)} %get-tuple-element.54), channel_id=1, source_target_pairs={{0,4},{2,6},{4,0},{6,2},{8,12},{10,14},{12,8},{14,10},{16,20},{18,... | collective-permute-start | bytes 786440 | tf_op jit(solution)/shard_map/ppermute | solution.py:749
  10.5 22.7 %collective-permute-start.7 = (bf16[1040,128]{1,0:T(8,128)(2,1)S(1)}, bf16[1040,128]{1,0:T(8,128)(2,1)S(1)}, u32[]{:S(2)}, u32[]{:S(2)}) collective-permute-start(bf16[1040,128]{1,0:T(8,128)(2,1)S(1)} %get-tuple-element.57), channel_id=1, source_target_pairs={{0,2},{2,0},{4,6},{6,4},{8,10},{10,8},{12,14},{14,12},{16,18},{18,... | collective-permute-start | bytes 798728 | tf_op jit(solution)/shard_map/ppermute | solution.py:749
  11.1 14.4 %collective-permute-start.2 = (bf16[1024,128]{1,0:T(8,128)(2,1)S(1)}, bf16[1024,128]{1,0:T(8,128)(2,1)S(1)}, u32[]{:S(2)}, u32[]{:S(2)}) collective-permute-start(bf16[1024,128]{1,0:T(8,128)(2,1)S(1)} %get-tuple-element.55), channel_id=1, source_target_pairs={{0,6},{2,4},{4,2},{6,0},{8,14},{10,12},{12,10},{14,8},{16,22},{18,... | collective-permute-start | bytes 786440 | tf_op jit(solution)/shard_map/ppermute | solution.py:749
  12.5 17.2 %collective-permute-start.3 = (bf16[1024,128]{1,0:T(8,128)(2,1)S(1)}, bf16[1024,128]{1,0:T(8,128)(2,1)S(1)}, u32[]{:S(2)}, u32[]{:S(2)}) collective-permute-start(bf16[1024,128]{1,0:T(8,128)(2,1)S(1)} %get-tuple-element.52.refs_0_.refs_4_), channel_id=1, source_target_pairs={{0,8},{2,10},{4,12},{6,14},{8,16},{10,18},{12,20},{14,22},{16,24},... | collective-permute-start | bytes 786440 | tf_op jit(solution)/shard_map/ppermute | solution.py:26
  16.0 21.3 %collective-permute-start.8 = (bf16[1040,128]{1,0:T(8,128)(2,1)S(1)}, bf16[1040,128]{1,0:T(8,128)(2,1)S(1)}, u32[]{:S(2)}, u32[]{:S(2)}) collective-permute-start(bf16[1040,128]{1,0:T(8,128)(2,1)S(1)} %get-tuple-element.58), channel_id=1, source_target_pairs={{0,4},{2,6},{4,0},{6,2},{8,12},{10,14},{12,8},{14,10},{16,20},{18,... | collective-permute-start | bytes 798728 | tf_op jit(solution)/shard_map/ppermute | solution.py:749
  17.6 21.0 %collective-permute-start.9 = (bf16[1040,128]{1,0:T(8,128)(2,1)S(1)}, bf16[1040,128]{1,0:T(8,128)(2,1)S(1)}, u32[]{:S(2)}, u32[]{:S(2)}) collective-permute-start(bf16[1040,128]{1,0:T(8,128)(2,1)S(1)} %get-tuple-element.59), channel_id=1, source_target_pairs={{0,6},{2,4},{4,2},{6,0},{8,14},{10,12},{12,10},{14,8},{16,22},{18,... | collective-permute-start | bytes 798728 | tf_op jit(solution)/shard_map/ppermute | solution.py:749
  25.5 21.0 %collective-permute-start.4 = (bf16[1024,128]{1,0:T(8,128)(2,1)S(1)}, bf16[1024,128]{1,0:T(8,128)(2,1)}, u32[]{:S(2)}, u32[]{:S(2)}) collective-permute-start(bf16[1024,128]{1,0:T(8,128)(2,1)S(1)} %collective-permute-done.refs_1_.refs_5_), channel_id=1, source_target_pairs={{0,8},{2,10},{4,12},{6,14},{8,16},{10,18},{12,20},{14,22},{16,24},... | collective-permute-start | bytes 786440 | tf_op jit(solution)/shard_map/ppermute | solution.py:26
  29.7 16.8 %collective-permute-start.5 = (bf16[1024,128]{1,0:T(8,128)(2,1)S(1)}, bf16[1024,128]{1,0:T(8,128)(2,1)}, u32[]{:S(2)}, u32[]{:S(2)}) collective-permute-start(bf16[1024,128]{1,0:T(8,128)(2,1)S(1)} %collective-permute-done.1.refs_2_.refs_6_), channel_id=1, source_target_pairs={{0,8},{2,10},{4,12},{6,14},{8,16},{10,18},{12,20},{14,22},{16,24},... | collective-permute-start | bytes 786440 | tf_op jit(solution)/shard_map/ppermute | solution.py:26
  33.2 13.3 %collective-permute-start.6 = (bf16[1024,128]{1,0:T(8,128)(2,1)S(1)}, bf16[1024,128]{1,0:T(8,128)(2,1)}, u32[]{:S(2)}, u32[]{:S(2)}) collective-permute-start(bf16[1024,128]{1,0:T(8,128)(2,1)S(1)} %collective-permute-done.2.refs_3_.refs_7_), channel_id=1, source_target_pairs={{0,8},{2,10},{4,12},{6,14},{8,16},{10,18},{12,20},{14,22},{16,24},... | collective-permute-start | bytes 786440 | tf_op jit(solution)/shard_map/ppermute | solution.py:26
  37.3 8.4 %collective-permute-start.10 = (bf16[2,128,128]{2,1,0:T(8,128)(2,1)S(1)}, bf16[2,128,128]{2,1,0:T(8,128)(2,1)S(1)}, u32[]{:S(2)}, u32[]{:S(2)}) collective-permute-start(bf16[2,128,128]{2,1,0:T(8,128)(2,1)S(1)} %get-tuple-element.67), channel_id=1, source_target_pairs={{0,16},{2,18},{4,20},{6,22},{8,24},{10,26},{12,28},{14,30},{1,17},... | collective-permute-start | bytes 196616 | tf_op jit(solution)/shard_map/ppermute | solution.py:26
  38.6 7.9 %collective-permute-start.11 = (bf16[2,128,128]{2,1,0:T(8,128)(2,1)S(1)}, bf16[2,128,128]{2,1,0:T(8,128)(2,1)S(1)}, u32[]{:S(2)}, u32[]{:S(2)}) collective-permute-start(bf16[2,128,128]{2,1,0:T(8,128)(2,1)S(1)} %get-tuple-element.67), channel_id=1, source_target_pairs={{0,24},{2,26},{4,28},{6,30},{1,25},{3,27},{5,29},{7,31}} | collective-permute-start | bytes 196616 | tf_op jit(solution)/shard_map/ppermute | solution.py:26
  59.7 39.8 %collective-permute-start.18 = (bf16[4,528,128]{2,1,0:T(8,128)(2,1)S(1)}, bf16[4,528,128]{2,1,0:T(8,128)(2,1)S(1)}, u32[]{:S(2)}, u32[]{:S(2)}) collective-permute-start(bf16[4,528,128]{2,1,0:T(8,128)(2,1)S(1)} %get-tuple-element.60.refs_16_.refs_18_.query_ref.index_ref.refs_8_.refs_12_), channel_id=1, source_target_pairs={{8,0},{10,2},{12,4},{14,6},{16,8},{18,10},{20,12},{22,14},{24,16},... | collective-permute-start | bytes 1622024 | tf_op jit(solution)/shard_map/ppermute | solution.py:26
  64.4 35.1 %collective-permute-start.19 = (bf16[4,512,128]{2,1,0:T(8,128)(2,1)S(1)}, bf16[4,512,128]{2,1,0:T(8,128)(2,1)S(1)}, u32[]{:S(2)}, u32[]{:S(2)}) collective-permute-start(bf16[4,512,128]{2,1,0:T(8,128)(2,1)S(1)} %get-tuple-element.70.refs_17_.low_ref.refs_9_), channel_id=1, source_target_pairs={{8,0},{10,2},{12,4},{14,6},{16,8},{18,10},{20,12},{22,14},{24,16},... | collective-permute-start | bytes 1572872 | tf_op jit(solution)/shard_map/ppermute | solution.py:26
  67.1 30.6 %collective-permute-start.20 = (bf16[2,128,128]{2,1,0:T(8,128)(2,1)S(1)}, bf16[2,128,128]{2,1,0:T(8,128)(2,1)S(1)}, u32[]{:S(2)}, u32[]{:S(2)}) collective-permute-start(bf16[2,128,128]{2,1,0:T(8,128)(2,1)S(1)} %shard_map.135), channel_id=1, source_target_pairs={{16,0},{18,2},{20,4},{22,6},{24,8},{26,10},{28,12},{30,14},{17,1},... | collective-permute-start | bytes 196616 | tf_op jit(solution)/shard_map/ppermute | solution.py:26
  68.4 29.6 %collective-permute-start.21 = (bf16[2,128,128]{2,1,0:T(8,128)(2,1)S(1)}, bf16[2,128,128]{2,1,0:T(8,128)(2,1)S(1)}, u32[]{:S(2)}, u32[]{:S(2)}) collective-permute-start(bf16[2,128,128]{2,1,0:T(8,128)(2,1)S(1)} %shard_map.135), channel_id=1, source_target_pairs={{24,0},{26,2},{28,4},{30,6},{25,1},{27,3},{29,5},{31,7}} | collective-permute-start | bytes 196616 | tf_op jit(solution)/shard_map/ppermute | solution.py:26
  85.6 4.6 %collective-permute-start.27 = (f32[16,128]{1,0:T(8,128)S(1)}, f32[16,128]{1,0:T(8,128)S(1)}, u32[]{:S(2)}, u32[]{:S(2)}) collective-permute-start(f32[16,128]{1,0:T(8,128)S(1)} %add.46), channel_id=1, source_target_pairs={{0,8},{2,10},{4,12},{6,14},{8,0},{10,2},{12,4},{14,6},{16,24},{18,... | collective-permute-start | bytes 24584 | tf_op jit(solution)/shard_map/ppermute | solution.py:749
  90.2 5.8 %collective-permute-start.28 = (f32[16,128]{1,0:T(8,128)S(1)}, f32[16,128]{1,0:T(8,128)S(1)}, u32[]{:S(2)}, u32[]{:S(2)}) collective-permute-start(f32[16,128]{1,0:T(8,128)S(1)} %add.47), channel_id=1, source_target_pairs={{0,16},{2,18},{4,20},{6,22},{8,24},{10,26},{12,28},{14,30},{16,0},... | collective-permute-start | bytes 24584 | tf_op jit(solution)/shard_map/ppermute | solution.py:749
  96.0 12.0 %collective-permute-start.15 = (bf16[1024,128]{1,0:T(8,128)(2,1)S(1)}, bf16[1024,128]{1,0:T(8,128)(2,1)S(1)}, u32[]{:S(2)}, u32[]{:S(2)}) collective-permute-start(bf16[1024,128]{1,0:T(8,128)(2,1)S(1)} %get-tuple-element.79), channel_id=1, source_target_pairs={{0,2},{2,0},{4,6},{6,4},{8,10},{10,8},{12,14},{14,12},{16,18},{18,... | collective-permute-start | bytes 786440 | tf_op jit(solution)/shard_map/ppermute | solution.py:749
  97.7 13.2 %collective-permute-start.16 = (bf16[1024,128]{1,0:T(8,128)(2,1)S(1)}, bf16[1024,128]{1,0:T(8,128)(2,1)S(1)}, u32[]{:S(2)}, u32[]{:S(2)}) collective-permute-start(bf16[1024,128]{1,0:T(8,128)(2,1)S(1)} %get-tuple-element.80), channel_id=1, source_target_pairs={{0,4},{2,6},{4,0},{6,2},{8,12},{10,14},{12,8},{14,10},{16,20},{18,... | collective-permute-start | bytes 786440 | tf_op jit(solution)/shard_map/ppermute | solution.py:749
  98.0 12.9 %collective-permute-start.17 = (bf16[1024,128]{1,0:T(8,128)(2,1)}, bf16[1024,128]{1,0:T(8,128)(2,1)S(1)}, u32[]{:S(2)}, u32[]{:S(2)}) collective-permute-start(bf16[1024,128]{1,0:T(8,128)(2,1)} %get-tuple-element.81), channel_id=1, source_target_pairs={{0,6},{2,4},{4,2},{6,0},{8,14},{10,12},{12,10},{14,8},{16,22},{18,... | collective-permute-start | bytes 786440 | tf_op jit(solution)/shard_map/ppermute | solution.py:749
  105.9 9.1 %collective-permute-start.22 = (bf16[1024,128]{1,0:T(8,128)(2,1)S(1)}, bf16[1024,128]{1,0:T(8,128)(2,1)S(1)}, u32[]{:S(2)}, u32[]{:S(2)}) collective-permute-start(bf16[1024,128]{1,0:T(8,128)(2,1)S(1)} %get-tuple-element.86), channel_id=1, source_target_pairs={{0,2},{2,0},{4,6},{6,4},{8,10},{10,8},{12,14},{14,12},{16,18},{18,... | collective-permute-start | bytes 786440 | tf_op jit(solution)/shard_map/ppermute | solution.py:749
  107.7 11.5 %collective-permute-start.23 = (bf16[1024,128]{1,0:T(8,128)(2,1)S(1)}, bf16[1024,128]{1,0:T(8,128)(2,1)S(1)}, u32[]{:S(2)}, u32[]{:S(2)}) collective-permute-start(bf16[1024,128]{1,0:T(8,128)(2,1)S(1)} %get-tuple-element.87), channel_id=1, source_target_pairs={{0,4},{2,6},{4,0},{6,2},{8,12},{10,14},{12,8},{14,10},{16,20},{18,... | collective-permute-start | bytes 786440 | tf_op jit(solution)/shard_map/ppermute | solution.py:749
  108.0 11.2 %collective-permute-start.24 = (bf16[1024,128]{1,0:T(8,128)(2,1)S(1)}, bf16[1024,128]{1,0:T(8,128)(2,1)S(1)}, u32[]{:S(2)}, u32[]{:S(2)}) collective-permute-start(bf16[1024,128]{1,0:T(8,128)(2,1)S(1)} %get-tuple-element.88), channel_id=1, source_target_pairs={{0,6},{2,4},{4,2},{6,0},{8,14},{10,12},{12,10},{14,8},{16,22},{18,... | collective-permute-start | bytes 786440 | tf_op jit(solution)/shard_map/ppermute | solution.py:749
  (12 other events, 54.6 us)
